TPU v7x, 512 devices: a whole 4x4x16 slice. The times are simulated.
512 devices in a mesh: src: 8 (over x, core), tgt: 64 (over y, z).
Axes of the slice: x: 4, y: 4, z: 16, core: 2. Of those that a mesh axis runs over, the one named last changes fastest.
Arguments:
- source_points: float32 [32, 16384], P(None, ('src', 'tgt')), may hold values from -1.25 to 1.25
- target_points: float32 [32, 65536], P('src', 'tgt'), may hold values from -1.2 to 1.2
- source_potential: float32 [16384], P(('src', 'tgt')), may hold values from -1.5 to 1.5
- target_potential: float32 [65536], P('tgt'), may hold values from -1.5 to 1.5
- source_weight: float32 [16384], P(('src', 'tgt')), may hold values from 0.5 to 2
- target_weight: float32 [65536], P('tgt'), may hold values from 0.5 to 2
- core_previous: float32 [34, 34], replicated, may hold values from -0.12 to 0.12
Outputs:
- source_new: float32 [16384], P(('src', 'tgt'))
- target_new: float32 [65536], P('tgt')
- core_new: float32 [34, 34], replicated
All inputs are finite; a program needn't handle non-finite values.
Results may differ from a plain program's by a relative error of at most 0.0002.
Values sent between devices are 32-bit elements; how exact they have to be, the bound alone decides.
No kernel may reach another device: no remote copies, remote signals or barrier semaphores. Data moves between devices by JAX's collectives and lax.ppermute only.
A program may use at most 64 MiB of HBM per device.

v0:
```python
import functools

import jax
import jax.numpy as jnp
from jax import lax
from jax.sharding import Mesh
from jax.sharding import PartitionSpec as P

TGT = ("tgt_0", "tgt_1")
SRC = ("src_0", "src_1")
SRC_TGT = ("src_0", "src_1", "tgt_0", "tgt_1")


EPSILON = 0.5
HIGHEST = lax.Precision.HIGHEST


def rows_first(arrays, axis, dims):
    turned = [jnp.moveaxis(a, dim, 0) for a, dim in zip(arrays, dims)]
    both = jnp.concatenate([t.reshape(len(t), -1) for t in turned], axis=1)
    filled, at, gathered = (lax.all_gather(both, axis, axis=0, tiled=True), 0, [])
    for t, dim in zip(turned, dims):
        slab = filled[:, at : at + t[0].size].reshape(-1, *t.shape[1:])
        gathered.append(jnp.moveaxis(slab, 0, dim))
        at += t[0].size
    return tuple(gathered)


def sent_to_all(x, axis):
    copies = jnp.broadcast_to(x, (lax.axis_size(axis), *x.shape))
    return lax.all_to_all(copies, axis, split_axis=0, concat_axis=0, tiled=True)


def laid_out(parts, dim):
    parts = jnp.moveaxis(parts, 0, dim)
    dims = parts.shape
    return parts.reshape(*dims[:dim], dims[dim] * dims[dim + 1], *dims[dim + 2 :])


def collect(x, axis, dim):
    parts = sent_to_all(x, axis)
    return laid_out(parts, dim)


def by_axis(x, axes):
    return functools.reduce(lax.psum, axes, x)


def collected_together(x, axis):
    leaves = jax.tree.leaves(x)
    sequence = sorted(range(len(leaves)), key=lambda k: -leaves[k].size)
    width = (1, *leaves[sequence[0]].shape)[-1]
    lines = [
        jnp.pad(leaves[k].reshape(-1), (0, -leaves[k].size % width)).reshape(-1, width)
        for k in sequence
    ]
    both, at, found = (lax.all_gather(jnp.concatenate(lines), axis), 0, {})
    for k, line in zip(sequence, lines):
        slab = both[:, at : at + len(line)].reshape(len(both), -1)
        found[k] = slab[:, : leaves[k].size].reshape(-1, *leaves[k].shape)
        at += len(line)
    numbers = iter(range(len(leaves)))
    return jax.tree.map(lambda _: found[next(numbers)], x)


def joined_all(x, axes, combine):
    for axis in axes:
        pieces = collected_together(x, axis)
        x = jax.tree.map(lambda part: part[0], pieces)
        for k in range(1, lax.axis_size(axis)):
            x = combine(x, jax.tree.map(lambda part: part[k], pieces))
    return x


def all_in_one(x, axis):
    leaves = jax.tree.leaves(x)
    sequence = sorted(range(len(leaves)), key=lambda k: -leaves[k].size)
    width = (1, *leaves[sequence[0]].shape)[-1]
    lines = [
        jnp.pad(leaves[k].reshape(-1), (0, -leaves[k].size % width)).reshape(-1, width)
        for k in sequence
    ]
    both, at, found = (sent_to_all(jnp.concatenate(lines), axis), 0, {})
    for k, line in zip(sequence, lines):
        slab = both[:, at : at + len(line)].reshape(len(both), -1)
        found[k] = slab[:, : leaves[k].size].reshape(-1, *leaves[k].shape)
        at += len(line)
    numbers = iter(range(len(leaves)))
    return jax.tree.map(lambda _: found[next(numbers)], x)


def combined_pairwise(pieces, combine):
    while len(jax.tree.leaves(pieces)[0]) > 1:
        pieces = jax.vmap(combine)(
            *(jax.tree.map(lambda part: part[side::2], pieces) for side in (0, 1))
        )
    return jax.tree.map(lambda part: part[0], pieces)


def combined_all(x, axis, combine):
    pieces = all_in_one(x, axis)
    return combined_pairwise(pieces, combine)


def factors(points):
    squares = jnp.sum(points * points, axis=0, keepdims=True)
    unit_row = jnp.ones_like(squares)
    return (
        jnp.concatenate([squares, unit_row, -2.0 * points], 0),
        jnp.concatenate([unit_row, squares, points], 0),
    )


def contract_rank(left_block, weighted):
    return lax.dot_general(
        left_block,
        weighted,
        (((0,), (0,)), ((), ())),
        precision=HIGHEST,
        preferred_element_type=jnp.float32,
    )


def contract_last(former, latter):
    return lax.dot_general(
        former,
        latter,
        (((1,), (1,)), ((), ())),
        precision=HIGHEST,
        preferred_element_type=jnp.float32,
    )


def row_blocks(values, block_size):
    number = values.shape[-1] // block_size
    shaped = values.reshape(values.shape[:-1] + (number, block_size))
    return jnp.moveaxis(shaped, -2, 0)


def combine_parts(former, latter):
    highest = jnp.maximum(former[0], latter[0])
    return (
        highest,
        former[1] * jnp.exp(former[0] - highest) + latter[1] * jnp.exp(latter[0] - highest),
    )


def on_device(
    source_points,
    target_points,
    source_potential,
    target_potential,
    source_weight,
    target_weight,
    core_previous,
):
    spread = lax.axis_size(TGT)
    sources = source_points.shape[1] * spread * lax.axis_size(SRC)
    targets = target_potential.shape[0] * spread
    points, potential, weight = rows_first(
        (source_points, source_potential, source_weight), TGT, (1, 0, 0)
    )
    features = collect(target_points, SRC, 0)
    log_source = jnp.log(weight) - jnp.log(jnp.float32(sources))
    log_target = jnp.log(target_weight) - jnp.log(jnp.float32(targets))
    left_source, right_source = factors(points)
    left_target, right_target = factors(features)
    row_count = points.shape[1]
    share_count = row_count // spread
    block_size = min(512, row_count)
    left_blocks = row_blocks(left_source, block_size)
    right_blocks = row_blocks(right_source, block_size)
    potential_blocks = row_blocks(potential, block_size)
    weight_blocks = row_blocks(log_source, block_size)
    rank_size = left_source.shape[0]
    previous_w = jnp.dot(core_previous, left_target, precision=HIGHEST)

    def plan_step(running, portion):
        left_block, right_block, source_part, log_weight = portion
        scores = contract_rank(left_block, previous_w)
        plan_tile = jnp.exp(
            log_weight[:, None]
            + log_target[None, :]
            + (source_part[:, None] + target_potential[None, :] + 2.0 * scores) / EPSILON
        )
        carried = contract_last(right_target, plan_tile)
        return (running + contract_last(right_block, carried), None)

    partial_core, _ = lax.scan(
        plan_step,
        jnp.zeros((rank_size, rank_size), jnp.float32),
        (left_blocks, right_blocks, potential_blocks, weight_blocks),
    )
    core_new = by_axis(partial_core, SRC_TGT)
    current = jnp.dot(core_new, left_target, precision=HIGHEST)

    def row_step(left_block):
        scores = (
            log_target[None, :]
            + (target_potential[None, :] + 2.0 * contract_rank(left_block, current)) / EPSILON
        )
        maxima = jnp.max(scores, axis=1)
        return (maxima, jnp.sum(jnp.exp(scores - maxima[:, None]), axis=1))

    local_max, local_sum = lax.map(row_step, left_blocks)
    local_max = local_max.reshape(row_count)
    local_sum = local_sum.reshape(row_count)
    offset = lax.axis_index(TGT) * share_count
    highest, summed = joined_all((local_max, local_sum), TGT, combine_parts)
    source_new = EPSILON * (log_source - highest - jnp.log(summed))
    own_rows = lax.dynamic_slice_in_dim(source_new, offset, share_count)
    new_blocks = row_blocks(source_new, block_size)

    def column_step(state, portion):
        maxima, totals = state
        left_block, log_weight, source_part = portion
        scores = (
            log_weight[:, None]
            + (source_part[:, None] + 2.0 * contract_rank(left_block, current)) / EPSILON
        )
        highest = jnp.maximum(maxima, jnp.max(scores, axis=0))
        totals = totals * jnp.exp(maxima - highest) + jnp.sum(
            jnp.exp(scores - highest[None, :]), axis=0
        )
        return ((highest, totals), None)

    columns = target_potential.shape[0]
    start = (jnp.full((columns,), -jnp.inf, jnp.float32), jnp.zeros((columns,), jnp.float32))
    (column_max, column_total), _ = lax.scan(
        column_step, start, (left_blocks, weight_blocks, new_blocks)
    )
    highest, summed = combined_all((column_max, column_total), SRC, combine_parts)
    target_new = EPSILON * (log_target - highest - jnp.log(summed))
    return (own_rows, target_new, core_new)


def solution(mesh):
    finer = Mesh(mesh.devices.reshape(4, 2, 4, 16), ("src_0", "src_1", "tgt_0", "tgt_1"))
    placed = (P(None, SRC_TGT), P(SRC, TGT), P(SRC_TGT), P(TGT), P(SRC_TGT), P(TGT), P())
    return jax.shard_map(
        on_device, mesh=finer, in_specs=placed, out_specs=(P(SRC_TGT), P(TGT), P()), check_vma=False
    )
```

profile of v0, /device:TPU:1, one launch (start us, length us, event | category | flops | bytes accessed | tf_op | source)
XLA Modules:
  0.0 303.7 jit_solution(410053554644530980)
XLA Ops:
  0.6 1.4 broadcast_in_dim.44
  2.0 10.1 %all-to-all-start = ((f32[8,4,1024]{2,1,0:T(4,128)}), f32[8,4,1024]{2,1,0:T(4,128)S(1)}, u32[]{:S(2)}, u32[]{:S(2)}) async-start(f32[8,4,1024]{2,1,0:T(4,128)} %broadcast_in_dim.44), calls=%async_computation | async-start | bytes 262144 | tf_op jit(solution)/shard_map/all_to_all | solution.py:31
  12.1 0.8 copy.36
  12.9 0.7 copy.37
  13.7 0.7 copy.38
  14.5 77.8 %all_gather.15 = f32[2048,34]{1,0:T(8,128)S(1)} all-gather(f32[32,34]{1,0:T(8,128)S(1)} %pad_maximum_fusion.4), channel_id=1, replica_groups=mesh['src_0'=4,'src_1'=2,'tgt_0'=4,'tgt_1'=16] {'tgt_0','tgt_1'}, dimensions={0}, use_global_device_ids=true | all-gather | bytes 282880 | tf_op jit(solution)/shard_map/all_gather | solution.py:21
  92.2 1.2 slice_reduce_fusion
  94.7 0.3 convolution_bitcast_fusion
  95.0 19.5 %while.37 = (s32[]{:T(128)}, f32[34,34]{1,0:T(8,128)S(1)}, f32[4,34,512]{2,0,1:T(4,128)S(1)}, f32[4,512]{1,0:T(4,128)S(1)}, f32[1024]{0:T(1024)S(1)}, /*index=5*...) while((s32[]{:T(128)}, f32[34,34]{1,0:T(8,128)S(1)}, ...), condition=%wide.region_3.4_spmd.clone, body=%wide.region_2.3_spmd.clone.sunk | while | flops 438069504 | bytes 4957355 | solution.py:189
  95.0 1.9 fusion.110
  96.9 2.7 fusion.111
  99.9 1.9 fusion.110
  101.8 2.7 fusion.111
  104.8 1.9 fusion.110
  106.7 2.7 fusion.111
  109.7 1.9 fusion.110
  111.5 2.7 fusion.111
  114.5 13.5 %psum.28 = f32[34,34]{1,0:T(8,128)S(1)} all-reduce(f32[34,34]{1,0:T(8,128)S(1)} %get-tuple-element.131), channel_id=1, replica_groups=mesh['src_0'=4,'src_1'=2,'tgt_0'=4,'tgt_1'=16] {'src_0'}, use_global_device_ids=true, to_apply=%region_4.5 | all-reduce | flops 1156 | bytes 9248 | tf_op jit(solution)/shard_map/psum | solution.py:46
  128.0 32.6 %psum.29 = f32[34,34]{1,0:T(8,128)S(1)} all-reduce(f32[34,34]{1,0:T(8,128)S(1)} %psum.28), channel_id=1, replica_groups=mesh['src_0'=4,'src_1'=2,'tgt_0'=4,'tgt_1'=16] {'src_1'}, use_global_device_ids=true, to_apply=%region_5.6 | all-reduce | flops 1156 | bytes 9248 | tf_op jit(solution)/shard_map/psum | solution.py:46
  160.7 12.5 %psum.30 = f32[34,34]{1,0:T(8,128)S(1)} all-reduce(f32[34,34]{1,0:T(8,128)S(1)} %psum.29), channel_id=1, replica_groups=mesh['src_0'=4,'src_1'=2,'tgt_0'=4,'tgt_1'=16] {'tgt_0'}, use_global_device_ids=true, to_apply=%region_6.7 | all-reduce | flops 1156 | bytes 9248 | tf_op jit(solution)/shard_map/psum | solution.py:46
  173.2 39.7 %psum.31 = f32[34,34]{1,0:T(8,128)S(1)} all-reduce(f32[34,34]{1,0:T(8,128)S(1)} %psum.30), channel_id=1, replica_groups=mesh['src_0'=4,'src_1'=2,'tgt_0'=4,'tgt_1'=16] {'tgt_1'}, use_global_device_ids=true, to_apply=%region_7.8 | all-reduce | flops 1156 | bytes 9248 | tf_op jit(solution)/shard_map/psum | solution.py:46
  213.5 11.3 %while.36 = (s32[]{:T(128)}, f32[4,512]{1,0:T(4,128)S(1)}, f32[4,512]{1,0:T(4,128)S(1)}, f32[1024]{0:T(1024)S(1)}, f32[1024]{0:T(1024)S(1)}, /*index=5*/f32[4,34...) while((s32[]{:T(128)}, f32[4,512]{1,0:T(4,128)S(1)}, f32[4,512]{1,0:T(4,128)S(1)}, ...), condition=%wide.region_11.12_spmd, body=%wide.region_8.11_spmd.sunk | while | flops 217578496 | bytes 4462697 | solution.py:205
  213.5 2.2 fusion.104
  215.7 0.5 exponential_reduce_fusion.4
  216.3 2.2 fusion.104
  218.5 0.5 exponential_reduce_fusion.4
  219.1 2.2 fusion.104
  221.3 0.5 exponential_reduce_fusion.4
  222.0 2.2 fusion.104
  224.2 0.5 exponential_reduce_fusion.4
  224.9 9.0 %all-gather.2 = f32[4,2,2048]{2,1,0:T(2,128)S(1)} all-gather(f32[1,2,2048]{2,1,0:T(2,128)S(1)} %maximum_bitcast_fusion.2), channel_id=2, replica_groups=mesh['src_0'=4,'src_1'=2,'tgt_0'=4,'tgt_1'=16] {'tgt_0'}, dimensions={0}, use_global_device_ids=true | all-gather | bytes 81920 | tf_op jit(solution)/shard_map/all_gather | solution.py:57
  233.9 20.8 %all-gather.3 = f32[16,2,2048]{2,1,0:T(2,128)S(1)} all-gather(f32[1,2,2048]{2,1,0:T(2,128)S(1)} %maximum_bitcast_fusion.3), channel_id=3, replica_groups=mesh['src_0'=4,'src_1'=2,'tgt_0'=4,'tgt_1'=16] {'tgt_1'}, dimensions={0}, use_global_device_ids=true | all-gather | bytes 278528 | tf_op jit(solution)/shard_map/all_gather | solution.py:57
  254.8 0.4 slice_reduce_fusion.16
  255.2 0.3 slice_reduce_fusion.14
  256.2 10.2 %while.38 = (s32[]{:T(128)}, f32[1024]{0:T(1024)S(1)}, f32[1024]{0:T(1024)S(1)}, f32[4,512]{1,0:T(4,128)S(1)}, f32[4,512]{1,0:T(4,128)S(1)}, /*index=5*/f32[4,34...) while((s32[]{:T(128)}, f32[1024]{0:T(1024)S(1)}, f32[1024]{0:T(1024)S(1)}, ...), condition=%wide.region_15.16_spmd.clone, body=%wide.region_12.15_spmd.clone.sunk | while | flops 217584640 | bytes 4505712 | solution.py:229
  256.3 2.1 fusion.113
  258.4 0.3 exponential_reduce_fusion.5
  258.8 2.1 fusion.113
  261.0 0.3 exponential_reduce_fusion.5
  261.4 2.1 fusion.113
  263.5 0.3 exponential_reduce_fusion.5
  263.9 2.1 fusion.113
  266.1 0.3 exponential_reduce_fusion.5
  266.5 0.6 broadcast_in_dim.49
  267.1 30.7 %all-to-all-start.1 = ((f32[8,2,1024]{2,1,0:T(2,128)}), f32[8,2,1024]{2,1,0:T(2,128)S(1)}, u32[]{:S(2)}, u32[]{:S(2)}) async-start(f32[8,2,1024]{2,1,0:T(2,128)} %broadcast_in_dim.49), calls=%async_computation.1 | async-start | bytes 131072 | tf_op jit(solution)/shard_map/all_to_all | solution.py:31
  298.0 0.6 fusion.73
  298.6 4.1 %all-to-all-done.1 = f32[8,2,1024]{2,1,0:T(2,128)S(1)} async-done(((f32[8,2,1024]{2,1,0:T(2,128)}), f32[8,2,1024]{2,1,0:T(2,128)S(1)}, u32[]{:S(2)}, u32[]{:S(2)}) %all-to-all-start.1) | async-done | bytes 65568 | tf_op jit(solution)/shard_map/all_to_all | solution.py:31
  303.1 0.6 subtract_multiply_fusion.1
  (126 shorter events, 4.7 us)
Async XLA Ops:
  0.6 94.0 %copy-start = (f32[34,34]{1,0:T(8,128)S(1)}, f32[34,34]{1,0:T(8,128)}, u32[]{:S(2)}) copy-start(f32[34,34]{1,0:T(8,128)} %param.19) | copy-start | bytes 13876
  2.0 92.5 %all-to-all-start = ((f32[8,4,1024]{2,1,0:T(4,128)}), f32[8,4,1024]{2,1,0:T(4,128)S(1)}, u32[]{:S(2)}, u32[]{:S(2)}) async-start(f32[8,4,1024]{2,1,0:T(4,128)} %broadcast_in_dim.44), calls=%async_computation | async-start | bytes 262144 | tf_op jit(solution)/shard_map/all_to_all | solution.py:31
  93.4 1.0 copy-start.2
  93.8 1.2 copy-start.3
  212.9 0.6 copy-start.1
  267.1 35.6 %all-to-all-start.1 = ((f32[8,2,1024]{2,1,0:T(2,128)}), f32[8,2,1024]{2,1,0:T(2,128)S(1)}, u32[]{:S(2)}, u32[]{:S(2)}) async-start(f32[8,2,1024]{2,1,0:T(2,128)} %broadcast_in_dim.49), calls=%async_computation.1 | async-start | bytes 131072 | tf_op jit(solution)/shard_map/all_to_all | solution.py:31
where the time goes:
time: 304 us
  blocking collectives  206 us (68%)
  starting transfers between devices  40.8 us (13%)
  matrix products  36.9 us (12%)
  local copies, waits for them, and re-layouts  7.68 us (3%)
  other arithmetic  6.67 us (2%)
  waiting for transfers between devices  4.13 us (1%)
    psum x4, blocking collectives, by_axis(): return functools.reduce(lax.psum, axes, x)  98.4 us
    all_gather x1, blocking collectives, rows_first(): lax.all_gather(both, axis, axis=0, tiled=True)  77.8 us
    all_to_all x2, starting transfers between devices, sent_to_all(): return lax.all_to_all(copies, axis, split_axis=0, concat_axis=0, tiled=True)  40.8 us
    all_gather x2, blocking collectives, collected_together(): both, at, found = (lax.all_gather(jnp.concatenate(lines), axis), 0, {})  29.8 us
    dot_general x12, matrix products, contract_rank(): lax.dot_general(left_block, weighted, (((0,), (0,)), ((), ())), precision...  24.7 us
    dot_general x8, matrix products, contract_last(): lax.dot_general(former, latter, (((1,), (1,)), ((), ())), precision=HIGHE...  11.6 us
  transfers between devices with their start and end apart: 2, of which 1 were waited for; matrix products, arithmetic and copies ran while one was open for 2% of the time, Pallas kernels for 0%

commit v1 on v0

v1 whole, which is shorter than its diff:
```python
import math

import jax
import jax.numpy as jnp
from jax import lax
from jax.sharding import Mesh
from jax.sharding import PartitionSpec as P

PLANE = ("x", "core", "y")
ALL = ("x", "core", "y", "z")
EPSILON = 0.5
HIGHEST = lax.Precision.HIGHEST


def to_all(flat, axis):
    copies = jnp.broadcast_to(flat, (lax.axis_size(axis), 1, flat.size))
    return lax.all_to_all(copies, axis, split_axis=0, concat_axis=0, tiled=True)


def factors(points):
    squares = jnp.sum(points * points, axis=0, keepdims=True)
    unit_row = jnp.ones_like(squares)
    return (
        jnp.concatenate([squares, unit_row, -2.0 * points], 0),
        jnp.concatenate([unit_row, squares, points], 0),
    )


def contract(former, latter, dims):
    return lax.dot_general(
        former, latter, (dims, ((), ())), precision=HIGHEST, preferred_element_type=jnp.float32
    )


def logsumexp(parts, axis):
    highest = jnp.max(parts, axis=axis, keepdims=True)
    total = jnp.sum(jnp.exp(parts - highest), axis=axis)
    return jnp.squeeze(highest, axis) + jnp.log(total)


def on_device(
    source_points,
    target_points,
    source_potential,
    target_potential,
    source_weight,
    target_weight,
    core_previous,
):
    emb, own = source_points.shape
    dims, span = target_points.shape
    n_z, n_y, n_src = lax.axis_size("z"), lax.axis_size("y"), lax.axis_size(("x", "core"))
    log_sources = math.log(own * n_z * n_y * n_src)
    log_targets = math.log(span * n_z * n_y)
    src = lax.axis_index(("x", "core"))
    z = lax.axis_index("z")
    share = span // n_src

    mine = jnp.concatenate(
        [source_points.reshape(-1), source_potential, source_weight, jnp.zeros((64,), jnp.float32)]
    )
    rows = to_all(mine, "z")
    rows = rows.reshape(n_z, -1)
    points = jnp.moveaxis(rows[:, : emb * own].reshape(n_z, emb, own), 0, 1).reshape(emb, -1)
    potential = rows[:, emb * own : emb * own + own].reshape(-1)
    weight = rows[:, emb * own + own : emb * own + 2 * own].reshape(-1)

    part = lambda a: lax.dynamic_slice_in_dim(a, src * share, share)
    theirs = jnp.concatenate(
        [target_points.reshape(-1), part(target_potential), part(target_weight)]
    )
    columns = to_all(theirs, PLANE)
    columns = columns.reshape(n_src, n_y, -1)
    features = jnp.moveaxis(
        columns[:, :, : dims * span].reshape(n_src, n_y, dims, span), 1, 2
    ).reshape(emb, -1)
    offsets = jnp.moveaxis(columns[:, :, dims * span : dims * span + share], 0, 1).reshape(-1)
    masses = jnp.moveaxis(columns[:, :, dims * span + share :], 0, 1).reshape(-1)

    log_source = jnp.log(weight) - jnp.float32(log_sources)
    log_target = jnp.log(masses) - jnp.float32(log_targets)
    left_source, right_source = factors(points)
    left_target, right_target = factors(features)

    weighted = contract(core_previous, left_source, ((0,), (0,)))
    scores = contract(left_target, weighted, ((0,), (0,)))
    plan = jnp.exp(
        log_source[None, :]
        + log_target[:, None]
        + (potential[None, :] + offsets[:, None] + 2.0 * scores) / EPSILON
    )
    carried = contract(right_source, plan, ((1,), (1,)))
    partial = contract(carried, right_target, ((1,), (1,)))
    rank = partial.shape[0]
    flat = jnp.pad(partial.reshape(-1), (0, -rank * rank % 128))
    flat = jnp.sum(to_all(flat, PLANE), axis=0).reshape(-1)
    flat = jnp.sum(to_all(flat, "z"), axis=0).reshape(-1)
    core_new = flat[: rank * rank].reshape(rank, rank)

    weighted = contract(core_new, left_source, ((0,), (0,)))
    cross = contract(left_target, weighted, ((0,), (0,)))
    row_parts = logsumexp(log_target[:, None] + (offsets[:, None] + 2.0 * cross) / EPSILON, 0)
    row_parts = to_all(row_parts, "z").reshape(n_z, -1)
    source_new = EPSILON * (log_source - logsumexp(row_parts, 0))
    own_rows = lax.dynamic_slice_in_dim(source_new, z * own, own)

    column_parts = logsumexp(log_source[None, :] + (source_new[None, :] + 2.0 * cross) / EPSILON, 1)
    pieces = column_parts.reshape(1, n_y, 1, span)
    pieces = jnp.broadcast_to(pieces, (n_src, n_y, 1, span)).reshape(-1, 1, span)
    pieces = lax.all_to_all(pieces, PLANE, split_axis=0, concat_axis=0, tiled=True)
    log_own = jnp.log(target_weight) - jnp.float32(log_targets)
    target_new = EPSILON * (log_own - logsumexp(pieces.reshape(-1, span), 0))
    return (own_rows, target_new, core_new)


def solution(mesh):
    finer = Mesh(mesh.devices.reshape(4, 2, 4, 16), ALL)
    source, target = P(ALL), P(("y", "z"))
    placed = (
        P(None, ALL),
        P(("x", "core"), ("y", "z")),
        source,
        target,
        source,
        target,
        P(),
    )
    return jax.shard_map(
        on_device, mesh=finer, in_specs=placed, out_specs=(source, target, P()), check_vma=False
    )
```

time: 304 us -> 153 us (0.50)
  blocking collectives: 206 us -> 42 us
  waiting for transfers between devices: 4.13 us -> 26.8 us
  matrix products: 36.9 us -> 25.7 us
  starting transfers between devices: 40.8 us -> 31.1 us
  other arithmetic: 6.67 us -> 13.2 us
  local copies, waits for them, and re-layouts: 7.68 us -> 12.5 us
    all_gather x3 -> x0, blocking collectives: 108 us -> none  [the longest x1 77.8 us: rows_first(): lax.all_gather(both, axis, axis=0, tiled=True)]
    psum x4 -> x0, blocking collectives: 98.4 us -> none  [by_axis(): return functools.reduce(lax.psum, axes, x)]
    all_to_all x0 -> x3, blocking collectives: none -> 42 us  [to_all(): return lax.all_to_all(copies, axis, split_axis=0, concat_axis=0, tiled=True)]
    all_to_all x2 -> x3, waiting for transfers between devices: 4.13 us -> 26.8 us  [the longest x2 19.7 us: to_all(): return lax.all_to_all(copies, axis, split_axis=0, concat_axis=0, tiled=True)]
    dot_general x22 -> x6, matrix products: 36.9 us -> 25.7 us  [contract(): lax.dot_general(former, latter, (dims, ((), ())), precision=HIGHEST, pref...]
    all_to_all x2 -> x3, starting transfers between devices: 40.8 us -> 31.1 us  [the longest x2 25.1 us: to_all(): return lax.all_to_all(copies, axis, split_axis=0, concat_axis=0, tiled=True)]
    reduce_max x0 -> x3, other arithmetic: none -> 5.12 us  [logsumexp(): highest = jnp.max(parts, axis=axis, keepdims=True)]
    unnamed x12 -> x14, local copies, waits for them, and re-layouts: 1.45 us -> 5.02 us
  transfers between devices with their start and end apart: 2 -> 3, of which waited for: 1 -> 3; matrix products, arithmetic and copies ran while one was open for 2% -> 3% of each run, Pallas kernels for 0% -> 0%
where the time goes in v1:
time: 153 us; the launch traced here: 152 us
  blocking collectives  42 us (27%)
  starting transfers between devices  31.1 us (20%)
  waiting for transfers between devices  26.8 us (18%)
  matrix products  25.7 us (17%)
  other arithmetic  13.2 us (9%)
  local copies, waits for them, and re-layouts  12.5 us (8%)
    all_to_all x3, blocking collectives, to_all(): return lax.all_to_all(copies, axis, split_axis=0, concat_axis=0, tiled=True)  42 us
    dot_general x6, matrix products, contract(): lax.dot_general(former, latter, (dims, ((), ())), precision=HIGHEST, pref...  25.7 us
    all_to_all x2, starting transfers between devices, to_all(): return lax.all_to_all(copies, axis, split_axis=0, concat_axis=0, tiled=True)  25.1 us
    all_to_all x2, waiting for transfers between devices, to_all(): return lax.all_to_all(copies, axis, split_axis=0, concat_axis=0, tiled=True)  19.7 us
    all_to_all x1, waiting for transfers between devices, on_device(): lax.all_to_all(pieces, PLANE, split_axis=0, concat_axis=0, tiled=True)  7.06 us
    all_to_all x1, starting transfers between devices, on_device(): lax.all_to_all(pieces, PLANE, split_axis=0, concat_axis=0, tiled=True)  6.01 us
    reduce_sum x4, other arithmetic, logsumexp(): total = jnp.sum(jnp.exp(parts - highest), axis=axis)  5.67 us
    reduce_max x3, other arithmetic, logsumexp(): highest = jnp.max(parts, axis=axis, keepdims=True)  5.12 us
  transfers between devices with their start and end apart: 3, of which 3 were waited for; matrix products, arithmetic and copies ran while one was open for 3% of the time, Pallas kernels for 0%

profile of v1, /device:TPU:1, one launch (start us, length us, event | category | flops | bytes accessed | tf_op | source)
XLA Modules:
  0.0 152.3 jit_solution(2726455358651262516)
XLA Ops:
  0.6 0.0 copy-start
  0.6 0.8 reshape.109
  1.4 0.7 concatenate.18
  2.2 0.7 broadcast_in_dim.47
  2.8 15.7 %all-to-all-start = ((f32[16,1,1152]{2,1,0:T(1,128)}), f32[16,1,1152]{2,1,0:T(1,128)S(1)}, u32[]{:S(2)}, u32[]{:S(2)}) async-start(f32[16,1,1152]{2,1,0:T(1,128)} %broadcast_in_dim.47), calls=%async_computation | async-start | bytes 147456 | tf_op jit(solution)/shard_map/all_to_all | solution.py:17
  18.6 0.8 dynamic_slice.9
  19.4 0.8 dynamic_slice.10
  20.1 0.7 copy.47
  20.9 9.4 %all-to-all-done = f32[16,1,1152]{2,1,0:T(1,128)S(1)} async-done(((f32[16,1,1152]{2,1,0:T(1,128)}), f32[16,1,1152]{2,1,0:T(1,128)S(1)}, u32[]{:S(2)}, u32[]{:S(2)}) %all-to-all-start) | async-done | bytes 73760 | tf_op jit(solution)/shard_map/all_to_all | solution.py:17
  30.3 1.1 broadcast_in_dim.48
  31.4 9.4 %all-to-all-start.1 = ((f32[32,1,4352]{2,1,0:T(1,128)}), f32[32,1,4352]{2,1,0:T(1,128)S(1)}, u32[]{:S(2)}, u32[]{:S(2)}) async-start(f32[32,1,4352]{2,1,0:T(1,128)} %broadcast_in_dim.48), calls=%async_computation.1 | async-start | bytes 1114112 | tf_op jit(solution)/shard_map/all_to_all | solution.py:17
  40.8 0.1 fusion.44
  40.9 0.1 add.121
  41.0 0.1 sub.61
  41.0 0.1 reshape.115
  41.2 0.1 broadcast_in_dim.52
  41.3 0.2 copy.26
  41.4 0.1 reshape.116
  41.6 0.3 fusion.31
  41.9 10.2 %all-to-all-done.1 = f32[32,1,4352]{2,1,0:T(1,128)S(1)} async-done(((f32[32,1,4352]{2,1,0:T(1,128)}), f32[32,1,4352]{2,1,0:T(1,128)S(1)}, u32[]{:S(2)}, u32[]{:S(2)}) %all-to-all-start.1) | async-done | bytes 557088 | tf_op jit(solution)/shard_map/all_to_all | solution.py:17
  52.1 1.3 reduce.6
  53.5 0.2 reshape.112
  53.7 0.1 multiply_reduce_fusion
  53.8 0.3 copy.39
  54.2 6.8 %fusion.22 = f32[4096,512]{1,0:T(8,128)S(1)} fusion(f32[512,34]{0,1:T(8,128)S(1)} %fusion.31, f32[32,4096]{1,0:T(8,128)S(1)} %broadcast_multiply_fusion, f32[1,4096]{1,0:T(1,128)S(1)} %broadcast_in_dim.50, f32[1,4096]{1,0:T(1,128)S(1)} %bitcast.50), kind=kOutput, calls=%fused_computation.28 | convolution fusion | flops 855916544 | bytes 9015296 | tf_op jit(solution)/shard_map/dot_general | solution.py:30
  61.1 9.6 %fusion = f32[34,4096]{1,0:T(8,128)S(1)} fusion(f32[4096,512]{1,0:T(8,128)S(1)} %fusion.22, f32[512]{0:T(512)S(1)} %add.121, f32[512]{0:T(512)S(1)} %sub.61, f32[4096]{0:T(1024)S(1)} %get-tuple-element.9, f32[4096]{0:T(1024)S(1)} %get-tuple-element.10, f32[32,512]{1,0:T(8,128)S(1)} %reshape.116, f32[1,512]{1,0:T(1,128)S(1)} %broadcast_in_dim.52, ...), kind=kOutput, calls=%fused_computation.4 | convolution fusion | flops 868255744 | bytes 9052160 | tf_op jit(solution)/shard_map/dot_general | solution.py:30
  70.7 0.7 fusion.15
  71.4 0.1 reshape.117
  71.6 0.1 broadcast_in_dim.53
  71.6 12.2 %all_to_all.30 = f32[32,1,1280]{2,1,0:T(1,128)S(1)} all-to-all(f32[32,1,1280]{2,1,0:T(1,128)S(1)} %broadcast_in_dim.53), channel_id=1, replica_groups=mesh['x'=4,'core'=2,'y'=4,'z'=16] {'x','core','y'}, dimensions={0} | all-to-all | bytes 327680 | tf_op jit(solution)/shard_map/all_to_all | solution.py:17
  83.8 0.1 reduce_sum.76
  84.0 14.3 %all_to_all.31 = f32[16,1,1280]{2,1,0:T(1,128)S(1)} all-to-all(f32[16,1,1280]{2,1,0:T(1,128)S(1)} %broadcast_in_dim.54), channel_id=1, replica_groups=mesh['x'=4,'core'=2,'y'=4,'z'=16] {'z'}, dimensions={0} | all-to-all | bytes 163840 | tf_op jit(solution)/shard_map/all_to_all | solution.py:17
  98.3 0.1 reduce_sum.77
  98.4 0.1 reshape.118
  98.5 0.3 fusion.30
  98.8 8.0 %fusion.8 = (f32[512]{0:T(512)S(1)}, f32[4096,512]{1,0:T(8,128)S(1)}) fusion(f32[4096]{0:T(1024)S(1)} %get-tuple-element.9, f32[4096]{0:T(1024)S(1)} %get-tuple-element.10, f32[34,512]{1,0:T(8,128)S(1)} %fusion.30, f32[32,4096]{1,0:T(8,128)S(1)} %broadcast_multiply_fusion, f32[1,4096]{1,0:T(1,128)S(1)} %broadcast_in_dim.50, f32[1,4096]{1,0:T(1,128)S(1)} %bitcast.52), kind=kOutput, calls=%fused_computation.12 | convolution fusion | flops 866401792 | bytes 9050112 | tf_op jit(solution)/shard_map/dot_general | solution.py:30
  106.8 3.2 %copy-done.1 = f32[4096,512]{1,0:T(8,128)} copy-done((f32[4096,512]{1,0:T(8,128)}, f32[4096,512]{1,0:T(8,128)S(1)}, u32[]{:S(2)}) %copy-start.1) | copy-done | bytes 8388632
  110.0 2.9 %exponential_reduce_fusion.1 = f32[512]{0:T(512)S(1)} fusion(f32[4096,512]{1,0:T(8,128)S(1)} %get-tuple-element.8, f32[512]{0:T(512)S(1)} %get-tuple-element.7, f32[4096]{0:T(1024)S(1)} %get-tuple-element.9, f32[4096]{0:T(1024)S(1)} %get-tuple-element.10), kind=kLoop, calls=%fused_computation.2 | loop fusion | flops 12582400 | bytes 8425472 | tf_op jit(solution)/shard_map/reduce_sum | solution.py:37
  113.0 15.6 %all_to_all.32 = f32[16,1,512]{2,1,0:T(1,128)S(1)} all-to-all(f32[16,1,512]{2,1,0:T(1,128)S(1)} %broadcast_in_dim.55), channel_id=1, replica_groups=mesh['x'=4,'core'=2,'y'=4,'z'=16] {'z'}, dimensions={0} | all-to-all | bytes 65536 | tf_op jit(solution)/shard_map/all_to_all | solution.py:17
  128.6 5.0 %fusion.9 = f32[4096]{0:T(1024)S(1)} fusion(f32[4096,512]{1,0:T(8,128)} %copy-done.1, f32[512]{0:T(512)S(1)} %subtract_multiply_fusion.1, f32[512]{0:T(512)S(1)} %sub.61), kind=kLoop, calls=%fused_computation.13 | loop fusion | flops 10481664 | bytes 8409088 | tf_op jit(solution)/shard_map/reduce_max | solution.py:36
  133.6 0.7 copy-done.2
  134.3 2.7 %exponential_reduce_fusion = f32[4096]{0:T(1024)S(1)} fusion(f32[4096,512]{1,0:T(8,128)S(1)} %copy-done.2, f32[4096]{0:T(1024)S(1)} %fusion.9, f32[512]{0:T(512)S(1)} %subtract_multiply_fusion.1, f32[512]{0:T(512)S(1)} %sub.61), kind=kLoop, calls=%fused_computation | loop fusion | flops 12578816 | bytes 8425472 | tf_op jit(solution)/shard_map/reduce_sum | solution.py:37
  137.1 0.8 broadcast_in_dim.57
  137.9 6.0 %all-to-all-start.5 = ((f32[32,1,1024]{2,1,0:T(1,128)}), f32[32,1,1024]{2,1,0:T(1,128)S(1)}, u32[]{:S(2)}, u32[]{:S(2)}) async-start(f32[32,1,1024]{2,1,0:T(1,128)} %broadcast_in_dim.57), calls=%async_computation.5 | async-start | bytes 262144 | tf_op jit(solution)/shard_map/all_to_all | solution.py:110
  143.9 0.6 dynamic_slice.11
  144.5 7.1 %all-to-all-done.5 = f32[32,1,1024]{2,1,0:T(1,128)S(1)} async-done(((f32[32,1,1024]{2,1,0:T(1,128)}), f32[32,1,1024]{2,1,0:T(1,128)S(1)}, u32[]{:S(2)}, u32[]{:S(2)}) %all-to-all-start.5) | async-done | bytes 131104 | tf_op jit(solution)/shard_map/all_to_all | solution.py:110
  151.6 0.1 reduce_max.39
  151.7 0.6 subtract_multiply_fusion
  (33 shorter events, 0.5 us)
Async XLA Ops:
  0.6 41.0 %copy-start = (f32[34,34]{1,0:T(8,128)S(1)}, f32[34,34]{1,0:T(8,128)}, u32[]{:S(2)}) copy-start(f32[34,34]{1,0:T(8,128)} %param.13) | copy-start | bytes 13876
  2.8 27.4 %all-to-all-start = ((f32[16,1,1152]{2,1,0:T(1,128)}), f32[16,1,1152]{2,1,0:T(1,128)S(1)}, u32[]{:S(2)}, u32[]{:S(2)}) async-start(f32[16,1,1152]{2,1,0:T(1,128)} %broadcast_in_dim.47), calls=%async_computation | async-start | bytes 147456 | tf_op jit(solution)/shard_map/all_to_all | solution.py:17
  31.4 20.8 %all-to-all-start.1 = ((f32[32,1,4352]{2,1,0:T(1,128)}), f32[32,1,4352]{2,1,0:T(1,128)S(1)}, u32[]{:S(2)}, u32[]{:S(2)}) async-start(f32[32,1,4352]{2,1,0:T(1,128)} %broadcast_in_dim.48), calls=%async_computation.1 | async-start | bytes 1114112 | tf_op jit(solution)/shard_map/all_to_all | solution.py:17
  98.5 8.3 %copy-start.3 = (f32[34,34]{1,0:T(8,128)}, f32[34,34]{1,0:T(8,128)S(1)}, u32[]{:S(2)}) copy-start(f32[34,34]{1,0:T(8,128)S(1)} %reshape.118) | copy-start | bytes 13876
  106.8 3.2 %copy-start.1 = (f32[4096,512]{1,0:T(8,128)}, f32[4096,512]{1,0:T(8,128)S(1)}, u32[]{:S(2)}) copy-start(f32[4096,512]{1,0:T(8,128)S(1)} %get-tuple-element.8) | copy-start | bytes 25165828
  128.6 5.8 %copy-start.2 = (f32[4096,512]{1,0:T(8,128)S(1)}, f32[4096,512]{1,0:T(8,128)}, u32[]{:S(2)}) copy-start(f32[4096,512]{1,0:T(8,128)} %copy-done.1) | copy-start | bytes 25165828
  128.6 23.1 %copy-start.4 = (f32[1024]{0:T(1024)S(1)}, f32[1024]{0:T(1024)}, u32[]{:S(2)}) copy-start(f32[1024]{0:T(1024)} %param.12) | copy-start | bytes 12292
  137.9 13.7 %all-to-all-start.5 = ((f32[32,1,1024]{2,1,0:T(1,128)}), f32[32,1,1024]{2,1,0:T(1,128)S(1)}, u32[]{:S(2)}, u32[]{:S(2)}) async-start(f32[32,1,1024]{2,1,0:T(1,128)} %broadcast_in_dim.57), calls=%async_computation.5 | async-start | bytes 262144 | tf_op jit(solution)/shard_map/all_to_all | solution.py:110

commit v2 on v1

v2 whole, which is shorter than its diff:
```python
import math

import jax
import jax.numpy as jnp
from jax import lax
from jax.experimental import pallas as pl
from jax.experimental.pallas import tpu as pltpu
from jax.sharding import Mesh
from jax.sharding import PartitionSpec as P

PLANE = ("x", "core", "y")
ALL = ("x", "core", "y", "z")
EPSILON = 0.5
HIGHEST = lax.Precision.HIGHEST
LANES = 128
PAD = 40
DEPTH = 256
LOG2E = math.log2(math.e)
LN2 = math.log(2.0)
F32, BF16 = jnp.float32, jnp.bfloat16
VMEM = pl.BlockSpec(memory_space=pltpu.VMEM)
SMEM = pl.BlockSpec(memory_space=pltpu.SMEM)


def call(body, outs, n_smem, args, scratch=(), name=None):
    specs = [SMEM] * n_smem + [VMEM] * (len(args) - n_smem)
    return pl.pallas_call(
        body,
        out_shape=tuple(jax.ShapeDtypeStruct(s, d) for s, d in outs),
        in_specs=specs,
        out_specs=tuple(VMEM for _ in outs),
        scratch_shapes=list(scratch),
        compiler_params=pltpu.CompilerParams(vmem_limit_bytes=48 * 2**20),
        name=name,
    )(*args)


def exchange(copies, axis):
    return lax.all_to_all(copies, axis, split_axis=0, concat_axis=0, tiled=True)


def dot(former, latter, dims, precision=None):
    return lax.dot_general(
        former, latter, (dims, ((), ())), precision=precision, preferred_element_type=F32
    )


def split(value):
    first = value.astype(BF16).astype(F32)
    rest = value - first
    second = rest.astype(BF16).astype(F32)
    return first, second, rest - second


def stacked(pieces, order):
    blocks = [pieces[k] for k in order]
    filler = jnp.zeros((DEPTH - PAD * len(order), pieces[0].shape[1]), F32)
    return jnp.concatenate([*blocks, filler], 0).astype(BF16)


LATTER_ORDER = (0, 0, 1, 0, 2, 1)
FORMER_ORDER = (0, 1, 0, 2, 0, 1)


def pack_rows(points, potential, weight, out):
    value = points[...]
    block = jnp.concatenate([value[8 * k : 8 * k + 8] for k in range(4)], axis=1)
    last = jnp.concatenate(
        [potential[...], weight[...], jnp.ones((1, LANES - 64), F32)], axis=1
    )
    both = jnp.concatenate([block, last], 0)
    for k in range(out.shape[0] // 9):
        out[9 * k : 9 * k + 9, :] = both


def pack_columns(where, points, potential, weight, out, held):
    for r in range(4):
        for k in range(8):
            held[8 * r + k : 8 * r + k + 1, :] = points[r : r + 1, LANES * k : LANES * k + LANES]
    src = where[0]
    held[32:33, :] = potential[pl.ds(src, 1), :]
    held[33:34, :] = weight[pl.ds(src, 1), :]
    both = held[0:34, :]
    for k in range(out.shape[0] // 34):
        out[34 * k : 34 * k + 34, :] = both


def column_stack(log_targets):
    def body(message, out):
        for y in range(4):
            for k in range(8):
                points = jnp.concatenate(
                    [message[pl.ds(34 * (4 * s + y) + k, 4, stride=8), :] for s in range(8)], 0
                )
                squares = jnp.sum(points * points, 0, keepdims=True)
                at = 34 * (4 * k + y) + 32
                offset = jnp.log(message[at + 1 : at + 2, :]) - log_targets
                offset = (offset + message[at : at + 1, :] * (1.0 / EPSILON)) * LOG2E
                tail = jnp.concatenate(
                    [squares, jnp.ones((1, LANES), F32), offset, jnp.zeros((5, LANES), F32)], 0
                )
                value = jnp.concatenate([points, tail], 0)
                col = 1024 * y + LANES * k
                out[:, col : col + LANES] = stacked(split(value), LATTER_ORDER)

    return body


def signs(core):
    row = lax.broadcasted_iota(jnp.int32, core.shape, 0)
    col = lax.broadcasted_iota(jnp.int32, core.shape, 1)
    core = jnp.where(row < 32, -2.0 * core, core)
    return jnp.where(col < 32, -2.0 * core, core)


def former_stack(core, features, row_term, column_factor):
    weighted = dot(signs(core), features, ((0,), (0,)), HIGHEST) * (2.0 / EPSILON * LOG2E)
    row = lax.broadcasted_iota(jnp.int32, weighted.shape, 0)
    if row_term is not None:
        weighted = jnp.where(row == 33, weighted + row_term * LOG2E, weighted)
    weighted = jnp.where(row == 34, column_factor, weighted)
    return stacked(split(weighted), FORMER_ORDER)


def core_kernel(log_sources, blocks):
    def body(message, columns, core, packed, features_out, log_out, former, total):
        pieces = []
        for k in range(4):
            pieces.append(
                jnp.concatenate(
                    [message[9 * z : 9 * z + 8, 32 * k : 32 * k + 32] for z in range(16)], 1
                )
            )
        points = jnp.concatenate(pieces, 0)
        last = jnp.concatenate([message[9 * z + 8 : 9 * z + 9, 0:32] for z in range(16)], 1)
        weight = jnp.concatenate([message[9 * z + 8 : 9 * z + 9, 32:64] for z in range(16)], 1)
        squares = jnp.sum(points * points, 0, keepdims=True)
        ones = jnp.ones_like(squares)
        zeros = jnp.zeros((6, squares.shape[1]), F32)
        features = jnp.concatenate([points, squares, ones, zeros], 0)
        log_source = jnp.log(weight) - log_sources
        features_out[...] = features
        log_out[...] = log_source
        former[...] = former_stack(
            core[...], features, log_source + last * (1.0 / EPSILON), 1.0
        )
        total[...] = jnp.zeros_like(total)
        width = columns.shape[1] // blocks

        def step(b, _):
            at = pl.multiple_of(b * width, width)
            stack = columns[:, pl.ds(at, width)]
            plan = jnp.exp2(dot(former[...], stack, ((0,), (0,))))
            high = plan.astype(BF16)
            low = (plan - high.astype(F32)).astype(BF16)
            total[...] += dot(high, stack, ((1,), (1,))) + dot(low, stack, ((1,), (1,)))
            return 0

        lax.fori_loop(0, blocks, step, 0)
        carried = (
            total[:, 0:PAD] + total[:, 2 * PAD : 3 * PAD] + total[:, 4 * PAD : 5 * PAD]
        )
        right = jnp.concatenate([points, ones, squares, zeros], 0)
        core_part = dot(right, carried, ((1,), (0,)), HIGHEST)
        col = lax.broadcasted_iota(jnp.int32, core_part.shape, 1)
        ahead = jnp.concatenate([core_part[:, 1:], core_part[:, :1]], 1)
        behind = jnp.concatenate([core_part[:, -1:], core_part[:, :-1]], 1)
        core_part = jnp.where(col == 32, ahead, jnp.where(col == 33, behind, core_part))
        core_part = jnp.where(col < 34, core_part, 0.0)
        both = jnp.concatenate(
            [core_part[12 * g : 12 * g + 12] for g in range(3)] + [jnp.zeros((12, 8), F32)], 1
        )
        for k in range(packed.shape[0] // 12):
            packed[12 * k : 12 * k + 12, :] = both

    return body


def row_kernel(blocks):
    def body(parts, features, columns, out, core_out, former, scores):
        both = parts[0:12, :]
        for k in range(1, parts.shape[0] // 12):
            both = both + parts[12 * k : 12 * k + 12, :]
        core = jnp.concatenate([both[:, PAD * g : PAD * g + PAD] for g in range(3)], 0)
        core = jnp.concatenate([core, jnp.zeros((PAD - 36, PAD), F32)], 0)
        core_out[...] = core
        former[...] = former_stack(core, features[...], None, 1.0)
        width = columns.shape[1] // blocks
        rows = features.shape[1]

        def fill(b, highest):
            at = pl.multiple_of(b * width, width)
            tile = dot(former[...], columns[:, pl.ds(at, width)], ((0,), (0,)))
            scores[:, pl.ds(at, width)] = tile
            for k in range(width // LANES):
                highest = jnp.maximum(highest, tile[:, LANES * k : LANES * k + LANES])
            return highest

        highest = lax.fori_loop(0, blocks, fill, jnp.full((rows, LANES), -jnp.inf, F32))
        highest = jnp.max(highest, 1, keepdims=True)

        def add(b, total):
            at = pl.multiple_of(b * width, width)
            tile = jnp.exp2(scores[:, pl.ds(at, width)] - highest)
            for k in range(width // LANES):
                total = total + tile[:, LANES * k : LANES * k + LANES]
            return total

        total = lax.fori_loop(0, blocks, add, jnp.zeros((rows, LANES), F32))
        total = jnp.sum(total, 1, keepdims=True)
        part = highest * LN2 + jnp.log(total)
        wide = jnp.broadcast_to(part, (rows, LANES))
        flat = [jnp.transpose(wide[LANES * k : LANES * k + LANES])[0:1] for k in range(4)]
        both = jnp.concatenate(flat, 0)
        for k in range(out.shape[0] // 4):
            out[4 * k : 4 * k + 4, :] = both

    return body


def combined(values):
    highest = functools_max(values)
    total = sum(jnp.exp(v - highest) for v in values)
    return highest + jnp.log(total)


def functools_max(values):
    highest = values[0]
    for v in values[1:]:
        highest = jnp.maximum(highest, v)
    return highest


def column_kernel(blocks):
    def body(where, parts, features, log_source, core, columns, source_out, out, former, held):
        merged = combined([parts[4 * k : 4 * k + 4, :] for k in range(parts.shape[0] // 4)])
        merged = jnp.concatenate([merged[k : k + 1] for k in range(4)], 1)
        logs = log_source[...]
        source_new = EPSILON * (logs - merged)
        source_out[...] = source_new
        former[...] = former_stack(
            core[...], features[...], logs + source_new * (1.0 / EPSILON), 0.0
        )
        width = columns.shape[1] // blocks
        per_piece = 1024 // width

        for b in range(blocks):
            tile = dot(former[...], columns[:, width * b : width * b + width], ((0,), (0,)))
            highest = jnp.max(tile, 0, keepdims=True)
            total = jnp.sum(jnp.exp2(tile - highest), 0, keepdims=True)
            part = highest * LN2 + jnp.log(total)
            for k in range(width // LANES):
                at = (b * width + LANES * k) // LANES
                held[at : at + 1, :] = part[:, LANES * k : LANES * k + LANES]
        for y in range(4):
            piece = held[8 * y : 8 * y + 8, :]
            for s in range(8):
                at = 8 * (4 * s + y)
                out[at : at + 8, :] = piece

    return body


def last_kernel(log_targets):
    def body(parts, weight, out):
        merged = combined([parts[8 * k : 8 * k + 8, :] for k in range(parts.shape[0] // 8)])
        out[...] = EPSILON * (jnp.log(weight[...]) - log_targets - merged)

    return body


def turned(core):
    core = jnp.concatenate([core[2:], core[:2]], 0)
    return jnp.concatenate([core[:, 2:], core[:, :2]], 1)


def turned_back(core):
    core = jnp.concatenate([core[32:34], core[:32]], 0)
    return jnp.concatenate([core[:, 32:34], core[:, :32]], 1)


def on_device(
    source_points,
    target_points,
    source_potential,
    target_potential,
    source_weight,
    target_weight,
    core_previous,
):
    emb, own = source_points.shape
    dims, span = target_points.shape
    n_z, n_y, n_src = lax.axis_size("z"), lax.axis_size("y"), lax.axis_size(("x", "core"))
    n_plane = n_src * n_y
    rows, columns = own * n_z, span * n_y
    log_sources = math.log(own * n_z * n_plane)
    log_targets = math.log(span * n_z * n_y)
    where = jnp.stack([lax.axis_index(("x", "core")), lax.axis_index("y")]).astype(jnp.int32)
    z = lax.axis_index("z")

    (mine,) = call(
        pack_rows,
        [((9 * n_z, LANES), F32)],
        0,
        (source_points, source_potential.reshape(1, own), source_weight.reshape(1, own)),
        name="pack_rows",
    )
    (theirs,) = call(
        pack_columns,
        [((34 * n_plane, LANES), F32)],
        1,
        (where, target_points, target_potential.reshape(8, LANES), target_weight.reshape(8, LANES)),
        scratch=[pltpu.VMEM((40, LANES), F32)],
        name="pack_columns",
    )
    theirs = exchange(theirs.reshape(n_plane, 1, 34 * LANES), PLANE).reshape(-1, LANES)
    mine = exchange(mine.reshape(n_z, 1, 9 * LANES), "z").reshape(-1, LANES)
    (stack,) = call(
        column_stack(log_targets), [((DEPTH, columns), BF16)], 0, (theirs,), name="column_stack"
    )
    previous = jnp.pad(turned(core_previous), ((0, PAD - 34), (0, PAD - 34)))
    former = pltpu.VMEM((DEPTH, rows), BF16)
    packed, features, log_source = call(
        core_kernel(log_sources, 8),
        [((12 * n_plane, LANES), F32), ((PAD, rows), F32), ((1, rows), F32)],
        0,
        (mine, stack, previous),
        scratch=[former, pltpu.VMEM((rows, DEPTH), F32)],
        name="core",
    )
    parts = exchange(packed.reshape(n_plane, 1, 12 * LANES), PLANE)
    parts = jnp.broadcast_to(jnp.sum(parts, 0, keepdims=True), (n_z, 1, 12 * LANES))
    parts = exchange(parts, "z").reshape(-1, LANES)

    row_parts, core_new = call(
        row_kernel(8),
        [((4 * n_z, LANES), F32), ((PAD, PAD), F32)],
        0,
        (parts, features, stack),
        scratch=[former, pltpu.VMEM((rows, columns), F32)],
        name="rows",
    )
    row_parts = exchange(row_parts.reshape(n_z, 1, rows), "z").reshape(-1, LANES)
    source_new, column_parts = call(
        column_kernel(8),
        [((1, rows), F32), ((8 * n_plane, LANES), F32)],
        1,
        (where, row_parts, features, log_source, core_new, stack),
        scratch=[former, pltpu.VMEM((columns // LANES, LANES), F32)],
        name="columns",
    )
    column_parts = exchange(column_parts.reshape(n_plane, 1, span), PLANE).reshape(-1, LANES)
    (target_new,) = call(
        last_kernel(log_targets),
        [((8, LANES), F32)],
        0,
        (column_parts, target_weight.reshape(8, LANES)),
        name="last",
    )
    own_rows = lax.dynamic_slice_in_dim(source_new.reshape(rows), z * own, own)
    return (own_rows, target_new.reshape(span), turned_back(core_new))


def solution(mesh):
    finer = Mesh(mesh.devices.reshape(4, 2, 4, 16), ALL)
    source, target = P(ALL), P(("y", "z"))
    placed = (
        P(None, ALL),
        P(("x", "core"), ("y", "z")),
        source,
        target,
        source,
        target,
        P(),
    )
    return jax.shard_map(
        on_device, mesh=finer, in_specs=placed, out_specs=(source, target, P()), check_vma=False
    )
```

time: 153 us -> 126 us (0.82)
  matrix products: 25.7 us -> 0 us
  Pallas kernels: 0 us -> 18 us
  blocking collectives: 42 us -> 28.4 us
  other arithmetic: 13.2 us -> 1.12 us
  waiting for transfers between devices: 26.8 us -> 36.2 us
  local copies, waits for them, and re-layouts: 12.5 us -> 6.17 us
  starting transfers between devices: 31.1 us -> 34.3 us
    dot_general x6 -> x0, matrix products: 25.7 us -> none  [contract(): lax.dot_general(former, latter, (dims, ((), ())), precision=HIGHEST, pref...]
    pallas_call x0 -> x7, Pallas kernels: none -> 18 us  [call(): pl.pallas_call(body, out_shape=tuple((jax.ShapeDtypeStruct(s, d) for s, d...]
    all_to_all x3 -> x2, blocking collectives: 42 us -> 28.4 us  [exchange(): return lax.all_to_all(copies, axis, split_axis=0, concat_axis=0, tiled=True)]
    all_to_all x3 -> x4, waiting for transfers between devices: 26.8 us -> 36.2 us  [exchange(): return lax.all_to_all(copies, axis, split_axis=0, concat_axis=0, tiled=True)]
    reduce_sum x8 -> x1, other arithmetic: 6.01 us -> 0.13 us  [on_device(): jnp.sum(parts, 0, keepdims=True)]
    reduce_max x3 -> x0, other arithmetic: 5.12 us -> none  [logsumexp(): highest = jnp.max(parts, axis=axis, keepdims=True)]
    all_to_all x3 -> x4, starting transfers between devices: 31.1 us -> 34.3 us  [exchange(): return lax.all_to_all(copies, axis, split_axis=0, concat_axis=0, tiled=True)]
    broadcast_in_dim x11 -> x1, local copies, waits for them, and re-layouts: 2.81 us -> 0.05 us  [on_device(): jnp.broadcast_to(jnp.sum(parts, 0, keepdims=True), (n_z, 1, 12 * LANES))]
  transfers between devices with their start and end apart: 3 -> 4, of which waited for: 3 -> 4; matrix products, arithmetic and copies ran while one was open for 3% -> 2% of each run, Pallas kernels for 0% -> 1%
where the time goes in v2:
time: 126 us; the launch traced here: 125 us
  waiting for transfers between devices  36.2 us (29%)
  starting transfers between devices  34.3 us (27%)
  blocking collectives  28.4 us (23%)
  Pallas kernels  18 us (14%)
  local copies, waits for them, and re-layouts  6.17 us (5%)
    all_to_all x4, waiting for transfers between devices, exchange(): return lax.all_to_all(copies, axis, split_axis=0, concat_axis=0, tiled=True)  36.2 us
    all_to_all x4, starting transfers between devices, exchange(): return lax.all_to_all(copies, axis, split_axis=0, concat_axis=0, tiled=True)  34.3 us
    all_to_all x2, blocking collectives, exchange(): return lax.all_to_all(copies, axis, split_axis=0, concat_axis=0, tiled=True)  28.4 us
    pallas_call x7, Pallas kernels, call(): pl.pallas_call(body, out_shape=tuple((jax.ShapeDtypeStruct(s, d) for s, d...  18 us
    unnamed x14, local copies, waits for them, and re-layouts  4.12 us
  transfers between devices with their start and end apart: 4, of which 4 were waited for; matrix products, arithmetic and copies ran while one was open for 2% of the time, Pallas kernels for 1%

profile of v2, /device:TPU:1, one launch (start us, length us, event | category | flops | bytes accessed | tf_op | source)
XLA Modules:
  0.0 124.9 jit_solution(15949574775259952056)
XLA Ops:
  0.6 0.1 pad_add_fusion.where
  0.7 0.0 copy-start
  0.7 0.7 copy-done
  1.4 0.0 copy-start.3
  1.4 0.7 copy-done.3
  2.1 0.0 copy-start.4
  2.1 0.7 copy-done.4
  2.8 1.4 %pack_columns.1 = f32[1088,128]{1,0:T(8,128)} custom-call(s32[2]{0:T(128)S(1)} %pad_add_fusion.where, f32[4,1024]{1,0:T(4,128)S(1)} %copy-done.3, f32[8,128]{1,0:T(8,128)S(1)} %bitcast.27, f32[8,128]{1,0:T(8,128)S(1)} %bitcast.25), custom_call_target="tpu_custom_call" | custom-call | tf_op jit(solution)/shard_map/pack_columns/pallas_call | solution.py:27
  4.2 10.4 %all-to-all-start.1 = ((f32[32,1,4352]{2,1,0:T(1,128)}), f32[32,1,4352]{2,1,0:T(1,128)S(1)}, u32[]{:S(2)}, u32[]{:S(2)}) async-start(f32[32,1,4352]{2,1,0:T(1,128)} %bitcast.8), calls=%async_computation.1 | async-start | bytes 1114112 | tf_op jit(solution)/shard_map/all_to_all | solution.py:39
  14.6 0.0 copy-start.2
  14.6 0.7 copy-done.2
  15.3 0.0 copy-start.5
  15.3 0.7 copy-done.5
  16.0 0.0 copy-start.6
  16.0 0.7 copy-done.6
  16.6 0.7 pack_rows.1
  17.4 8.7 %all-to-all-done.1 = f32[32,1,4352]{2,1,0:T(1,128)S(1)} async-done(((f32[32,1,4352]{2,1,0:T(1,128)}), f32[32,1,4352]{2,1,0:T(1,128)S(1)}, u32[]{:S(2)}, u32[]{:S(2)}) %all-to-all-start.1) | async-done | bytes 557088 | tf_op jit(solution)/shard_map/all_to_all | solution.py:39
  26.1 13.0 %all-to-all-start = ((f32[16,1,1152]{2,1,0:T(1,128)}), f32[16,1,1152]{2,1,0:T(1,128)S(1)}, u32[]{:S(2)}, u32[]{:S(2)}) async-start(f32[16,1,1152]{2,1,0:T(1,128)} %bitcast.4), calls=%async_computation | async-start | bytes 147456 | tf_op jit(solution)/shard_map/all_to_all | solution.py:39
  39.1 0.7 slice.24
  39.8 0.7 slice.25
  40.5 0.1 slice_maximum_fusion.1
  40.6 0.1 select_maximum_fusion.core
  40.7 0.4 column_stack.1.columns
  41.1 9.7 %all-to-all-done = f32[16,1,1152]{2,1,0:T(1,128)S(1)} async-done(((f32[16,1,1152]{2,1,0:T(1,128)}), f32[16,1,1152]{2,1,0:T(1,128)S(1)}, u32[]{:S(2)}, u32[]{:S(2)}) %all-to-all-start) | async-done | bytes 73760 | tf_op jit(solution)/shard_map/all_to_all | solution.py:39
  50.8 5.7 %core.1 = (f32[384,128]{1,0:T(8,128)S(1)}, f32[40,512]{1,0:T(8,128)S(1)}, f32[1,512]{1,0:T(1,128)S(1)}) custom-call(f32[144,128]{1,0:T(8,128)S(1)} %bitcast.22, bf16[256,4096]{1,0:T(8,128)(2,1)S(1)} %column_stack.1.columns, f32[40,40]{1,0:T(8,128)S(1)} %select_maximum_fusion.core), custom_call_target="tpu_custom_call" | custom-call | tf_op jit(solution)/shard_map/core/pallas_call | solution.py:27
  56.5 14.0 %all_to_all.30 = f32[32,1,1536]{2,1,0:T(1,128)S(1)} all-to-all(f32[32,1,1536]{2,1,0:T(1,128)S(1)} %bitcast.23), channel_id=1, replica_groups=mesh['x'=4,'core'=2,'y'=4,'z'=16] {'x','core','y'}, dimensions={0} | all-to-all | bytes 393216 | tf_op jit(solution)/shard_map/all_to_all | solution.py:39
  70.5 0.1 reduce_sum.9
  70.6 0.1 broadcast_in_dim.2
  70.7 14.4 %all_to_all.31 = f32[16,1,1536]{2,1,0:T(1,128)S(1)} all-to-all(f32[16,1,1536]{2,1,0:T(1,128)S(1)} %broadcast_in_dim.2), channel_id=1, replica_groups=mesh['x'=4,'core'=2,'y'=4,'z'=16] {'z'}, dimensions={0} | all-to-all | bytes 196608 | tf_op jit(solution)/shard_map/all_to_all | solution.py:39
  85.1 0.0 copy-start.1
  85.1 5.4 %rows.1 = (f32[64,128]{1,0:T(8,128)}, f32[40,40]{1,0:T(8,128)S(1)}) custom-call(f32[192,128]{1,0:T(8,128)S(1)} %bitcast.21, f32[40,512]{1,0:T(8,128)S(1)} %get-tuple-element.11.features, bf16[256,4096]{1,0:T(8,128)(2,1)S(1)} %column_stack.1.columns), custom_call_target="tpu_custom_call" | custom-call | tf_op jit(solution)/shard_map/rows/pallas_call | solution.py:27
  90.5 4.7 %all-to-all-start.4 = ((f32[16,1,512]{2,1,0:T(1,128)}), f32[16,1,512]{2,1,0:T(1,128)S(1)}, u32[]{:S(2)}, u32[]{:S(2)}) async-start(f32[16,1,512]{2,1,0:T(1,128)} %bitcast.12), calls=%async_computation.4 | async-start | bytes 65536 | tf_op jit(solution)/shard_map/all_to_all | solution.py:39
  95.2 0.1 slice_maximum_fusion
  95.3 11.4 %all-to-all-done.4 = f32[16,1,512]{2,1,0:T(1,128)S(1)} async-done(((f32[16,1,512]{2,1,0:T(1,128)}), f32[16,1,512]{2,1,0:T(1,128)S(1)}, u32[]{:S(2)}, u32[]{:S(2)}) %all-to-all-start.4) | async-done | bytes 32800 | tf_op jit(solution)/shard_map/all_to_all | solution.py:39
  106.7 3.7 %columns.1 = (f32[1,512]{1,0:T(1,128)S(1)}, f32[256,128]{1,0:T(8,128)}) custom-call(s32[2]{0:T(128)S(1)} %pad_add_fusion.where, f32[64,128]{1,0:T(8,128)S(1)} %bitcast.24, f32[40,512]{1,0:T(8,128)S(1)} %get-tuple-element.11.features, f32[1,512]{1,0:T(1,128)S(1)} %get-tuple-element.13.log_source, f32[40,40]{1,0:T(8,128)S(1)} %get-tuple-element.14.core, ...), custom_call_target="tpu_custom_call" | custom-call | tf_op jit(solution)/shard_map/columns/pallas_call | solution.py:27
  110.4 6.1 %all-to-all-start.5 = ((f32[32,1,1024]{2,1,0:T(1,128)}), f32[32,1,1024]{2,1,0:T(1,128)S(1)}, u32[]{:S(2)}, u32[]{:S(2)}) async-start(f32[32,1,1024]{2,1,0:T(1,128)} %bitcast.15), calls=%async_computation.5 | async-start | bytes 262144 | tf_op jit(solution)/shard_map/all_to_all | solution.py:39
  116.6 0.7 fusion
  117.3 0.6 dynamic-slice_bitcast_fusion
  117.9 6.4 %all-to-all-done.5 = f32[32,1,1024]{2,1,0:T(1,128)S(1)} async-done(((f32[32,1,1024]{2,1,0:T(1,128)}), f32[32,1,1024]{2,1,0:T(1,128)S(1)}, u32[]{:S(2)}, u32[]{:S(2)}) %all-to-all-start.5) | async-done | bytes 131104 | tf_op jit(solution)/shard_map/all_to_all | solution.py:39
  124.2 0.0 copy-done.1
  124.2 0.7 last.1
  (2 shorter events, 0.0 us)
Async XLA Ops:
  0.7 0.7 copy-start
  1.4 0.7 copy-start.3
  2.1 0.7 copy-start.4
  4.2 21.9 %all-to-all-start.1 = ((f32[32,1,4352]{2,1,0:T(1,128)}), f32[32,1,4352]{2,1,0:T(1,128)S(1)}, u32[]{:S(2)}, u32[]{:S(2)}) async-start(f32[32,1,4352]{2,1,0:T(1,128)} %bitcast.8), calls=%async_computation.1 | async-start | bytes 1114112 | tf_op jit(solution)/shard_map/all_to_all | solution.py:39
  14.6 0.7 copy-start.2
  15.3 0.7 copy-start.5
  16.0 0.7 copy-start.6
  26.1 24.7 %all-to-all-start = ((f32[16,1,1152]{2,1,0:T(1,128)}), f32[16,1,1152]{2,1,0:T(1,128)S(1)}, u32[]{:S(2)}, u32[]{:S(2)}) async-start(f32[16,1,1152]{2,1,0:T(1,128)} %bitcast.4), calls=%async_computation | async-start | bytes 147456 | tf_op jit(solution)/shard_map/all_to_all | solution.py:39
  85.1 39.1 %copy-start.1 = (f32[1024]{0:T(1024)S(1)}, f32[1024]{0:T(1024)}, u32[]{:S(2)}) copy-start(f32[1024]{0:T(1024)} %param.12) | copy-start | bytes 12292
  90.5 16.2 %all-to-all-start.4 = ((f32[16,1,512]{2,1,0:T(1,128)}), f32[16,1,512]{2,1,0:T(1,128)S(1)}, u32[]{:S(2)}, u32[]{:S(2)}) async-start(f32[16,1,512]{2,1,0:T(1,128)} %bitcast.12), calls=%async_computation.4 | async-start | bytes 65536 | tf_op jit(solution)/shard_map/all_to_all | solution.py:39
  110.4 13.8 %all-to-all-start.5 = ((f32[32,1,1024]{2,1,0:T(1,128)}), f32[32,1,1024]{2,1,0:T(1,128)S(1)}, u32[]{:S(2)}, u32[]{:S(2)}) async-start(f32[32,1,1024]{2,1,0:T(1,128)} %bitcast.15), calls=%async_computation.5 | async-start | bytes 262144 | tf_op jit(solution)/shard_map/all_to_all | solution.py:39

commit v3 on v2

--- a/solution.py
+++ b/solution.py
@@ -22,7 +22,7 @@
 SMEM = pl.BlockSpec(memory_space=pltpu.SMEM)
 
 
-def call(body, outs, n_smem, args, scratch=(), name=None):
+def call(body, outs, n_smem, args, scratch=()):
     specs = [SMEM] * n_smem + [VMEM] * (len(args) - n_smem)
     return pl.pallas_call(
         body,
@@ -31,7 +31,6 @@
         out_specs=tuple(VMEM for _ in outs),
         scratch_shapes=list(scratch),
         compiler_params=pltpu.CompilerParams(vmem_limit_bytes=48 * 2**20),
-        name=name,
     )(*args)
 
 
@@ -62,7 +61,14 @@
 FORMER_ORDER = (0, 1, 0, 2, 0, 1)
 
 
-def pack_rows(points, potential, weight, out):
+def pack(where, *refs):
+    given, (out, column_out), held, (sem, *into) = refs[:6], refs[6:8], refs[8], refs[9:]
+    copies = [pltpu.make_async_copy(a, b, sem.at[k]) for k, (a, b) in enumerate(zip(given, into))]
+    for copy in copies:
+        copy.start()
+    for copy in copies:
+        copy.wait()
+    points, potential, weight, column_points, column_potential, column_weight = into
     value = points[...]
     block = jnp.concatenate([value[8 * k : 8 * k + 8] for k in range(4)], axis=1)
     last = jnp.concatenate(
@@ -71,29 +77,29 @@
     both = jnp.concatenate([block, last], 0)
     for k in range(out.shape[0] // 9):
         out[9 * k : 9 * k + 9, :] = both
-
-
-def pack_columns(where, points, potential, weight, out, held):
     for r in range(4):
         for k in range(8):
-            held[8 * r + k : 8 * r + k + 1, :] = points[r : r + 1, LANES * k : LANES * k + LANES]
+            held[8 * r + k : 8 * r + k + 1, :] = column_points[
+                r : r + 1, LANES * k : LANES * k + LANES
+            ]
     src = where[0]
-    held[32:33, :] = potential[pl.ds(src, 1), :]
-    held[33:34, :] = weight[pl.ds(src, 1), :]
+    held[32:33, :] = column_potential[pl.ds(src, 1), :]
+    held[33:34, :] = column_weight[pl.ds(src, 1), :]
     both = held[0:34, :]
-    for k in range(out.shape[0] // 34):
-        out[34 * k : 34 * k + 34, :] = both
+    for k in range(column_out.shape[0] // 34):
+        column_out[34 * k : 34 * k + 34, :] = both
 
 
 def column_stack(log_targets):
-    def body(message, out):
-        for y in range(4):
+    def body(*refs):
+        *messages, out = refs
+        for y, message in enumerate(messages):
             for k in range(8):
                 points = jnp.concatenate(
-                    [message[pl.ds(34 * (4 * s + y) + k, 4, stride=8), :] for s in range(8)], 0
+                    [message[pl.ds(34 * s + k, 4, stride=8), :] for s in range(8)], 0
                 )
                 squares = jnp.sum(points * points, 0, keepdims=True)
-                at = 34 * (4 * k + y) + 32
+                at = 34 * k + 32
                 offset = jnp.log(message[at + 1 : at + 2, :]) - log_targets
                 offset = (offset + message[at : at + 1, :] * (1.0 / EPSILON)) * LOG2E
                 tail = jnp.concatenate(
@@ -242,7 +248,6 @@
             core[...], features[...], logs + source_new * (1.0 / EPSILON), 0.0
         )
         width = columns.shape[1] // blocks
-        per_piece = 1024 // width
 
         for b in range(blocks):
             tile = dot(former[...], columns[:, width * b : width * b + width], ((0,), (0,)))
@@ -253,7 +258,8 @@
                 at = (b * width + LANES * k) // LANES
                 held[at : at + 1, :] = part[:, LANES * k : LANES * k + LANES]
         for y in range(4):
-            piece = held[8 * y : 8 * y + 8, :]
+            turn = lax.rem(where[1] - y + 4, 4)
+            piece = held[pl.ds(pl.multiple_of(8 * turn, 8), 8), :]
             for s in range(8):
                 at = 8 * (4 * s + y)
                 out[at : at + 8, :] = piece
@@ -288,8 +294,8 @@
     target_weight,
     core_previous,
 ):
-    emb, own = source_points.shape
-    dims, span = target_points.shape
+    _, own = source_points.shape
+    _, span = target_points.shape
     n_z, n_y, n_src = lax.axis_size("z"), lax.axis_size("y"), lax.axis_size(("x", "core"))
     n_plane = n_src * n_y
     rows, columns = own * n_z, span * n_y
@@ -298,26 +304,37 @@
     where = jnp.stack([lax.axis_index(("x", "core")), lax.axis_index("y")]).astype(jnp.int32)
     z = lax.axis_index("z")
 
-    (mine,) = call(
-        pack_rows,
-        [((9 * n_z, LANES), F32)],
-        0,
-        (source_points, source_potential.reshape(1, own), source_weight.reshape(1, own)),
-        name="pack_rows",
-    )
-    (theirs,) = call(
-        pack_columns,
-        [((34 * n_plane, LANES), F32)],
-        1,
-        (where, target_points, target_potential.reshape(8, LANES), target_weight.reshape(8, LANES)),
-        scratch=[pltpu.VMEM((40, LANES), F32)],
-        name="pack_columns",
-    )
-    theirs = exchange(theirs.reshape(n_plane, 1, 34 * LANES), PLANE).reshape(-1, LANES)
+    given = (
+        source_points,
+        source_potential.reshape(1, own),
+        source_weight.reshape(1, own),
+        target_points,
+        target_potential.reshape(8, LANES),
+        target_weight.reshape(8, LANES),
+    )
+    mine, theirs = pl.pallas_call(
+        pack,
+        out_shape=(
+            jax.ShapeDtypeStruct((9 * n_z, LANES), F32),
+            jax.ShapeDtypeStruct((34 * n_src, LANES), F32),
+        ),
+        in_specs=[SMEM] + [pl.BlockSpec(memory_space=pl.ANY)] * len(given),
+        out_specs=(VMEM, VMEM),
+        scratch_shapes=[
+            pltpu.VMEM((PAD, LANES), F32),
+            pltpu.SemaphoreType.DMA((len(given),)),
+            *(pltpu.VMEM(a.shape, F32) for a in given),
+        ],
+        name="pack",
+    )(where, *given)
+    theirs = exchange(theirs.reshape(n_src, 1, 34 * LANES), ("x", "core"))
     mine = exchange(mine.reshape(n_z, 1, 9 * LANES), "z").reshape(-1, LANES)
-    (stack,) = call(
-        column_stack(log_targets), [((DEPTH, columns), BF16)], 0, (theirs,), name="column_stack"
-    )
+    turns = [
+        lax.ppermute(theirs, "y", [(i, (i + k) % n_y) for i in range(n_y)])
+        for k in range(1, n_y)
+    ]
+    messages = [m.reshape(-1, LANES) for m in (theirs, *turns)]
+    (stack,) = call(column_stack(log_targets), [((DEPTH, columns), BF16)], 0, messages)
     previous = jnp.pad(turned(core_previous), ((0, PAD - 34), (0, PAD - 34)))
     former = pltpu.VMEM((DEPTH, rows), BF16)
     packed, features, log_source = call(
@@ -326,7 +343,6 @@
         0,
         (mine, stack, previous),
         scratch=[former, pltpu.VMEM((rows, DEPTH), F32)],
-        name="core",
     )
     parts = exchange(packed.reshape(n_plane, 1, 12 * LANES), PLANE)
     parts = jnp.broadcast_to(jnp.sum(parts, 0, keepdims=True), (n_z, 1, 12 * LANES))
@@ -338,7 +354,6 @@
         0,
         (parts, features, stack),
         scratch=[former, pltpu.VMEM((rows, columns), F32)],
-        name="rows",
     )
     row_parts = exchange(row_parts.reshape(n_z, 1, rows), "z").reshape(-1, LANES)
     source_new, column_parts = call(
@@ -347,7 +362,6 @@
         1,
         (where, row_parts, features, log_source, core_new, stack),
         scratch=[former, pltpu.VMEM((columns // LANES, LANES), F32)],
-        name="columns",
     )
     column_parts = exchange(column_parts.reshape(n_plane, 1, span), PLANE).reshape(-1, LANES)
     (target_new,) = call(
@@ -355,7 +369,6 @@
         [((8, LANES), F32)],
         0,
         (column_parts, target_weight.reshape(8, LANES)),
-        name="last",
     )
     own_rows = lax.dynamic_slice_in_dim(source_new.reshape(rows), z * own, own)
     return (own_rows, target_new.reshape(span), turned_back(core_new))

time: 126 us -> 130 us (1.032)
  blocking collectives: 28.4 us -> 54.3 us
  waiting for transfers between devices: 36.2 us -> 20.5 us
  local copies, waits for them, and re-layouts: 6.17 us -> 2.07 us
  starting transfers between devices: 34.3 us -> 32.1 us
    all_to_all x2 -> x3, blocking collectives: 28.4 us -> 54.3 us  [exchange(): return lax.all_to_all(copies, axis, split_axis=0, concat_axis=0, tiled=True)]
    all_to_all x4 -> x3, waiting for transfers between devices: 36.2 us -> 17.8 us  [exchange(): return lax.all_to_all(copies, axis, split_axis=0, concat_axis=0, tiled=True)]
    all_to_all x4 -> x3, starting transfers between devices: 34.3 us -> 21.4 us  [exchange(): return lax.all_to_all(copies, axis, split_axis=0, concat_axis=0, tiled=True)]
    ppermute x0 -> x3, starting transfers between devices: none -> 10.7 us  [on_device(): lax.ppermute(theirs, 'y', [(i, (i + k) % n_y) for i in range(n_y)])]
    unnamed x14 -> x4, local copies, waits for them, and re-layouts: 4.12 us -> 0.01 us
    ppermute x0 -> x3, waiting for transfers between devices: none -> 2.65 us  [on_device(): lax.ppermute(theirs, 'y', [(i, (i + k) % n_y) for i in range(n_y)])]
    pallas_call x0 -> x1, Pallas kernels: none -> 2.22 us  [on_device(): pl.pallas_call(pack, out_shape=(jax.ShapeDtypeStruct((9 * n_z, LANES), F3...]
    pallas_call x7 -> x5, Pallas kernels: 18 us -> 15.9 us  [call(): pl.pallas_call(body, out_shape=tuple((jax.ShapeDtypeStruct(s, d) for s, d...]
  transfers between devices with their start and end apart: 4 -> 6, of which waited for: 4 -> 4; matrix products, arithmetic and copies ran while one was open for 2% -> 2% of each run, Pallas kernels for 1% -> 0%
where the time goes in v3:
time: 130 us; the launch traced here: 129 us
  blocking collectives  54.3 us (42%)
  starting transfers between devices  32.1 us (25%)
  waiting for transfers between devices  20.5 us (16%)
  Pallas kernels  18.2 us (14%)
  local copies, waits for them, and re-layouts  2.07 us (2%)
  other arithmetic  1.63 us (1%)
    all_to_all x3, blocking collectives, exchange(): return lax.all_to_all(copies, axis, split_axis=0, concat_axis=0, tiled=True)  54.3 us
    all_to_all x3, starting transfers between devices, exchange(): return lax.all_to_all(copies, axis, split_axis=0, concat_axis=0, tiled=True)  21.4 us
    all_to_all x3, waiting for transfers between devices, exchange(): return lax.all_to_all(copies, axis, split_axis=0, concat_axis=0, tiled=True)  17.8 us
    pallas_call x5, Pallas kernels, call(): pl.pallas_call(body, out_shape=tuple((jax.ShapeDtypeStruct(s, d) for s, d...  15.9 us
    ppermute x3, starting transfers between devices, on_device(): lax.ppermute(theirs, 'y', [(i, (i + k) % n_y) for i in range(n_y)])  10.7 us
    ppermute x3, waiting for transfers between devices, on_device(): lax.ppermute(theirs, 'y', [(i, (i + k) % n_y) for i in range(n_y)])  2.65 us
  transfers between devices with their start and end apart: 6, of which 4 were waited for; matrix products, arithmetic and copies ran while one was open for 2% of the time, Pallas kernels for 0%

profile of v3, /device:TPU:1, one launch (start us, length us, event | category | flops | bytes accessed | tf_op | source)
XLA Modules:
  0.0 129.5 jit_solution(6707883136945328015)
XLA Ops:
  0.6 0.6 pad_add_fusion.where
  1.2 2.2 %pack.1 = (f32[144,128]{1,0:T(8,128)}, f32[272,128]{1,0:T(8,128)}) custom-call(s32[2]{0:T(128)} %pad_add_fusion.where, f32[32,32]{1,0:T(8,128)} %refs_0_.1, f32[1,32]{1,0:T(1,128)} %bitcast.37, f32[1,32]{1,0:T(1,128)} %bitcast.38, f32[4,1024]{1,0:T(4,128)} %refs_3_.1, f32[8,128]{1,0:T(8,128)} %bitcast.36, f32[8,128]{1,0:T(8,128)} %bitcast.31), custom_call_target="tpu_custom_call" | custom-call | tf_op jit(solution)/shard_map/pack/pallas_call | solution.py:315
  3.4 15.4 %all_to_all.30 = f32[8,1,4352]{2,1,0:T(1,128)S(1)} all-to-all(f32[8,1,4352]{2,1,0:T(1,128)} %bitcast.33), channel_id=1, replica_groups=mesh['x'=4,'core'=2,'y'=4,'z'=16] {'x','core'}, dimensions={0} | all-to-all | bytes 278528 | tf_op jit(solution)/shard_map/all_to_all | solution.py:38
  18.9 10.6 %all-to-all-start = ((f32[16,1,1152]{2,1,0:T(1,128)}), f32[16,1,1152]{2,1,0:T(1,128)S(1)}, u32[]{:S(2)}, u32[]{:S(2)}) async-start(f32[16,1,1152]{2,1,0:T(1,128)} %bitcast.34), calls=%async_computation | async-start | bytes 147456 | tf_op jit(solution)/shard_map/all_to_all | solution.py:38
  29.5 0.7 slice.25
  30.2 0.7 slice.24
  30.9 3.2 %collective-permute-start = (f32[8,1,4352]{2,1,0:T(1,128)S(1)}, f32[8,1,4352]{2,1,0:T(1,128)S(1)}, u32[]{:S(2)}, u32[]{:S(2)}) collective-permute-start(f32[8,1,4352]{2,1,0:T(1,128)S(1)} %all_to_all.30), channel_id=1, source_target_pairs={{0,16},{16,32},{32,48},{48,0},{1,17},{17,33},{33,49},{49,1},{2,18}... | collective-permute-start | bytes 417800 | tf_op jit(solution)/shard_map/ppermute | solution.py:333
  34.1 4.5 %collective-permute-start.1 = (f32[8,1,4352]{2,1,0:T(1,128)S(1)}, f32[8,1,4352]{2,1,0:T(1,128)S(1)}, u32[]{:S(2)}, u32[]{:S(2)}) collective-permute-start(f32[8,1,4352]{2,1,0:T(1,128)S(1)} %all_to_all.30), channel_id=1, source_target_pairs={{0,32},{16,48},{32,0},{48,16},{1,33},{17,49},{33,1},{49,17},{2,34}... | collective-permute-start | bytes 417800 | tf_op jit(solution)/shard_map/ppermute | solution.py:333
  38.6 3.0 %collective-permute-start.2 = (f32[8,1,4352]{2,1,0:T(1,128)S(1)}, f32[8,1,4352]{2,1,0:T(1,128)S(1)}, u32[]{:S(2)}, u32[]{:S(2)}) collective-permute-start(f32[8,1,4352]{2,1,0:T(1,128)S(1)} %all_to_all.30), channel_id=1, source_target_pairs={{0,48},{16,0},{32,16},{48,32},{1,49},{17,1},{33,17},{49,33},{2,50}... | collective-permute-start | bytes 417800 | tf_op jit(solution)/shard_map/ppermute | solution.py:333
  41.6 0.1 slice_maximum_fusion.1
  41.7 0.1 select_maximum_fusion.core
  41.8 0.0 collective-permute-done
  41.8 1.2 collective-permute-done.1
  43.0 1.5 %collective-permute-done.2 = f32[8,1,4352]{2,1,0:T(1,128)S(1)} collective-permute-done((f32[8,1,4352]{2,1,0:T(1,128)S(1)}, f32[8,1,4352]{2,1,0:T(1,128)S(1)}, u32[]{:S(2)}, u32[]{:S(2)}) %collective-permute-start.2) | collective-permute-done | bytes 139296 | tf_op jit(solution)/shard_map/ppermute | solution.py:333
  44.4 0.4 shard_map.94.columns
  44.9 0.0 all-to-all-done
  44.9 5.7 %shard_map.95 = (f32[384,128]{1,0:T(8,128)S(1)}, f32[40,512]{1,0:T(8,128)S(1)}, f32[1,512]{1,0:T(1,128)S(1)}) custom-call(f32[144,128]{1,0:T(8,128)S(1)} %bitcast.25, bf16[256,4096]{1,0:T(8,128)(2,1)S(1)} %shard_map.94.columns, f32[40,40]{1,0:T(8,128)S(1)} %select_maximum_fusion.core), custom_call_target="tpu_custom_call" | custom-call | tf_op jit(solution)/shard_map/pallas_call | solution.py:27
  50.6 0.0 copy-start.1
  50.6 15.4 %all_to_all.31 = f32[32,1,1536]{2,1,0:T(1,128)S(1)} all-to-all(f32[32,1,1536]{2,1,0:T(1,128)S(1)} %bitcast.26), channel_id=1, replica_groups=mesh['x'=4,'core'=2,'y'=4,'z'=16] {'x','core','y'}, dimensions={0} | all-to-all | bytes 393216 | tf_op jit(solution)/shard_map/all_to_all | solution.py:38
  66.0 0.1 reduce_sum.9
  66.2 0.1 broadcast_in_dim.2
  66.2 23.4 %all_to_all.32 = f32[16,1,1536]{2,1,0:T(1,128)S(1)} all-to-all(f32[16,1,1536]{2,1,0:T(1,128)S(1)} %broadcast_in_dim.2), channel_id=1, replica_groups=mesh['x'=4,'core'=2,'y'=4,'z'=16] {'z'}, dimensions={0} | all-to-all | bytes 196608 | tf_op jit(solution)/shard_map/all_to_all | solution.py:38
  89.6 0.0 copy-start
  89.6 5.4 %shard_map.96 = (f32[64,128]{1,0:T(8,128)}, f32[40,40]{1,0:T(8,128)S(1)}) custom-call(f32[192,128]{1,0:T(8,128)S(1)} %bitcast.24, f32[40,512]{1,0:T(8,128)S(1)} %get-tuple-element.15.features, bf16[256,4096]{1,0:T(8,128)(2,1)S(1)} %shard_map.94.columns), custom_call_target="tpu_custom_call" | custom-call | tf_op jit(solution)/shard_map/pallas_call | solution.py:27
  95.0 4.8 %all-to-all-start.4 = ((f32[16,1,512]{2,1,0:T(1,128)}), f32[16,1,512]{2,1,0:T(1,128)S(1)}, u32[]{:S(2)}, u32[]{:S(2)}) async-start(f32[16,1,512]{2,1,0:T(1,128)} %bitcast.15), calls=%async_computation.4 | async-start | bytes 65536 | tf_op jit(solution)/shard_map/all_to_all | solution.py:38
  99.9 0.1 slice_maximum_fusion
  99.9 11.4 %all-to-all-done.4 = f32[16,1,512]{2,1,0:T(1,128)S(1)} async-done(((f32[16,1,512]{2,1,0:T(1,128)}), f32[16,1,512]{2,1,0:T(1,128)S(1)}, u32[]{:S(2)}, u32[]{:S(2)}) %all-to-all-start.4) | async-done | bytes 32800 | tf_op jit(solution)/shard_map/all_to_all | solution.py:38
  111.4 0.0 copy-done.1
  111.4 3.8 %shard_map.97 = (f32[1,512]{1,0:T(1,128)S(1)}, f32[256,128]{1,0:T(8,128)}) custom-call(s32[2]{0:T(128)S(1)} %copy-done.1, f32[64,128]{1,0:T(8,128)S(1)} %bitcast.30, f32[40,512]{1,0:T(8,128)S(1)} %get-tuple-element.15.features, f32[1,512]{1,0:T(1,128)S(1)} %get-tuple-element.17.log_source, f32[40,40]{1,0:T(8,128)S(1)} %get-tuple-element.18.core, ...), custom_call_target="tpu_custom_call" | custom-call | tf_op jit(solution)/shard_map/pallas_call | solution.py:27
  115.2 6.0 %all-to-all-start.5 = ((f32[32,1,1024]{2,1,0:T(1,128)}), f32[32,1,1024]{2,1,0:T(1,128)S(1)}, u32[]{:S(2)}, u32[]{:S(2)}) async-start(f32[32,1,1024]{2,1,0:T(1,128)} %bitcast.18), calls=%async_computation.5 | async-start | bytes 262144 | tf_op jit(solution)/shard_map/all_to_all | solution.py:38
  121.2 0.7 fusion
  121.9 0.6 dynamic-slice_bitcast_fusion
  122.4 6.4 %all-to-all-done.5 = f32[32,1,1024]{2,1,0:T(1,128)S(1)} async-done(((f32[32,1,1024]{2,1,0:T(1,128)}), f32[32,1,1024]{2,1,0:T(1,128)S(1)}, u32[]{:S(2)}, u32[]{:S(2)}) %all-to-all-start.5) | async-done | bytes 131104 | tf_op jit(solution)/shard_map/all_to_all | solution.py:38
  128.8 0.0 copy-done
  128.8 0.7 shard_map.98
  (2 shorter events, 0.0 us)
Async XLA Ops:
  18.9 26.0 %all-to-all-start = ((f32[16,1,1152]{2,1,0:T(1,128)}), f32[16,1,1152]{2,1,0:T(1,128)S(1)}, u32[]{:S(2)}, u32[]{:S(2)}) async-start(f32[16,1,1152]{2,1,0:T(1,128)} %bitcast.34), calls=%async_computation | async-start | bytes 147456 | tf_op jit(solution)/shard_map/all_to_all | solution.py:38
  30.9 10.9 %collective-permute-start = (f32[8,1,4352]{2,1,0:T(1,128)S(1)}, f32[8,1,4352]{2,1,0:T(1,128)S(1)}, u32[]{:S(2)}, u32[]{:S(2)}) collective-permute-start(f32[8,1,4352]{2,1,0:T(1,128)S(1)} %all_to_all.30), channel_id=1, source_target_pairs={{0,16},{16,32},{32,48},{48,0},{1,17},{17,33},{33,49},{49,1},{2,18}... | collective-permute-start | bytes 417800 | tf_op jit(solution)/shard_map/ppermute | solution.py:333
  34.1 8.9 %collective-permute-start.1 = (f32[8,1,4352]{2,1,0:T(1,128)S(1)}, f32[8,1,4352]{2,1,0:T(1,128)S(1)}, u32[]{:S(2)}, u32[]{:S(2)}) collective-permute-start(f32[8,1,4352]{2,1,0:T(1,128)S(1)} %all_to_all.30), channel_id=1, source_target_pairs={{0,32},{16,48},{32,0},{48,16},{1,33},{17,49},{33,1},{49,17},{2,34}... | collective-permute-start | bytes 417800 | tf_op jit(solution)/shard_map/ppermute | solution.py:333
  38.6 5.8 %collective-permute-start.2 = (f32[8,1,4352]{2,1,0:T(1,128)S(1)}, f32[8,1,4352]{2,1,0:T(1,128)S(1)}, u32[]{:S(2)}, u32[]{:S(2)}) collective-permute-start(f32[8,1,4352]{2,1,0:T(1,128)S(1)} %all_to_all.30), channel_id=1, source_target_pairs={{0,48},{16,0},{32,16},{48,32},{1,49},{17,1},{33,17},{49,33},{2,50}... | collective-permute-start | bytes 417800 | tf_op jit(solution)/shard_map/ppermute | solution.py:333
  50.6 60.8 %copy-start.1 = (s32[2]{0:T(128)S(1)}, s32[2]{0:T(128)}, u32[]{:S(2)}) copy-start(s32[2]{0:T(128)} %pad_add_fusion.where) | copy-start | bytes 28
  89.6 39.2 %copy-start = (f32[1024]{0:T(1024)S(1)}, f32[1024]{0:T(1024)}, u32[]{:S(2)}) copy-start(f32[1024]{0:T(1024)} %param.12) | copy-start | bytes 12292
  95.0 16.4 %all-to-all-start.4 = ((f32[16,1,512]{2,1,0:T(1,128)}), f32[16,1,512]{2,1,0:T(1,128)S(1)}, u32[]{:S(2)}, u32[]{:S(2)}) async-start(f32[16,1,512]{2,1,0:T(1,128)} %bitcast.15), calls=%async_computation.4 | async-start | bytes 65536 | tf_op jit(solution)/shard_map/all_to_all | solution.py:38
  115.2 13.6 %all-to-all-start.5 = ((f32[32,1,1024]{2,1,0:T(1,128)}), f32[32,1,1024]{2,1,0:T(1,128)S(1)}, u32[]{:S(2)}, u32[]{:S(2)}) async-start(f32[32,1,1024]{2,1,0:T(1,128)} %bitcast.18), calls=%async_computation.5 | async-start | bytes 262144 | tf_op jit(solution)/shard_map/all_to_all | solution.py:38

commit v4 on v3

v4 whole, which is shorter than its diff:
```python
import functools
import math

import jax
import jax.numpy as jnp
from jax import lax
from jax.experimental import pallas as pl
from jax.experimental.pallas import tpu as pltpu
from jax.sharding import Mesh
from jax.sharding import PartitionSpec as P

PLANE = ("x", "core", "y")
ALL = ("x", "core", "y", "z")
EPSILON = 0.5
HIGHEST = lax.Precision.HIGHEST
LANES = 128
PAD = 40
DEPTH = 256
LOG2E = math.log2(math.e)
LN2 = math.log(2.0)
F32, BF16 = jnp.float32, jnp.bfloat16
VMEM = pl.BlockSpec(memory_space=pltpu.VMEM)


def call(body, outs, args, scratch=(), name=None):
    return pl.pallas_call(
        body,
        out_shape=tuple(jax.ShapeDtypeStruct(s, d) for s, d in outs),
        in_specs=[VMEM] * len(args),
        out_specs=tuple(VMEM for _ in outs),
        scratch_shapes=list(scratch),
        compiler_params=pltpu.CompilerParams(vmem_limit_bytes=48 * 2**20),
        name=name,
    )(*args)


def exchange(copies, axis):
    return lax.all_to_all(copies, axis, split_axis=0, concat_axis=0, tiled=True)


def dot(former, latter, dims, precision=None):
    return lax.dot_general(
        former, latter, (dims, ((), ())), precision=precision, preferred_element_type=F32
    )


def split(value):
    first = value.astype(BF16).astype(F32)
    rest = value - first
    second = rest.astype(BF16).astype(F32)
    return first, second, rest - second


def stacked(pieces, order):
    blocks = [pieces[k] for k in order]
    filler = jnp.zeros((DEPTH - PAD * len(order), pieces[0].shape[1]), F32)
    return jnp.concatenate([*blocks, filler], 0).astype(BF16)


LATTER_ORDER = (0, 0, 1, 0, 2, 1)
FORMER_ORDER = (0, 1, 0, 2, 0, 1)


def pack(*refs):
    given, (out, column_out), held, (sem, *into) = refs[:6], refs[6:8], refs[8], refs[9:]
    copies = [pltpu.make_async_copy(a, b, sem.at[k]) for k, (a, b) in enumerate(zip(given, into))]
    for copy in copies:
        copy.start()
    for copy in copies:
        copy.wait()
    points, potential, weight, column_points, column_potential, column_weight = into
    value = points[...]
    block = jnp.concatenate([value[8 * k : 8 * k + 8] for k in range(4)], axis=1)
    last = jnp.concatenate(
        [potential[...], weight[...], jnp.ones((1, LANES - 64), F32)], axis=1
    )
    both = jnp.concatenate([block, last], 0)
    for k in range(out.shape[0] // 9):
        out[9 * k : 9 * k + 9, :] = both
    for r in range(4):
        for k in range(8):
            held[8 * r + k : 8 * r + k + 1, :] = column_points[
                r : r + 1, LANES * k : LANES * k + LANES
            ]
    src = lax.axis_index(("x", "core"))
    held[32:33, :] = column_potential[pl.ds(src, 1), :]
    held[33:34, :] = column_weight[pl.ds(src, 1), :]
    both = held[0:34, :]
    for k in range(column_out.shape[0] // 34):
        column_out[34 * k : 34 * k + 34, :] = both


def column_stack(message, out, log_targets):
    def step(y, _):
        for k in range(8):
            points = jnp.concatenate(
                [message[pl.ds(34 * (4 * s + y) + k, 4, stride=8), :] for s in range(8)], 0
            )
            squares = jnp.sum(points * points, 0, keepdims=True)
            at = 34 * (4 * k + y) + 32
            offset = jnp.log(message[pl.ds(at + 1, 1), :]) - log_targets
            offset = (offset + message[pl.ds(at, 1), :] * (1.0 / EPSILON)) * LOG2E
            tail = jnp.concatenate(
                [squares, jnp.ones((1, LANES), F32), offset, jnp.zeros((5, LANES), F32)], 0
            )
            value = jnp.concatenate([points, tail], 0)
            col = pl.multiple_of(1024 * y + LANES * k, LANES)
            out[:, pl.ds(col, LANES)] = stacked(split(value), LATTER_ORDER)
        return 0

    lax.fori_loop(0, 4, step, 0)


def in_turns(former, columns, consume, tiles):
    even, odd = tiles
    width = even.shape[1]
    blocks = columns.shape[1] // width

    def tile(b):
        at = pl.multiple_of(b * width, width)
        return dot(former[...], columns[:, pl.ds(at, width)], ((0,), (0,)))

    even[...] = tile(0)

    def step(i, _):
        odd[...] = tile(2 * i + 1)
        consume(even, 2 * i)
        even[...] = tile(jnp.minimum(2 * i + 2, blocks - 1))
        consume(odd, 2 * i + 1)
        return 0

    lax.fori_loop(0, blocks // 2, step, 0)


def signs(core):
    row = lax.broadcasted_iota(jnp.int32, core.shape, 0)
    col = lax.broadcasted_iota(jnp.int32, core.shape, 1)
    core = jnp.where(row < 32, -2.0 * core, core)
    return jnp.where(col < 32, -2.0 * core, core)


def former_stack(core, features, row_term, column_factor):
    weighted = dot(signs(core), features, ((0,), (0,)), HIGHEST) * (2.0 / EPSILON * LOG2E)
    row = lax.broadcasted_iota(jnp.int32, weighted.shape, 0)
    if row_term is not None:
        weighted = jnp.where(row == 33, weighted + row_term * LOG2E, weighted)
    weighted = jnp.where(row == 34, column_factor, weighted)
    return stacked(split(weighted), FORMER_ORDER)


def turned(core):
    core = jnp.concatenate([core[2:34], core[0:2], jnp.zeros((PAD - 34, 34), F32)], 0)
    return jnp.concatenate([core[:, 2:34], core[:, 0:2], jnp.zeros((PAD, PAD - 34), F32)], 1)


def turned_back(core):
    core = jnp.concatenate([core[32:34], core[0:32]], 0)
    return jnp.concatenate([core[:, 32:34], core[:, 0:32]], 1)


def core_kernel(log_sources, log_targets):
    def body(message, arrived, core, packed, features_out, log_out, columns, former, total, *tiles):
        column_stack(arrived, columns, log_targets)
        pieces = []
        for k in range(4):
            pieces.append(
                jnp.concatenate(
                    [message[9 * z : 9 * z + 8, 32 * k : 32 * k + 32] for z in range(16)], 1
                )
            )
        points = jnp.concatenate(pieces, 0)
        last = jnp.concatenate([message[9 * z + 8 : 9 * z + 9, 0:32] for z in range(16)], 1)
        weight = jnp.concatenate([message[9 * z + 8 : 9 * z + 9, 32:64] for z in range(16)], 1)
        squares = jnp.sum(points * points, 0, keepdims=True)
        ones = jnp.ones_like(squares)
        zeros = jnp.zeros((6, squares.shape[1]), F32)
        features = jnp.concatenate([points, squares, ones, zeros], 0)
        log_source = jnp.log(weight) - log_sources
        features_out[...] = features
        log_out[...] = log_source
        former[...] = former_stack(
            turned(core[...]), features, log_source + last * (1.0 / EPSILON), 1.0
        )
        total[...] = jnp.zeros_like(total)

        def consume(tile, b):
            width = tile.shape[1]
            stack = columns[:, pl.ds(pl.multiple_of(b * width, width), width)]
            plan = jnp.exp2(tile[...])
            high = plan.astype(BF16)
            low = (plan - high.astype(F32)).astype(BF16)
            total[...] += dot(high, stack, ((1,), (1,))) + dot(low, stack, ((1,), (1,)))

        in_turns(former, columns, consume, tiles)
        carried = (
            total[:, 0:PAD] + total[:, 2 * PAD : 3 * PAD] + total[:, 4 * PAD : 5 * PAD]
        )
        right = jnp.concatenate([points, ones, squares, zeros], 0)
        core_part = dot(right, carried, ((1,), (0,)), HIGHEST)
        col = lax.broadcasted_iota(jnp.int32, core_part.shape, 1)
        ahead = jnp.concatenate([core_part[:, 1:], core_part[:, :1]], 1)
        behind = jnp.concatenate([core_part[:, -1:], core_part[:, :-1]], 1)
        core_part = jnp.where(col == 32, ahead, jnp.where(col == 33, behind, core_part))
        core_part = jnp.where(col < 34, core_part, 0.0)
        both = jnp.concatenate(
            [core_part[12 * g : 12 * g + 12] for g in range(3)] + [jnp.zeros((12, 8), F32)], 1
        )
        for k in range(packed.shape[0] // 12):
            packed[12 * k : 12 * k + 12, :] = both

    return body


def row_kernel(parts, features, columns, out, core_out, core_new, former, highest, total, *tiles):
    both = parts[0:12, :]
    for k in range(1, parts.shape[0] // 12):
        both = both + parts[12 * k : 12 * k + 12, :]
    core = jnp.concatenate([both[:, PAD * g : PAD * g + PAD] for g in range(3)], 0)
    core = jnp.concatenate([core, jnp.zeros((PAD - 36, PAD), F32)], 0)
    core_out[...] = core
    core_new[...] = turned_back(core)
    former[...] = former_stack(core, features[...], None, 1.0)
    rows = features.shape[1]
    highest[...] = jnp.full(highest.shape, jnp.finfo(F32).min, F32)
    total[...] = jnp.zeros_like(total)

    def consume(tile, _):
        for r in range(0, rows, 64):
            at = pl.ds(r, 64)
            pieces = [tile[at, LANES * k : LANES * k + LANES] for k in range(tile.shape[1] // LANES)]
            before = highest[at, :]
            now = largest([before, *pieces])
            highest[at, :] = now
            total[at, :] = total[at, :] * jnp.exp2(before - now) + sum(
                jnp.exp2(p - now) for p in pieces
            )

    in_turns(former, columns, consume, tiles)
    lanes = highest[...]
    top = jnp.max(lanes, 1, keepdims=True)
    added = jnp.sum(total[...] * jnp.exp2(lanes - top), 1, keepdims=True)
    part = top * LN2 + jnp.log(added)
    wide = jnp.broadcast_to(part, (rows, LANES))
    flat = [jnp.transpose(wide[LANES * k : LANES * k + LANES])[0:1] for k in range(4)]
    both = jnp.concatenate(flat, 0)
    for k in range(out.shape[0] // 4):
        out[4 * k : 4 * k + 4, :] = both


def largest(values):
    return functools.reduce(jnp.maximum, values)


def combined(values):
    highest = largest(values)
    total = sum(jnp.exp(v - highest) for v in values)
    return highest + jnp.log(total)


def column_kernel(
    parts, features, log_source, core, columns, own_out, out, former, held, mine, *tiles
):
    merged = combined([parts[4 * k : 4 * k + 4, :] for k in range(parts.shape[0] // 4)])
    merged = jnp.concatenate([merged[k : k + 1] for k in range(4)], 1)
    logs = log_source[...]
    source_new = EPSILON * (logs - merged)
    own = own_out.shape[1]
    for k in range(mine.shape[0]):
        mine[k : k + 1, :] = source_new[:, own * k : own * k + own]
    own_out[...] = mine[pl.ds(lax.axis_index("z"), 1), :]
    former[...] = former_stack(core[...], features[...], logs + source_new * (1.0 / EPSILON), 0.0)

    def consume(tile, b):
        count = tile.shape[1] // LANES
        for k in range(count):
            piece = tile[:, LANES * k : LANES * k + LANES]
            highest = jnp.max(piece, 0, keepdims=True)
            total = jnp.sum(jnp.exp2(piece - highest), 0, keepdims=True)
            held[pl.ds(b * count + k, 1), :] = highest * LN2 + jnp.log(total)

    in_turns(former, columns, consume, tiles)
    for y in range(4):
        piece = held[8 * y : 8 * y + 8, :]
        for s in range(8):
            at = 8 * (4 * s + y)
            out[at : at + 8, :] = piece


def last_kernel(log_targets):
    def body(parts, weight, out):
        merged = combined([parts[8 * k : 8 * k + 8, :] for k in range(parts.shape[0] // 8)])
        out[...] = EPSILON * (jnp.log(weight[...]) - log_targets - merged)

    return body


def on_device(
    source_points,
    target_points,
    source_potential,
    target_potential,
    source_weight,
    target_weight,
    core_previous,
):
    emb, own = source_points.shape
    dims, span = target_points.shape
    n_z, n_y, n_src = lax.axis_size("z"), lax.axis_size("y"), lax.axis_size(("x", "core"))
    n_plane = n_src * n_y
    rows, columns = own * n_z, span * n_y
    log_sources = math.log(own * n_z * n_plane)
    log_targets = math.log(span * n_z * n_y)
    given = (
        source_points,
        source_potential.reshape(1, own),
        source_weight.reshape(1, own),
        target_points,
        target_potential.reshape(8, LANES),
        target_weight.reshape(8, LANES),
    )
    mine, theirs = pl.pallas_call(
        pack,
        out_shape=(
            jax.ShapeDtypeStruct((9 * n_z, LANES), F32),
            jax.ShapeDtypeStruct((34 * n_plane, LANES), F32),
        ),
        in_specs=[pl.BlockSpec(memory_space=pl.ANY)] * len(given),
        out_specs=(VMEM, VMEM),
        scratch_shapes=[
            pltpu.VMEM((PAD, LANES), F32),
            pltpu.SemaphoreType.DMA((len(given),)),
            *(pltpu.VMEM(a.shape, F32) for a in given),
        ],
        name="pack",
    )(*given)
    theirs = exchange(theirs.reshape(n_plane, 1, 34 * LANES), PLANE).reshape(-1, LANES)
    mine = exchange(mine.reshape(n_z, 1, 9 * LANES), "z").reshape(-1, LANES)
    former = pltpu.VMEM((DEPTH, rows), BF16)
    tiles = (pltpu.VMEM((rows, 512), F32), pltpu.VMEM((rows, 512), F32))
    packed, features, log_source, stack = call(
        core_kernel(log_sources, log_targets),
        [
            ((12 * n_plane, LANES), F32),
            ((PAD, rows), F32),
            ((1, rows), F32),
            ((DEPTH, columns), BF16),
        ],
        (mine, theirs, core_previous),
        scratch=[former, pltpu.VMEM((rows, DEPTH), F32), *tiles],
        name="core",
    )
    parts = exchange(packed.reshape(n_plane, 1, 12 * LANES), PLANE)
    parts = jnp.broadcast_to(jnp.sum(parts, 0, keepdims=True), (n_z, 1, 12 * LANES))
    parts = exchange(parts, "z").reshape(-1, LANES)

    per_lane = pltpu.VMEM((rows, LANES), F32)
    row_parts, core, core_new = call(
        row_kernel,
        [((4 * n_z, LANES), F32), ((PAD, PAD), F32), (core_previous.shape, F32)],
        (parts, features, stack),
        scratch=[former, per_lane, per_lane, *tiles],
        name="rows",
    )
    row_parts = exchange(row_parts.reshape(n_z, 1, rows), "z").reshape(-1, LANES)
    own_rows, column_parts = call(
        column_kernel,
        [((1, own), F32), ((8 * n_plane, LANES), F32)],
        (row_parts, features, log_source, core, stack),
        scratch=[
            former,
            pltpu.VMEM((columns // LANES, LANES), F32),
            pltpu.VMEM((n_z, own), F32),
            *tiles,
        ],
        name="columns",
    )
    column_parts = exchange(column_parts.reshape(n_plane, 1, span), PLANE).reshape(-1, LANES)
    (target_new,) = call(
        last_kernel(log_targets),
        [((8, LANES), F32)],
        (column_parts, target_weight.reshape(8, LANES)),
        name="last",
    )
    return (own_rows.reshape(own), target_new.reshape(span), core_new)


def solution(mesh):
    finer = Mesh(mesh.devices.reshape(4, 2, 4, 16), ALL)
    source, target = P(ALL), P(("y", "z"))
    placed = (
        P(None, ALL),
        P(("x", "core"), ("y", "z")),
        source,
        target,
        source,
        target,
        P(),
    )
    return jax.shard_map(
        on_device, mesh=finer, in_specs=placed, out_specs=(source, target, P()), check_vma=False
    )
```

time: 130 us -> 122 us (0.938)
  blocking collectives: 54.3 us -> 104 us
  starting transfers between devices: 32.1 us -> 0 us
  waiting for transfers between devices: 20.5 us -> 0 us
  Pallas kernels: 18.2 us -> 15.5 us
  other arithmetic: 1.63 us -> 0.13 us
    all_to_all x3 -> x6, blocking collectives: 54.3 us -> 104 us  [exchange(): return lax.all_to_all(copies, axis, split_axis=0, concat_axis=0, tiled=True)]
    all_to_all x3 -> x0, starting transfers between devices: 21.4 us -> none  [exchange(): return lax.all_to_all(copies, axis, split_axis=0, concat_axis=0, tiled=True)]
    all_to_all x3 -> x0, waiting for transfers between devices: 17.8 us -> none  [exchange(): return lax.all_to_all(copies, axis, split_axis=0, concat_axis=0, tiled=True)]
    ppermute x3 -> x0, starting transfers between devices: 10.7 us -> none  [on_device(): lax.ppermute(theirs, 'y', [(i, (i + k) % n_y) for i in range(n_y)])]
    ppermute x3 -> x0, waiting for transfers between devices: 2.65 us -> none  [on_device(): lax.ppermute(theirs, 'y', [(i, (i + k) % n_y) for i in range(n_y)])]
    pallas_call x5 -> x4, Pallas kernels: 15.9 us -> 13.8 us  [call(): pl.pallas_call(body, out_shape=tuple((jax.ShapeDtypeStruct(s, d) for s, d...]
    slice x4 -> x0, local copies, waits for them, and re-layouts: 1.43 us -> none  [the longest x2 1.42 us: turned(): core = jnp.concatenate([core[2:], core[:2]], 0)]
  transfers between devices with their start and end apart: 6 -> 0, of which waited for: 4 -> 0; matrix products, arithmetic and copies ran while one was open for 2% -> 0% of each run, Pallas kernels for 0% -> 0%
where the time goes in v4:
time: 122 us; the launch traced here: 121 us
  blocking collectives  104 us (85%)
  Pallas kernels  15.5 us (13%)
    all_to_all x6, blocking collectives, exchange(): return lax.all_to_all(copies, axis, split_axis=0, concat_axis=0, tiled=True)  104 us
    pallas_call x4, Pallas kernels, call(): pl.pallas_call(body, out_shape=tuple((jax.ShapeDtypeStruct(s, d) for s, d...  13.8 us

profile of v4, /device:TPU:1, one launch (start us, length us, event | category | flops | bytes accessed | tf_op | source)
XLA Modules:
  0.0 121.3 jit_solution(7504190728124173552)
XLA Ops:
  0.6 1.7 %pack.1 = (f32[144,128]{1,0:T(8,128)}, f32[1088,128]{1,0:T(8,128)}) custom-call(f32[32,32]{1,0:T(8,128)} %refs_0_.1, f32[1,32]{1,0:T(1,128)} %bitcast.30, f32[1,32]{1,0:T(1,128)} %bitcast.31, f32[4,1024]{1,0:T(4,128)} %refs_3_.1, f32[8,128]{1,0:T(8,128)} %bitcast.29, f32[8,128]{1,0:T(8,128)} %bitcast.24), custom_call_target="tpu_custom_call" | custom-call | tf_op jit(solution)/shard_map/pack/pallas_call | solution.py:321
  2.4 27.4 %all_to_all.30 = f32[16,1,1152]{2,1,0:T(1,128)S(1)} all-to-all(f32[16,1,1152]{2,1,0:T(1,128)} %bitcast.27), channel_id=1, replica_groups=mesh['x'=4,'core'=2,'y'=4,'z'=16] {'z'}, dimensions={0} | all-to-all | bytes 147456 | tf_op jit(solution)/shard_map/all_to_all | solution.py:38
  29.8 20.8 %all_to_all.31 = f32[32,1,4352]{2,1,0:T(1,128)S(1)} all-to-all(f32[32,1,4352]{2,1,0:T(1,128)} %bitcast.26), channel_id=1, replica_groups=mesh['x'=4,'core'=2,'y'=4,'z'=16] {'x','core','y'}, dimensions={0} | all-to-all | bytes 1114112 | tf_op jit(solution)/shard_map/all_to_all | solution.py:38
  50.6 0.0 copy-start
  50.6 0.7 copy-done
  51.3 6.4 %core.2 = (f32[384,128]{1,0:T(8,128)S(1)}, f32[40,512]{1,0:T(8,128)S(1)}, f32[1,512]{1,0:T(1,128)S(1)}, bf16[256,4096]{1,0:T(8,128)(2,1)S(1)}) custom-call(f32[144,128]{1,0:T(8,128)S(1)} %bitcast.19, f32[1088,128]{1,0:T(8,128)S(1)} %bitcast.16, f32[34,34]{1,0:T(8,128)S(1)} %copy-done), custom_call_target="tpu_custom_call" | custom-call | tf_op jit(solution)/shard_map/core/pallas_call | solution.py:26
  57.7 12.5 %all_to_all.32 = f32[32,1,1536]{2,1,0:T(1,128)S(1)} all-to-all(f32[32,1,1536]{2,1,0:T(1,128)S(1)} %bitcast.20), channel_id=1, replica_groups=mesh['x'=4,'core'=2,'y'=4,'z'=16] {'x','core','y'}, dimensions={0} | all-to-all | bytes 393216 | tf_op jit(solution)/shard_map/all_to_all | solution.py:38
  70.2 0.1 reduce_sum.9
  70.3 0.1 broadcast_in_dim.2
  70.4 14.4 %all_to_all.33 = f32[16,1,1536]{2,1,0:T(1,128)S(1)} all-to-all(f32[16,1,1536]{2,1,0:T(1,128)S(1)} %broadcast_in_dim.2), channel_id=1, replica_groups=mesh['x'=4,'core'=2,'y'=4,'z'=16] {'z'}, dimensions={0} | all-to-all | bytes 196608 | tf_op jit(solution)/shard_map/all_to_all | solution.py:38
  84.7 0.0 copy-start.1
  84.7 3.2 %rows.1 = (f32[64,128]{1,0:T(8,128)S(1)}, f32[40,40]{1,0:T(8,128)S(1)}, f32[34,34]{1,0:T(8,128)}) custom-call(f32[192,128]{1,0:T(8,128)S(1)} %bitcast.18, f32[40,512]{1,0:T(8,128)S(1)} %get-tuple-element.17.features, bf16[256,4096]{1,0:T(8,128)(2,1)S(1)} %get-tuple-element.18.columns), custom_call_target="tpu_custom_call" | custom-call | tf_op jit(solution)/shard_map/rows/pallas_call | solution.py:26
  88.0 16.0 %all_to_all.34 = f32[16,1,512]{2,1,0:T(1,128)S(1)} all-to-all(f32[16,1,512]{2,1,0:T(1,128)S(1)} %bitcast.23), channel_id=1, replica_groups=mesh['x'=4,'core'=2,'y'=4,'z'=16] {'z'}, dimensions={0} | all-to-all | bytes 65536 | tf_op jit(solution)/shard_map/all_to_all | solution.py:38
  104.0 3.5 %columns.1 = (f32[1,32]{1,0:T(1,128)}, f32[256,128]{1,0:T(8,128)S(1)}) custom-call(f32[64,128]{1,0:T(8,128)S(1)} %bitcast.21, f32[40,512]{1,0:T(8,128)S(1)} %get-tuple-element.17.features, f32[1,512]{1,0:T(1,128)S(1)} %get-tuple-element.20.log_source, f32[40,40]{1,0:T(8,128)S(1)} %get-tuple-element.21.core, bf16[256,4096]{1,0:T(8,128)(2,1)S(1)} %get-tuple-element.18.columns), custom_call_target="tpu_custom_call" | custom-call | tf_op jit(solution)/shard_map/columns/pallas_call | solution.py:26
  107.5 13.1 %all_to_all.35 = f32[32,1,1024]{2,1,0:T(1,128)S(1)} all-to-all(f32[32,1,1024]{2,1,0:T(1,128)S(1)} %bitcast.22), channel_id=1, replica_groups=mesh['x'=4,'core'=2,'y'=4,'z'=16] {'x','core','y'}, dimensions={0} | all-to-all | bytes 262144 | tf_op jit(solution)/shard_map/all_to_all | solution.py:38
  120.6 0.0 copy-done.1
  120.6 0.7 last.1
Async XLA Ops:
  50.6 0.7 copy-start
  84.7 35.9 %copy-start.1 = (f32[1024]{0:T(1024)S(1)}, f32[1024]{0:T(1024)}, u32[]{:S(2)}) copy-start(f32[1024]{0:T(1024)} %param.12) | copy-start | bytes 12292

commit v5 on v4

--- a/solution.py
+++ b/solution.py
@@ -18,18 +18,19 @@
 DEPTH = 256
 LOG2E = math.log2(math.e)
 LN2 = math.log(2.0)
+FLOOR = 2.0**-60
 F32, BF16 = jnp.float32, jnp.bfloat16
 VMEM = pl.BlockSpec(memory_space=pltpu.VMEM)
 
 
-def call(body, outs, args, scratch=(), name=None):
+def call(body, outs, args, scratch=(), name=None, grant=8):
     return pl.pallas_call(
         body,
         out_shape=tuple(jax.ShapeDtypeStruct(s, d) for s, d in outs),
         in_specs=[VMEM] * len(args),
         out_specs=tuple(VMEM for _ in outs),
         scratch_shapes=list(scratch),
-        compiler_params=pltpu.CompilerParams(vmem_limit_bytes=48 * 2**20),
+        compiler_params=pltpu.CompilerParams(vmem_limit_bytes=grant * 2**20),
         name=name,
     )(*args)
 
@@ -62,13 +63,14 @@
 
 
 def pack(*refs):
-    given, (out, column_out), held, (sem, *into) = refs[:6], refs[6:8], refs[8], refs[9:]
+    given, (out, column_out, core_out), (held, sem, *into) = refs[:7], refs[7:10], refs[10:]
     copies = [pltpu.make_async_copy(a, b, sem.at[k]) for k, (a, b) in enumerate(zip(given, into))]
     for copy in copies:
         copy.start()
     for copy in copies:
         copy.wait()
-    points, potential, weight, column_points, column_potential, column_weight = into
+    points, potential, weight, column_points, column_potential, column_weight, core = into
+    core_out[...] = turned(core[...])
     value = points[...]
     block = jnp.concatenate([value[8 * k : 8 * k + 8] for k in range(4)], axis=1)
     last = jnp.concatenate(
@@ -139,8 +141,11 @@
     return jnp.where(col < 32, -2.0 * core, core)
 
 
-def former_stack(core, features, row_term, column_factor):
-    weighted = dot(signs(core), features, ((0,), (0,)), HIGHEST) * (2.0 / EPSILON * LOG2E)
+def weighted_core(core, features):
+    return dot(signs(core), features, ((0,), (0,)), HIGHEST) * (2.0 / EPSILON * LOG2E)
+
+
+def former_stack(weighted, row_term, column_factor):
     row = lax.broadcasted_iota(jnp.int32, weighted.shape, 0)
     if row_term is not None:
         weighted = jnp.where(row == 33, weighted + row_term * LOG2E, weighted)
@@ -158,9 +163,8 @@
     return jnp.concatenate([core[:, 32:34], core[:, 0:32]], 1)
 
 
-def core_kernel(log_sources, log_targets):
-    def body(message, arrived, core, packed, features_out, log_out, columns, former, total, *tiles):
-        column_stack(arrived, columns, log_targets)
+def source_kernel(log_sources):
+    def body(message, core, features_out, log_out, former):
         pieces = []
         for k in range(4):
             pieces.append(
@@ -179,8 +183,31 @@
         features_out[...] = features
         log_out[...] = log_source
         former[...] = former_stack(
-            turned(core[...]), features, log_source + last * (1.0 / EPSILON), 1.0
+            weighted_core(core[...], features), log_source + last * (1.0 / EPSILON), 1.0
         )
+
+    return body
+
+
+def core_to_rows(core):
+    tail = jnp.concatenate(
+        [core[30:34, 0:26], jnp.concatenate([core[30:34, 26:34], jnp.zeros((4, 18), F32)], 1)], 0
+    )
+    tail = jnp.concatenate([tail, jnp.zeros((2, 26), F32)], 0)
+    groups = [core[10 * g : 10 * g + 10, 0:34] for g in range(3)]
+    return jnp.concatenate([*groups, tail], 1)
+
+
+def core_from_rows(both):
+    top = jnp.concatenate([both[:, 34 * g : 34 * g + 34] for g in range(3)], 0)
+    last = jnp.concatenate([both[0:4, 102:128], both[4:8, 102:110]], 1)
+    core = jnp.concatenate([top, last, jnp.zeros((PAD - 34, 34), F32)], 0)
+    return jnp.concatenate([core, jnp.zeros((PAD, PAD - 34), F32)], 1)
+
+
+def core_kernel(log_targets):
+    def body(arrived, features, former, packed, columns, total, *tiles):
+        column_stack(arrived, columns, log_targets)
         total[...] = jnp.zeros_like(total)
 
         def consume(tile, b):
@@ -195,31 +222,21 @@
         carried = (
             total[:, 0:PAD] + total[:, 2 * PAD : 3 * PAD] + total[:, 4 * PAD : 5 * PAD]
         )
-        right = jnp.concatenate([points, ones, squares, zeros], 0)
-        core_part = dot(right, carried, ((1,), (0,)), HIGHEST)
-        col = lax.broadcasted_iota(jnp.int32, core_part.shape, 1)
-        ahead = jnp.concatenate([core_part[:, 1:], core_part[:, :1]], 1)
-        behind = jnp.concatenate([core_part[:, -1:], core_part[:, :-1]], 1)
-        core_part = jnp.where(col == 32, ahead, jnp.where(col == 33, behind, core_part))
-        core_part = jnp.where(col < 34, core_part, 0.0)
-        both = jnp.concatenate(
-            [core_part[12 * g : 12 * g + 12] for g in range(3)] + [jnp.zeros((12, 8), F32)], 1
-        )
-        for k in range(packed.shape[0] // 12):
-            packed[12 * k : 12 * k + 12, :] = both
+        part = dot(features[...], carried, ((1,), (0,)), HIGHEST)
+        part = jnp.concatenate([part[0:32], part[33:34], part[32:33]], 0)
+        part = jnp.concatenate([part[:, 0:32], part[:, 33:34], part[:, 32:33]], 1)
+        both = core_to_rows(part)
+        for k in range(packed.shape[0] // 10):
+            packed[10 * k : 10 * k + 10, :] = both
 
     return body
 
 
 def row_kernel(parts, features, columns, out, core_out, core_new, former, highest, total, *tiles):
-    both = parts[0:12, :]
-    for k in range(1, parts.shape[0] // 12):
-        both = both + parts[12 * k : 12 * k + 12, :]
-    core = jnp.concatenate([both[:, PAD * g : PAD * g + PAD] for g in range(3)], 0)
-    core = jnp.concatenate([core, jnp.zeros((PAD - 36, PAD), F32)], 0)
+    core = core_from_rows(sum(parts[10 * k : 10 * k + 10, :] for k in range(parts.shape[0] // 10)))
     core_out[...] = core
     core_new[...] = turned_back(core)
-    former[...] = former_stack(core, features[...], None, 1.0)
+    former[...] = former_stack(weighted_core(core, features[...]), None, 1.0)
     rows = features.shape[1]
     highest[...] = jnp.full(highest.shape, jnp.finfo(F32).min, F32)
     total[...] = jnp.zeros_like(total)
@@ -257,33 +274,63 @@
     return highest + jnp.log(total)
 
 
+def column_pieces(tile, b):
+    count = tile.shape[1] // LANES
+    return [(pl.ds(b * count + k, 1), tile[:, LANES * k : LANES * k + LANES]) for k in range(count)]
+
+
+def in_lanes(rows):
+    return jnp.concatenate([rows[k : k + 1] for k in range(rows.shape[0])], 1)
+
+
+def ahead_kernel(own_parts, features, log_source, core, columns, weighted_out, bound, former, *tiles):
+    weighted = weighted_core(core[...], features[...])
+    weighted_out[...] = weighted
+    term = 2.0 * log_source[...] - in_lanes(own_parts[0:4, :])
+    former[...] = former_stack(weighted, term, 0.0)
+
+    def consume(tile, b):
+        for at, piece in column_pieces(tile, b):
+            bound[at, :] = jnp.max(piece, 0, keepdims=True)
+
+    in_turns(former, columns, consume, tiles)
+
+
 def column_kernel(
-    parts, features, log_source, core, columns, own_out, out, former, held, mine, *tiles
+    parts, log_source, weighted, bound, columns, own_out, out, former, sums, shift, mine, *tiles
 ):
-    merged = combined([parts[4 * k : 4 * k + 4, :] for k in range(parts.shape[0] // 4)])
-    merged = jnp.concatenate([merged[k : k + 1] for k in range(4)], 1)
+    merged = in_lanes(combined([parts[4 * k : 4 * k + 4, :] for k in range(parts.shape[0] // 4)]))
     logs = log_source[...]
     source_new = EPSILON * (logs - merged)
     own = own_out.shape[1]
     for k in range(mine.shape[0]):
         mine[k : k + 1, :] = source_new[:, own * k : own * k + own]
     own_out[...] = mine[pl.ds(lax.axis_index("z"), 1), :]
-    former[...] = former_stack(core[...], features[...], logs + source_new * (1.0 / EPSILON), 0.0)
-
-    def consume(tile, b):
-        count = tile.shape[1] // LANES
-        for k in range(count):
-            piece = tile[:, LANES * k : LANES * k + LANES]
-            highest = jnp.max(piece, 0, keepdims=True)
-            total = jnp.sum(jnp.exp2(piece - highest), 0, keepdims=True)
-            held[pl.ds(b * count + k, 1), :] = highest * LN2 + jnp.log(total)
-
-    in_turns(former, columns, consume, tiles)
+    former[...] = former_stack(weighted[...], logs + source_new * (1.0 / EPSILON), 0.0)
+    shift[...] = bound[...]
+
+    def add(tile, b):
+        for at, piece in column_pieces(tile, b):
+            sums[at, :] = jnp.sum(jnp.exp2(piece - shift[at, :]), 0, keepdims=True)
+
+    in_turns(former, columns, add, tiles)
+    safe = jnp.min(sums[...]) >= FLOOR
+
+    @pl.when(jnp.logical_not(safe))
+    def _():
+        def add_over_largest(tile, b):
+            for at, piece in column_pieces(tile, b):
+                highest = jnp.max(piece, 0, keepdims=True)
+                shift[at, :] = highest
+                sums[at, :] = jnp.sum(jnp.exp2(piece - highest), 0, keepdims=True)
+
+        in_turns(former, columns, add_over_largest, tiles)
+
+    part = shift[...] * LN2 + jnp.log(sums[...])
     for y in range(4):
-        piece = held[8 * y : 8 * y + 8, :]
         for s in range(8):
             at = 8 * (4 * s + y)
-            out[at : at + 8, :] = piece
+            out[at : at + 8, :] = part[8 * y : 8 * y + 8]
 
 
 def last_kernel(log_targets):
@@ -317,15 +364,17 @@
         target_points,
         target_potential.reshape(8, LANES),
         target_weight.reshape(8, LANES),
-    )
-    mine, theirs = pl.pallas_call(
+        core_previous,
+    )
+    mine, theirs, previous = pl.pallas_call(
         pack,
         out_shape=(
             jax.ShapeDtypeStruct((9 * n_z, LANES), F32),
             jax.ShapeDtypeStruct((34 * n_plane, LANES), F32),
+            jax.ShapeDtypeStruct((PAD, PAD), F32),
         ),
-        in_specs=[pl.BlockSpec(memory_space=pl.ANY)] * len(given),
-        out_specs=(VMEM, VMEM),
+        in_specs=[pl.BlockSpec(memory_space=pltpu.HBM)] * len(given),
+        out_specs=(VMEM, VMEM, VMEM),
         scratch_shapes=[
             pltpu.VMEM((PAD, LANES), F32),
             pltpu.SemaphoreType.DMA((len(given),)),
@@ -337,42 +386,56 @@
     mine = exchange(mine.reshape(n_z, 1, 9 * LANES), "z").reshape(-1, LANES)
     former = pltpu.VMEM((DEPTH, rows), BF16)
     tiles = (pltpu.VMEM((rows, 512), F32), pltpu.VMEM((rows, 512), F32))
-    packed, features, log_source, stack = call(
-        core_kernel(log_sources, log_targets),
-        [
-            ((12 * n_plane, LANES), F32),
-            ((PAD, rows), F32),
-            ((1, rows), F32),
-            ((DEPTH, columns), BF16),
-        ],
-        (mine, theirs, core_previous),
-        scratch=[former, pltpu.VMEM((rows, DEPTH), F32), *tiles],
+    features, log_source, core_former = call(
+        source_kernel(log_sources),
+        [((PAD, rows), F32), ((1, rows), F32), ((DEPTH, rows), BF16)],
+        (mine, previous),
+        name="sources",
+    )
+    packed, stack = call(
+        core_kernel(log_targets),
+        [((10 * n_plane, LANES), F32), ((DEPTH, columns), BF16)],
+        (theirs, features, core_former),
+        scratch=[pltpu.VMEM((rows, DEPTH), F32), *tiles],
         name="core",
-    )
-    parts = exchange(packed.reshape(n_plane, 1, 12 * LANES), PLANE)
-    parts = jnp.broadcast_to(jnp.sum(parts, 0, keepdims=True), (n_z, 1, 12 * LANES))
+        grant=16,
+    )
+    parts = exchange(packed.reshape(n_plane, 1, 10 * LANES), PLANE)
+    parts = jnp.broadcast_to(jnp.sum(parts, 0, keepdims=True), (n_z, 1, 10 * LANES))
     parts = exchange(parts, "z").reshape(-1, LANES)
 
     per_lane = pltpu.VMEM((rows, LANES), F32)
-    row_parts, core, core_new = call(
+    own_parts, core, core_new = call(
         row_kernel,
         [((4 * n_z, LANES), F32), ((PAD, PAD), F32), (core_previous.shape, F32)],
         (parts, features, stack),
         scratch=[former, per_lane, per_lane, *tiles],
         name="rows",
-    )
-    row_parts = exchange(row_parts.reshape(n_z, 1, rows), "z").reshape(-1, LANES)
+        grant=16,
+    )
+    row_parts = exchange(own_parts.reshape(n_z, 1, rows), "z").reshape(-1, LANES)
+    per_column = (columns // LANES, LANES)
+    weighted, bound = call(
+        ahead_kernel,
+        [((PAD, rows), F32), (per_column, F32)],
+        (own_parts, features, log_source, core, stack),
+        scratch=[former, *tiles],
+        name="ahead",
+        grant=16,
+    )
     own_rows, column_parts = call(
         column_kernel,
         [((1, own), F32), ((8 * n_plane, LANES), F32)],
-        (row_parts, features, log_source, core, stack),
+        (row_parts, log_source, weighted, bound, stack),
         scratch=[
             former,
-            pltpu.VMEM((columns // LANES, LANES), F32),
+            pltpu.VMEM(per_column, F32),
+            pltpu.VMEM(per_column, F32),
             pltpu.VMEM((n_z, own), F32),
             *tiles,
         ],
         name="columns",
+        grant=16,
     )
     column_parts = exchange(column_parts.reshape(n_plane, 1, span), PLANE).reshape(-1, LANES)
     (target_new,) = call(

time: 122 us -> 124 us (1.016)
  blocking collectives: 104 us -> 66.9 us
  waiting for transfers between devices: 0 us -> 18.4 us
  starting transfers between devices: 0 us -> 13.8 us
  Pallas kernels: 15.5 us -> 22.5 us
    all_to_all x6 -> x4, blocking collectives: 104 us -> 66.9 us  [exchange(): return lax.all_to_all(copies, axis, split_axis=0, concat_axis=0, tiled=True)]
    all_to_all x0 -> x2, waiting for transfers between devices: none -> 18.4 us  [exchange(): return lax.all_to_all(copies, axis, split_axis=0, concat_axis=0, tiled=True)]
    all_to_all x0 -> x2, starting transfers between devices: none -> 13.8 us  [exchange(): return lax.all_to_all(copies, axis, split_axis=0, concat_axis=0, tiled=True)]
    pallas_call x4 -> x6, Pallas kernels: 13.8 us -> 20.8 us  [call(): pl.pallas_call(body, out_shape=tuple((jax.ShapeDtypeStruct(s, d) for s, d...]
  transfers between devices with their start and end apart: 0 -> 2, of which waited for: 0 -> 2; matrix products, arithmetic and copies ran while one was open for 0% -> 0% of each run, Pallas kernels for 0% -> 3%
where the time goes in v5:
time: 124 us; the launch traced here: 123 us
  blocking collectives  66.9 us (54%)
  Pallas kernels  22.5 us (18%)
  waiting for transfers between devices  18.4 us (15%)
  starting transfers between devices  13.8 us (11%)
    all_to_all x4, blocking collectives, exchange(): return lax.all_to_all(copies, axis, split_axis=0, concat_axis=0, tiled=True)  66.9 us
    pallas_call x6, Pallas kernels, call(): pl.pallas_call(body, out_shape=tuple((jax.ShapeDtypeStruct(s, d) for s, d...  20.8 us
    all_to_all x2, waiting for transfers between devices, exchange(): return lax.all_to_all(copies, axis, split_axis=0, concat_axis=0, tiled=True)  18.4 us
    all_to_all x2, starting transfers between devices, exchange(): return lax.all_to_all(copies, axis, split_axis=0, concat_axis=0, tiled=True)  13.8 us
  transfers between devices with their start and end apart: 2, of which 2 were waited for; matrix products, arithmetic and copies ran while one was open for 0% of the time, Pallas kernels for 3%

profile of v5, /device:TPU:1, one launch (start us, length us, event | category | flops | bytes accessed | tf_op | source)
XLA Modules:
  0.0 123.2 jit_solution(10697087580772872665)
XLA Ops:
  0.6 1.8 %pack.1 = (f32[144,128]{1,0:T(8,128)}, f32[1088,128]{1,0:T(8,128)}, f32[40,40]{1,0:T(8,128)}) custom-call(f32[32,32]{1,0:T(8,128)} %refs_0_.1, f32[1,32]{1,0:T(1,128)} %bitcast.29, f32[1,32]{1,0:T(1,128)} %bitcast.30, f32[4,1024]{1,0:T(4,128)} %refs_3_.1, f32[8,128]{1,0:T(8,128)} %bitcast.28, f32[8,128]{1,0:T(8,128)} %bitcast.23, f32[34,34]{1,0:T(8,128)} %refs_6_.1), custom_call_target="tpu_custom_call" | custom-call | tf_op jit(solution)/shard_map/pack/pallas_call | solution.py:369
  2.4 27.4 %all_to_all.30 = f32[16,1,1152]{2,1,0:T(1,128)S(1)} all-to-all(f32[16,1,1152]{2,1,0:T(1,128)} %bitcast.26), channel_id=1, replica_groups=mesh['x'=4,'core'=2,'y'=4,'z'=16] {'z'}, dimensions={0} | all-to-all | bytes 147456 | tf_op jit(solution)/shard_map/all_to_all | solution.py:39
  29.8 9.4 %all-to-all-start = ((f32[32,1,4352]{2,1,0:T(1,128)}), f32[32,1,4352]{2,1,0:T(1,128)S(1)}, u32[]{:S(2)}, u32[]{:S(2)}) async-start(f32[32,1,4352]{2,1,0:T(1,128)} %bitcast.25), calls=%async_computation | async-start | bytes 1114112 | tf_op jit(solution)/shard_map/all_to_all | solution.py:39
  39.3 0.0 copy-start
  39.3 0.7 copy-done
  40.0 0.4 sources.1
  40.4 10.3 %all-to-all-done = f32[32,1,4352]{2,1,0:T(1,128)S(1)} async-done(((f32[32,1,4352]{2,1,0:T(1,128)}), f32[32,1,4352]{2,1,0:T(1,128)S(1)}, u32[]{:S(2)}, u32[]{:S(2)}) %all-to-all-start) | async-done | bytes 557088 | tf_op jit(solution)/shard_map/all_to_all | solution.py:39
  50.6 6.1 %core.1 = (f32[320,128]{1,0:T(8,128)S(1)}, bf16[256,4096]{1,0:T(8,128)(2,1)S(1)}) custom-call(f32[1088,128]{1,0:T(8,128)S(1)} %bitcast.16, f32[40,512]{1,0:T(8,128)S(1)} %get-tuple-element.21.features, bf16[256,512]{1,0:T(8,128)(2,1)S(1)} %get-tuple-element.22.former), custom_call_target="tpu_custom_call" | custom-call | tf_op jit(solution)/shard_map/core/pallas_call | solution.py:27
  56.8 12.2 %all_to_all.31 = f32[32,1,1280]{2,1,0:T(1,128)S(1)} all-to-all(f32[32,1,1280]{2,1,0:T(1,128)S(1)} %bitcast.20), channel_id=1, replica_groups=mesh['x'=4,'core'=2,'y'=4,'z'=16] {'x','core','y'}, dimensions={0} | all-to-all | bytes 327680 | tf_op jit(solution)/shard_map/all_to_all | solution.py:39
  68.9 0.1 reduce_sum.9
  69.1 14.3 %all_to_all.32 = f32[16,1,1280]{2,1,0:T(1,128)S(1)} all-to-all(f32[16,1,1280]{2,1,0:T(1,128)S(1)} %broadcast_in_dim.2), channel_id=1, replica_groups=mesh['x'=4,'core'=2,'y'=4,'z'=16] {'z'}, dimensions={0} | all-to-all | bytes 163840 | tf_op jit(solution)/shard_map/all_to_all | solution.py:39
  83.4 3.9 %rows.1 = (f32[64,128]{1,0:T(8,128)}, f32[40,40]{1,0:T(8,128)S(1)}, f32[34,34]{1,0:T(8,128)}) custom-call(f32[160,128]{1,0:T(8,128)S(1)} %bitcast.18, f32[40,512]{1,0:T(8,128)S(1)} %get-tuple-element.21.features, bf16[256,4096]{1,0:T(8,128)(2,1)S(1)} %get-tuple-element.24.columns), custom_call_target="tpu_custom_call" | custom-call | tf_op jit(solution)/shard_map/rows/pallas_call | solution.py:27
  87.3 4.4 %all-to-all-start.4 = ((f32[16,1,512]{2,1,0:T(1,128)}), f32[16,1,512]{2,1,0:T(1,128)S(1)}, u32[]{:S(2)}, u32[]{:S(2)}) async-start(f32[16,1,512]{2,1,0:T(1,128)} %bitcast.10), calls=%async_computation.4 | async-start | bytes 65536 | tf_op jit(solution)/shard_map/all_to_all | solution.py:39
  91.8 0.0 copy-start.1
  91.8 3.3 %ahead.1 = (f32[40,512]{1,0:T(8,128)S(1)}, f32[32,128]{1,0:T(8,128)S(1)}) custom-call(f32[64,128]{1,0:T(8,128)} %get-tuple-element.25.own_parts, f32[40,512]{1,0:T(8,128)S(1)} %get-tuple-element.21.features, f32[1,512]{1,0:T(1,128)S(1)} %get-tuple-element.26.log_source, f32[40,40]{1,0:T(8,128)S(1)} %get-tuple-element.27.core, ...), custom_call_target="tpu_custom_call" | custom-call | tf_op jit(solution)/shard_map/ahead/pallas_call | solution.py:27
  95.1 8.1 %all-to-all-done.4 = f32[16,1,512]{2,1,0:T(1,128)S(1)} async-done(((f32[16,1,512]{2,1,0:T(1,128)}), f32[16,1,512]{2,1,0:T(1,128)S(1)}, u32[]{:S(2)}, u32[]{:S(2)}) %all-to-all-start.4) | async-done | bytes 32800 | tf_op jit(solution)/shard_map/all_to_all | solution.py:39
  103.2 6.4 %columns.1 = (f32[1,32]{1,0:T(1,128)}, f32[256,128]{1,0:T(8,128)S(1)}) custom-call(f32[64,128]{1,0:T(8,128)S(1)} %bitcast.21, f32[1,512]{1,0:T(1,128)S(1)} %get-tuple-element.26.log_source, f32[40,512]{1,0:T(8,128)S(1)} %get-tuple-element.28.weighted, f32[32,128]{1,0:T(8,128)S(1)} %get-tuple-element.29.bound, bf16[256,4096]{1,0:T(8,128)(2,1)S(1)} %get-tuple-element.24.columns), custom_call_target="tpu_custom_call" | custom-call | tf_op jit(solution)/shard_map/columns/pallas_call | solution.py:27
  109.6 12.9 %all_to_all.33 = f32[32,1,1024]{2,1,0:T(1,128)S(1)} all-to-all(f32[32,1,1024]{2,1,0:T(1,128)S(1)} %bitcast.22), channel_id=1, replica_groups=mesh['x'=4,'core'=2,'y'=4,'z'=16] {'x','core','y'}, dimensions={0} | all-to-all | bytes 262144 | tf_op jit(solution)/shard_map/all_to_all | solution.py:39
  122.6 0.0 copy-done.1
  122.6 0.7 last.1
  (1 shorter events, 0.0 us)
Async XLA Ops:
  29.8 20.8 %all-to-all-start = ((f32[32,1,4352]{2,1,0:T(1,128)}), f32[32,1,4352]{2,1,0:T(1,128)S(1)}, u32[]{:S(2)}, u32[]{:S(2)}) async-start(f32[32,1,4352]{2,1,0:T(1,128)} %bitcast.25), calls=%async_computation | async-start | bytes 1114112 | tf_op jit(solution)/shard_map/all_to_all | solution.py:39
  39.3 0.7 copy-start
  87.3 15.9 %all-to-all-start.4 = ((f32[16,1,512]{2,1,0:T(1,128)}), f32[16,1,512]{2,1,0:T(1,128)S(1)}, u32[]{:S(2)}, u32[]{:S(2)}) async-start(f32[16,1,512]{2,1,0:T(1,128)} %bitcast.10), calls=%async_computation.4 | async-start | bytes 65536 | tf_op jit(solution)/shard_map/all_to_all | solution.py:39
  91.8 30.8 %copy-start.1 = (f32[1024]{0:T(1024)S(1)}, f32[1024]{0:T(1024)}, u32[]{:S(2)}) copy-start(f32[1024]{0:T(1024)} %param.12) | copy-start | bytes 12292

commit v6 on v5

v6 whole, which is shorter than its diff:
```python
import functools
import math

import jax
import jax.numpy as jnp
from jax import lax
from jax.experimental import pallas as pl
from jax.experimental.pallas import tpu as pltpu
from jax.sharding import Mesh
from jax.sharding import PartitionSpec as P

PLANE = ("x", "core", "y")
ALL = ("x", "core", "y", "z")
EPSILON = 0.5
HIGHEST = lax.Precision.HIGHEST
LANES = 128
PAD = 40
DEPTH = 256
LOG2E = math.log2(math.e)
LN2 = math.log(2.0)
F32, BF16 = jnp.float32, jnp.bfloat16
VMEM = pl.BlockSpec(memory_space=pltpu.VMEM)


def call(body, outs, args, scratch=(), name=None, grant=8):
    return pl.pallas_call(
        body,
        out_shape=tuple(jax.ShapeDtypeStruct(s, d) for s, d in outs),
        in_specs=[VMEM] * len(args),
        out_specs=tuple(VMEM for _ in outs),
        scratch_shapes=list(scratch),
        compiler_params=pltpu.CompilerParams(vmem_limit_bytes=grant * 2**20),
        name=name,
    )(*args)


def exchange(copies, axis):
    return lax.all_to_all(copies, axis, split_axis=0, concat_axis=0, tiled=True)


def dot(former, latter, dims, precision=None):
    return lax.dot_general(
        former, latter, (dims, ((), ())), precision=precision, preferred_element_type=F32
    )


def split(value):
    first = value.astype(BF16).astype(F32)
    rest = value - first
    second = rest.astype(BF16).astype(F32)
    return first, second, rest - second


def stacked(pieces, order):
    blocks = [pieces[k] for k in order]
    filler = jnp.zeros((DEPTH - PAD * len(order), pieces[0].shape[1]), F32)
    return jnp.concatenate([*blocks, filler], 0).astype(BF16)


LATTER_ORDER = (0, 0, 1, 0, 2, 1)
FORMER_ORDER = (0, 1, 0, 2, 0, 1)


def pack(*refs):
    given, (out, column_out), (held, sem, *into) = refs[:7], refs[7:9], refs[9:]
    copies = [pltpu.make_async_copy(a, b, sem.at[k]) for k, (a, b) in enumerate(zip(given, into))]
    for copy in copies:
        copy.start()
    for copy in copies:
        copy.wait()
    points, potential, weight, column_points, column_potential, column_weight, core = into
    value = points[...]
    block = jnp.concatenate([value[8 * k : 8 * k + 8] for k in range(4)], axis=1)
    last = jnp.concatenate(
        [potential[...], weight[...], jnp.ones((1, LANES - 64), F32)], axis=1
    )
    held[0:34, 0:34] = core[...]
    z = lax.axis_index("z")
    share = [held[pl.ds(z + 16 * g, 1), 0:34] for g in range(3)]
    share = jnp.concatenate([*share, jnp.zeros((1, LANES - 3 * 34), F32)], 1)
    both = jnp.concatenate([block, last, share], 0)
    for k in range(out.shape[0] // 10):
        out[10 * k : 10 * k + 10, :] = both
    for r in range(4):
        for k in range(8):
            held[8 * r + k : 8 * r + k + 1, :] = column_points[
                r : r + 1, LANES * k : LANES * k + LANES
            ]
    src = lax.axis_index(("x", "core"))
    held[32:33, :] = column_potential[pl.ds(src, 1), :]
    held[33:34, :] = column_weight[pl.ds(src, 1), :]
    both = held[0:34, :]
    for k in range(column_out.shape[0] // 34):
        column_out[34 * k : 34 * k + 34, :] = both


def column_stack(message, out, y, log_targets):
    for k in range(8):
        points = jnp.concatenate(
            [message[pl.ds(34 * (4 * s + y) + k, 4, stride=8), :] for s in range(8)], 0
        )
        squares = jnp.sum(points * points, 0, keepdims=True)
        at = 34 * (4 * k + y) + 32
        offset = jnp.log(message[pl.ds(at + 1, 1), :]) - log_targets
        offset = (offset + message[pl.ds(at, 1), :] * (1.0 / EPSILON)) * LOG2E
        tail = jnp.concatenate(
            [squares, jnp.ones((1, LANES), F32), offset, jnp.zeros((5, LANES), F32)], 0
        )
        value = jnp.concatenate([points, tail], 0)
        col = pl.multiple_of(1024 * y + LANES * k, LANES)
        out[:, pl.ds(col, LANES)] = stacked(split(value), LATTER_ORDER)


def in_turns(former, columns, consume, tiles, prepare=None):
    count = len(tiles)
    lead = count // 2
    width = tiles[0].shape[1]
    blocks = columns.shape[1] // width

    def fill(k, b):
        at = pl.multiple_of(jnp.minimum(b, blocks - 1) * width, width)
        tiles[k][...] = dot(former[...], columns[:, pl.ds(at, width)], ((0,), (0,)))

    for k in range(lead):
        fill(k, k)

    def step(i, _):
        for k in range(count):
            if prepare and k == count // 2:
                prepare(i + 1)
            fill((k + lead) % count, count * i + k + lead)
            consume(tiles[k], count * i + k)
        return 0

    lax.fori_loop(0, blocks // count, step, 0)


def signs(core):
    row = lax.broadcasted_iota(jnp.int32, core.shape, 0)
    col = lax.broadcasted_iota(jnp.int32, core.shape, 1)
    core = jnp.where(row < 32, -2.0 * core, core)
    return jnp.where(col < 32, -2.0 * core, core)


def weighted_core(core, features):
    return dot(signs(core), features, ((0,), (0,)), HIGHEST) * (2.0 / EPSILON * LOG2E)


def former_stack(weighted, row_term, column_factor):
    row = lax.broadcasted_iota(jnp.int32, weighted.shape, 0)
    if row_term is not None:
        weighted = jnp.where(row == 33, weighted + row_term * LOG2E, weighted)
    weighted = jnp.where(row == 34, column_factor, weighted)
    return stacked(split(weighted), FORMER_ORDER)


def turned(core):
    core = jnp.concatenate([core[2:34], core[0:2], jnp.zeros((PAD - 34, 34), F32)], 0)
    return jnp.concatenate([core[:, 2:34], core[:, 0:2], jnp.zeros((PAD, PAD - 34), F32)], 1)


def turned_back(core):
    core = jnp.concatenate([core[32:34], core[0:32]], 0)
    return jnp.concatenate([core[:, 32:34], core[:, 0:32]], 1)


def unpacked_sources(message, log_sources):
    pieces = []
    for k in range(4):
        pieces.append(
            jnp.concatenate(
                [message[10 * z : 10 * z + 8, 32 * k : 32 * k + 32] for z in range(16)], 1
            )
        )
    points = jnp.concatenate(pieces, 0)
    last = jnp.concatenate([message[10 * z + 8 : 10 * z + 9, 0:32] for z in range(16)], 1)
    weight = jnp.concatenate([message[10 * z + 8 : 10 * z + 9, 32:64] for z in range(16)], 1)
    squares = jnp.sum(points * points, 0, keepdims=True)
    zeros = jnp.zeros((6, squares.shape[1]), F32)
    features = jnp.concatenate([points, squares, jnp.ones_like(squares), zeros], 0)
    shares = message[pl.ds(9, 16, stride=10), :]
    core = jnp.concatenate([shares[:, 34 * g : 34 * g + 34] for g in range(3)], 0)
    return features, jnp.log(weight) - log_sources, last, turned(core)


def core_to_rows(core):
    tail = jnp.concatenate(
        [core[30:34, 0:26], jnp.concatenate([core[30:34, 26:34], jnp.zeros((4, 18), F32)], 1)], 0
    )
    tail = jnp.concatenate([tail, jnp.zeros((2, 26), F32)], 0)
    groups = [core[10 * g : 10 * g + 10, 0:34] for g in range(3)]
    return jnp.concatenate([*groups, tail], 1)


def core_from_rows(both):
    top = jnp.concatenate([both[:, 34 * g : 34 * g + 34] for g in range(3)], 0)
    last = jnp.concatenate([both[0:4, 102:128], both[4:8, 102:110]], 1)
    core = jnp.concatenate([top, last, jnp.zeros((PAD - 34, 34), F32)], 0)
    return jnp.concatenate([core, jnp.zeros((PAD, PAD - 34), F32)], 1)


def core_kernel(log_sources, log_targets):
    def body(message, arrived, packed, columns, features, log_out, former, total, *tiles):
        value, log_source, potential, core = unpacked_sources(message, log_sources)
        features[...] = value
        log_out[...] = log_source
        former[...] = former_stack(
            weighted_core(core, value), log_source + potential * (1.0 / EPSILON), 1.0
        )
        total[...] = jnp.zeros_like(total)

        def prepare(y):
            column_stack(arrived, columns, jnp.minimum(y, 3), log_targets)

        prepare(0)

        def consume(tile, b):
            width = tile.shape[1]
            stack = columns[:, pl.ds(pl.multiple_of(b * width, width), width)]
            plan = jnp.exp2(tile[...])
            high = plan.astype(BF16)
            low = (plan - high.astype(F32)).astype(BF16)
            total[...] += dot(high, stack, ((1,), (1,))) + dot(low, stack, ((1,), (1,)))

        in_turns(former, columns, consume, tiles, prepare)
        carried = (
            total[:, 0:PAD] + total[:, 2 * PAD : 3 * PAD] + total[:, 4 * PAD : 5 * PAD]
        )
        part = dot(features[...], carried, ((1,), (0,)), HIGHEST)
        part = jnp.concatenate([part[0:32], part[33:34], part[32:33]], 0)
        part = jnp.concatenate([part[:, 0:32], part[:, 33:34], part[:, 32:33]], 1)
        both = core_to_rows(part)
        for k in range(packed.shape[0] // 10):
            packed[10 * k : 10 * k + 10, :] = both

    return body


def row_kernel(parts, features, columns, out, core_out, former, highest, total, *tiles):
    core = core_from_rows(sum(parts[10 * k : 10 * k + 10, :] for k in range(parts.shape[0] // 10)))
    core_out[...] = core
    former[...] = former_stack(weighted_core(core, features[...]), None, 1.0)
    rows = features.shape[1]
    highest[...] = jnp.full(highest.shape, jnp.finfo(F32).min, F32)
    total[...] = jnp.zeros_like(total)

    def consume(tile, _):
        for r in range(0, rows, 64):
            at = pl.ds(r, 64)
            pieces = [tile[at, LANES * k : LANES * k + LANES] for k in range(tile.shape[1] // LANES)]
            before = highest[at, :]
            now = largest([before, *pieces])
            highest[at, :] = now
            total[at, :] = total[at, :] * jnp.exp2(before - now) + sum(
                jnp.exp2(p - now) for p in pieces
            )

    in_turns(former, columns, consume, tiles)
    lanes = highest[...]
    top = jnp.max(lanes, 1, keepdims=True)
    added = jnp.sum(total[...] * jnp.exp2(lanes - top), 1, keepdims=True)
    part = top * LN2 + jnp.log(added)
    wide = jnp.broadcast_to(part, (rows, LANES))
    flat = [jnp.transpose(wide[LANES * k : LANES * k + LANES])[0:1] for k in range(4)]
    both = jnp.concatenate(flat, 0)
    for k in range(out.shape[0] // 4):
        out[4 * k : 4 * k + 4, :] = both


def largest(values):
    return functools.reduce(jnp.maximum, values)


def combined(values):
    highest = largest(values)
    total = sum(jnp.exp(v - highest) for v in values)
    return highest + jnp.log(total)


def column_pieces(tile, b):
    count = tile.shape[1] // LANES
    return [(pl.ds(b * count + k, 1), tile[:, LANES * k : LANES * k + LANES]) for k in range(count)]


def in_lanes(rows):
    return jnp.concatenate([rows[k : k + 1] for k in range(rows.shape[0])], 1)


def column_kernel(
    parts, log_source, features, core, columns, own_out, out, former, held, mine, *tiles
):
    merged = in_lanes(combined([parts[4 * k : 4 * k + 4, :] for k in range(parts.shape[0] // 4)]))
    logs = log_source[...]
    source_new = EPSILON * (logs - merged)
    own = own_out.shape[1]
    for k in range(mine.shape[0]):
        mine[k : k + 1, :] = source_new[:, own * k : own * k + own]
    own_out[...] = mine[pl.ds(lax.axis_index("z"), 1), :]
    weighted = weighted_core(core[...], features[...])
    former[...] = former_stack(weighted, logs + source_new * (1.0 / EPSILON), 0.0)

    def consume(tile, b):
        for at, piece in column_pieces(tile, b):
            highest = jnp.max(piece, 0, keepdims=True)
            total = jnp.sum(jnp.exp2(piece - highest), 0, keepdims=True)
            held[at, :] = highest * LN2 + jnp.log(total)

    in_turns(former, columns, consume, tiles)
    for y in range(4):
        piece = held[8 * y : 8 * y + 8, :]
        for s in range(8):
            at = 8 * (4 * s + y)
            out[at : at + 8, :] = piece


def last_kernel(log_targets):
    def body(parts, weight, own_rows, core, out, own_out, core_out):
        own_out[...] = own_rows[...]
        core_out[...] = turned_back(core[...])
        merged = combined([parts[8 * k : 8 * k + 8, :] for k in range(parts.shape[0] // 8)])
        out[...] = EPSILON * (jnp.log(weight[...]) - log_targets - merged)

    return body


def on_device(
    source_points,
    target_points,
    source_potential,
    target_potential,
    source_weight,
    target_weight,
    core_previous,
):
    emb, own = source_points.shape
    dims, span = target_points.shape
    n_z, n_y, n_src = lax.axis_size("z"), lax.axis_size("y"), lax.axis_size(("x", "core"))
    n_plane = n_src * n_y
    rows, columns = own * n_z, span * n_y
    log_sources = math.log(own * n_z * n_plane)
    log_targets = math.log(span * n_z * n_y)
    given = (
        source_points,
        source_potential.reshape(1, own),
        source_weight.reshape(1, own),
        target_points,
        target_potential.reshape(8, LANES),
        target_weight.reshape(8, LANES),
        core_previous,
    )
    mine, theirs = pl.pallas_call(
        pack,
        out_shape=(
            jax.ShapeDtypeStruct((10 * n_z, LANES), F32),
            jax.ShapeDtypeStruct((34 * n_plane, LANES), F32),
        ),
        in_specs=[pl.BlockSpec(memory_space=pltpu.HBM)] * len(given),
        out_specs=(VMEM, VMEM),
        scratch_shapes=[
            pltpu.VMEM((48, LANES), F32),
            pltpu.SemaphoreType.DMA((len(given),)),
            *(pltpu.VMEM(a.shape, F32) for a in given),
        ],
        name="pack",
    )(*given)
    theirs = exchange(theirs.reshape(n_plane, 1, 34 * LANES), PLANE).reshape(-1, LANES)
    mine = exchange(mine.reshape(n_z, 1, 10 * LANES), "z").reshape(-1, LANES)
    former = pltpu.VMEM((DEPTH, rows), BF16)
    tile = pltpu.VMEM((rows, 512), F32)
    packed, stack, features, log_source = call(
        core_kernel(log_sources, log_targets),
        [
            ((10 * n_plane, LANES), F32),
            ((DEPTH, columns), BF16),
            ((PAD, rows), F32),
            ((1, rows), F32),
        ],
        (mine, theirs),
        scratch=[former, pltpu.VMEM((rows, DEPTH), F32), tile, tile],
        name="core",
        grant=16,
    )
    parts = exchange(packed.reshape(n_plane, 1, 10 * LANES), PLANE)
    parts = jnp.broadcast_to(jnp.sum(parts, 0, keepdims=True), (n_z, 1, 10 * LANES))
    parts = exchange(parts, "z").reshape(-1, LANES)

    per_lane = pltpu.VMEM((rows, LANES), F32)
    row_parts, core = call(
        row_kernel,
        [((4 * n_z, LANES), F32), ((PAD, PAD), F32)],
        (parts, features, stack),
        scratch=[former, per_lane, per_lane, tile, tile, tile, tile],
        name="rows",
        grant=16,
    )
    row_parts = exchange(row_parts.reshape(n_z, 1, rows), "z").reshape(-1, LANES)
    own_rows, column_parts = call(
        column_kernel,
        [((1, own), F32), ((8 * n_plane, LANES), F32)],
        (row_parts, log_source, features, core, stack),
        scratch=[
            former,
            pltpu.VMEM((columns // LANES, LANES), F32),
            pltpu.VMEM((n_z, own), F32),
            *(tile, tile, tile, tile),
        ],
        name="columns",
        grant=16,
    )
    column_parts = exchange(column_parts.reshape(n_plane, 1, span), PLANE).reshape(-1, LANES)
    target_new, own_rows, core_new = call(
        last_kernel(log_targets),
        [((8, LANES), F32), ((1, own), F32), (core_previous.shape, F32)],
        (column_parts, target_weight.reshape(8, LANES), own_rows, core),
        name="last",
    )
    return (own_rows.reshape(own), target_new.reshape(span), core_new)


def solution(mesh):
    finer = Mesh(mesh.devices.reshape(4, 2, 4, 16), ALL)
    source, target = P(ALL), P(("y", "z"))
    placed = (
        P(None, ALL),
        P(("x", "core"), ("y", "z")),
        source,
        target,
        source,
        target,
        P(),
    )
    return jax.shard_map(
        on_device, mesh=finer, in_specs=placed, out_specs=(source, target, P()), check_vma=False
    )
```

time: 124 us -> 120 us (0.968)
  blocking collectives: 66.9 us -> 103 us
  waiting for transfers between devices: 18.4 us -> 0 us
  starting transfers between devices: 13.8 us -> 0 us
  Pallas kernels: 22.5 us -> 15.1 us
    all_to_all x4 -> x6, blocking collectives: 66.9 us -> 103 us  [exchange(): return lax.all_to_all(copies, axis, split_axis=0, concat_axis=0, tiled=True)]
    all_to_all x2 -> x0, waiting for transfers between devices: 18.4 us -> none  [exchange(): return lax.all_to_all(copies, axis, split_axis=0, concat_axis=0, tiled=True)]
    all_to_all x2 -> x0, starting transfers between devices: 13.8 us -> none  [exchange(): return lax.all_to_all(copies, axis, split_axis=0, concat_axis=0, tiled=True)]
    pallas_call x6 -> x4, Pallas kernels: 20.8 us -> 13.3 us  [call(): pl.pallas_call(body, out_shape=tuple((jax.ShapeDtypeStruct(s, d) for s, d...]
  transfers between devices with their start and end apart: 2 -> 0, of which waited for: 2 -> 0; matrix products, arithmetic and copies ran while one was open for 0% -> 0% of each run, Pallas kernels for 3% -> 0%
where the time goes in v6:
time: 120 us; the launch traced here: 119 us
  blocking collectives  103 us (86%)
  Pallas kernels  15.1 us (13%)
    all_to_all x6, blocking collectives, exchange(): return lax.all_to_all(copies, axis, split_axis=0, concat_axis=0, tiled=True)  103 us
    pallas_call x4, Pallas kernels, call(): pl.pallas_call(body, out_shape=tuple((jax.ShapeDtypeStruct(s, d) for s, d...  13.3 us

profile of v6, /device:TPU:1, one launch (start us, length us, event | category | flops | bytes accessed | tf_op | source)
XLA Modules:
  0.0 119.4 jit_solution(2034503029351612836)
XLA Ops:
  0.6 1.8 %pack.1 = (f32[160,128]{1,0:T(8,128)}, f32[1088,128]{1,0:T(8,128)}) custom-call(f32[32,32]{1,0:T(8,128)} %refs_0_.1, f32[1,32]{1,0:T(1,128)} %bitcast.29, f32[1,32]{1,0:T(1,128)} %bitcast.30, f32[4,1024]{1,0:T(4,128)} %refs_3_.1, f32[8,128]{1,0:T(8,128)} %bitcast.28, f32[8,128]{1,0:T(8,128)} %bitcast.24, f32[34,34]{1,0:T(8,128)} %refs_6_.1), custom_call_target="tpu_custom_call" | custom-call | tf_op jit(solution)/shard_map/pack/pallas_call | solution.py:351
  2.4 27.5 %all_to_all.30 = f32[16,1,1280]{2,1,0:T(1,128)S(1)} all-to-all(f32[16,1,1280]{2,1,0:T(1,128)} %bitcast.27), channel_id=1, replica_groups=mesh['x'=4,'core'=2,'y'=4,'z'=16] {'z'}, dimensions={0} | all-to-all | bytes 163840 | tf_op jit(solution)/shard_map/all_to_all | solution.py:38
  30.0 20.8 %all_to_all.31 = f32[32,1,4352]{2,1,0:T(1,128)S(1)} all-to-all(f32[32,1,4352]{2,1,0:T(1,128)} %bitcast.26), channel_id=1, replica_groups=mesh['x'=4,'core'=2,'y'=4,'z'=16] {'x','core','y'}, dimensions={0} | all-to-all | bytes 1114112 | tf_op jit(solution)/shard_map/all_to_all | solution.py:38
  50.8 6.5 %core.1 = (f32[320,128]{1,0:T(8,128)S(1)}, bf16[256,4096]{1,0:T(8,128)(2,1)S(1)}, f32[40,512]{1,0:T(8,128)S(1)}, f32[1,512]{1,0:T(1,128)S(1)}) custom-call(f32[160,128]{1,0:T(8,128)S(1)} %bitcast.19, f32[1088,128]{1,0:T(8,128)S(1)} %bitcast.16), custom_call_target="tpu_custom_call" | custom-call | tf_op jit(solution)/shard_map/core/pallas_call | solution.py:26
  57.2 12.2 %all_to_all.32 = f32[32,1,1280]{2,1,0:T(1,128)S(1)} all-to-all(f32[32,1,1280]{2,1,0:T(1,128)S(1)} %bitcast.20), channel_id=1, replica_groups=mesh['x'=4,'core'=2,'y'=4,'z'=16] {'x','core','y'}, dimensions={0} | all-to-all | bytes 327680 | tf_op jit(solution)/shard_map/all_to_all | solution.py:38
  69.4 0.1 reduce_sum.9
  69.6 14.5 %all_to_all.33 = f32[16,1,1280]{2,1,0:T(1,128)S(1)} all-to-all(f32[16,1,1280]{2,1,0:T(1,128)S(1)} %broadcast_in_dim.2), channel_id=1, replica_groups=mesh['x'=4,'core'=2,'y'=4,'z'=16] {'z'}, dimensions={0} | all-to-all | bytes 163840 | tf_op jit(solution)/shard_map/all_to_all | solution.py:38
  84.1 0.0 copy-start
  84.1 3.0 %rows.1 = (f32[64,128]{1,0:T(8,128)S(1)}, f32[40,40]{1,0:T(8,128)S(1)}) custom-call(f32[160,128]{1,0:T(8,128)S(1)} %bitcast.18, f32[40,512]{1,0:T(8,128)S(1)} %get-tuple-element.19.features, bf16[256,4096]{1,0:T(8,128)(2,1)S(1)} %get-tuple-element.20.columns), custom_call_target="tpu_custom_call" | custom-call | tf_op jit(solution)/shard_map/rows/pallas_call | solution.py:26
  87.1 15.6 %all_to_all.34 = f32[16,1,512]{2,1,0:T(1,128)S(1)} all-to-all(f32[16,1,512]{2,1,0:T(1,128)S(1)} %bitcast.23), channel_id=1, replica_groups=mesh['x'=4,'core'=2,'y'=4,'z'=16] {'z'}, dimensions={0} | all-to-all | bytes 65536 | tf_op jit(solution)/shard_map/all_to_all | solution.py:38
  102.7 3.2 %columns.1 = (f32[1,32]{1,0:T(1,128)S(1)}, f32[256,128]{1,0:T(8,128)S(1)}) custom-call(f32[64,128]{1,0:T(8,128)S(1)} %bitcast.21, f32[1,512]{1,0:T(1,128)S(1)} %get-tuple-element.22.log_source, f32[40,512]{1,0:T(8,128)S(1)} %get-tuple-element.19.features, f32[40,40]{1,0:T(8,128)S(1)} %get-tuple-element.23.core, bf16[256,4096]{1,0:T(8,128)(2,1)S(1)} %get-tuple-element.20.columns), custom_call_target="tpu_custom_call" | custom-call | tf_op jit(solution)/shard_map/columns/pallas_call | solution.py:26
  105.9 12.8 %all_to_all.35 = f32[32,1,1024]{2,1,0:T(1,128)S(1)} all-to-all(f32[32,1,1024]{2,1,0:T(1,128)S(1)} %bitcast.22), channel_id=1, replica_groups=mesh['x'=4,'core'=2,'y'=4,'z'=16] {'x','core','y'}, dimensions={0} | all-to-all | bytes 262144 | tf_op jit(solution)/shard_map/all_to_all | solution.py:38
  118.7 0.0 copy-done
  118.7 0.7 last.1
  (1 shorter events, 0.0 us)
Async XLA Ops:
  84.1 34.5 %copy-start = (f32[1024]{0:T(1024)S(1)}, f32[1024]{0:T(1024)}, u32[]{:S(2)}) copy-start(f32[1024]{0:T(1024)} %param.12) | copy-start | bytes 12292

commit v7 on v6

--- a/solution.py
+++ b/solution.py
@@ -351,8 +351,8 @@
     mine, theirs = pl.pallas_call(
         pack,
         out_shape=(
-            jax.ShapeDtypeStruct((10 * n_z, LANES), F32),
-            jax.ShapeDtypeStruct((34 * n_plane, LANES), F32),
+            pltpu.VMEM((10 * n_z, LANES), F32),
+            pltpu.VMEM((34 * n_plane, LANES), F32),
         ),
         in_specs=[pl.BlockSpec(memory_space=pltpu.HBM)] * len(given),
         out_specs=(VMEM, VMEM),
@@ -361,8 +361,9 @@
             pltpu.SemaphoreType.DMA((len(given),)),
             *(pltpu.VMEM(a.shape, F32) for a in given),
         ],
+        compiler_params=pltpu.CompilerParams(vmem_limit_bytes=16 * 2**20),
         name="pack",
-    )(*given)
+    )(*(pltpu.with_memory_space_constraint(a, pltpu.HBM) for a in given))
     theirs = exchange(theirs.reshape(n_plane, 1, 34 * LANES), PLANE).reshape(-1, LANES)
     mine = exchange(mine.reshape(n_z, 1, 10 * LANES), "z").reshape(-1, LANES)
     former = pltpu.VMEM((DEPTH, rows), BF16)

time: 120 us -> 119 us (level)
  no operation moved by 1% of the time
where the time goes in v7:
time: 119 us; the launch traced here: 118 us
  blocking collectives  103 us (87%)
  Pallas kernels  14.2 us (12%)
    all_to_all x6, blocking collectives, exchange(): return lax.all_to_all(copies, axis, split_axis=0, concat_axis=0, tiled=True)  103 us
    pallas_call x4, Pallas kernels, call(): pl.pallas_call(body, out_shape=tuple((jax.ShapeDtypeStruct(s, d) for s, d...  13.3 us

profile of v7, /device:TPU:1, one launch (start us, length us, event | category | flops | bytes accessed | tf_op | source)
XLA Modules:
  0.0 118.1 jit_solution(6492235718957145715)
XLA Ops:
  0.6 1.0 pack.1
  1.6 27.3 %all_to_all.30 = f32[16,1,1280]{2,1,0:T(1,128)S(1)} all-to-all(f32[16,1,1280]{2,1,0:T(1,128)S(1)} %bitcast.24), channel_id=1, replica_groups=mesh['x'=4,'core'=2,'y'=4,'z'=16] {'z'}, dimensions={0} | all-to-all | bytes 163840 | tf_op jit(solution)/shard_map/all_to_all | solution.py:38
  28.9 20.6 %all_to_all.31 = f32[32,1,4352]{2,1,0:T(1,128)S(1)} all-to-all(f32[32,1,4352]{2,1,0:T(1,128)S(1)} %bitcast.17), channel_id=1, replica_groups=mesh['x'=4,'core'=2,'y'=4,'z'=16] {'x','core','y'}, dimensions={0} | all-to-all | bytes 1114112 | tf_op jit(solution)/shard_map/all_to_all | solution.py:38
  49.5 6.5 %core.1 = (f32[320,128]{1,0:T(8,128)S(1)}, bf16[256,4096]{1,0:T(8,128)(2,1)S(1)}, f32[40,512]{1,0:T(8,128)S(1)}, f32[1,512]{1,0:T(1,128)S(1)}) custom-call(f32[160,128]{1,0:T(8,128)S(1)} %bitcast.20, f32[1088,128]{1,0:T(8,128)S(1)} %bitcast.16), custom_call_target="tpu_custom_call" | custom-call | tf_op jit(solution)/shard_map/core/pallas_call | solution.py:26
  56.0 12.2 %all_to_all.32 = f32[32,1,1280]{2,1,0:T(1,128)S(1)} all-to-all(f32[32,1,1280]{2,1,0:T(1,128)S(1)} %bitcast.21), channel_id=1, replica_groups=mesh['x'=4,'core'=2,'y'=4,'z'=16] {'x','core','y'}, dimensions={0} | all-to-all | bytes 327680 | tf_op jit(solution)/shard_map/all_to_all | solution.py:38
  68.2 0.1 reduce_sum.9
  68.3 14.5 %all_to_all.33 = f32[16,1,1280]{2,1,0:T(1,128)S(1)} all-to-all(f32[16,1,1280]{2,1,0:T(1,128)S(1)} %broadcast_in_dim.2), channel_id=1, replica_groups=mesh['x'=4,'core'=2,'y'=4,'z'=16] {'z'}, dimensions={0} | all-to-all | bytes 163840 | tf_op jit(solution)/shard_map/all_to_all | solution.py:38
  82.9 0.0 copy-start
  82.9 2.9 %rows.1 = (f32[64,128]{1,0:T(8,128)S(1)}, f32[40,40]{1,0:T(8,128)S(1)}) custom-call(f32[160,128]{1,0:T(8,128)S(1)} %bitcast.19, f32[40,512]{1,0:T(8,128)S(1)} %get-tuple-element.19.features, bf16[256,4096]{1,0:T(8,128)(2,1)S(1)} %get-tuple-element.20.columns), custom_call_target="tpu_custom_call" | custom-call | tf_op jit(solution)/shard_map/rows/pallas_call | solution.py:26
  85.8 15.6 %all_to_all.34 = f32[16,1,512]{2,1,0:T(1,128)S(1)} all-to-all(f32[16,1,512]{2,1,0:T(1,128)S(1)} %bitcast.25), channel_id=1, replica_groups=mesh['x'=4,'core'=2,'y'=4,'z'=16] {'z'}, dimensions={0} | all-to-all | bytes 65536 | tf_op jit(solution)/shard_map/all_to_all | solution.py:38
  101.5 3.2 %columns.1 = (f32[1,32]{1,0:T(1,128)S(1)}, f32[256,128]{1,0:T(8,128)S(1)}) custom-call(f32[64,128]{1,0:T(8,128)S(1)} %bitcast.22, f32[1,512]{1,0:T(1,128)S(1)} %get-tuple-element.22.log_source, f32[40,512]{1,0:T(8,128)S(1)} %get-tuple-element.19.features, f32[40,40]{1,0:T(8,128)S(1)} %get-tuple-element.23.core, bf16[256,4096]{1,0:T(8,128)(2,1)S(1)} %get-tuple-element.20.columns), custom_call_target="tpu_custom_call" | custom-call | tf_op jit(solution)/shard_map/columns/pallas_call | solution.py:26
  104.6 12.8 %all_to_all.35 = f32[32,1,1024]{2,1,0:T(1,128)S(1)} all-to-all(f32[32,1,1024]{2,1,0:T(1,128)S(1)} %bitcast.23), channel_id=1, replica_groups=mesh['x'=4,'core'=2,'y'=4,'z'=16] {'x','core','y'}, dimensions={0} | all-to-all | bytes 262144 | tf_op jit(solution)/shard_map/all_to_all | solution.py:38
  117.4 0.0 copy-done
  117.4 0.7 last.1
  (1 shorter events, 0.0 us)
Async XLA Ops:
  82.9 34.5 %copy-start = (f32[1024]{0:T(1024)S(1)}, f32[1024]{0:T(1024)}, u32[]{:S(2)}) copy-start(f32[1024]{0:T(1024)} %param.12) | copy-start | bytes 12292

commit v8 on v7

--- a/solution.py
+++ b/solution.py
@@ -18,6 +18,8 @@
 DEPTH = 256
 LOG2E = math.log2(math.e)
 LN2 = math.log(2.0)
+FLOOR = 2.0**-70
+LIFT = 12.0
 F32, BF16 = jnp.float32, jnp.bfloat16
 VMEM = pl.BlockSpec(memory_space=pltpu.VMEM)
 
@@ -94,7 +96,7 @@
         column_out[34 * k : 34 * k + 34, :] = both
 
 
-def column_stack(message, out, y, log_targets):
+def column_stack(message, out, offsets, y, log_targets):
     for k in range(8):
         points = jnp.concatenate(
             [message[pl.ds(34 * (4 * s + y) + k, 4, stride=8), :] for s in range(8)], 0
@@ -103,6 +105,7 @@
         at = 34 * (4 * k + y) + 32
         offset = jnp.log(message[pl.ds(at + 1, 1), :]) - log_targets
         offset = (offset + message[pl.ds(at, 1), :] * (1.0 / EPSILON)) * LOG2E
+        offsets[pl.ds(8 * y + k, 1), :] = offset
         tail = jnp.concatenate(
             [squares, jnp.ones((1, LANES), F32), offset, jnp.zeros((5, LANES), F32)], 0
         )
@@ -200,7 +203,9 @@
 
 
 def core_kernel(log_sources, log_targets):
-    def body(message, arrived, packed, columns, features, log_out, former, total, *tiles):
+    def body(
+        message, arrived, packed, columns, features, log_out, offsets, former, total, *tiles
+    ):
         value, log_source, potential, core = unpacked_sources(message, log_sources)
         features[...] = value
         log_out[...] = log_source
@@ -210,7 +215,7 @@
         total[...] = jnp.zeros_like(total)
 
         def prepare(y):
-            column_stack(arrived, columns, jnp.minimum(y, 3), log_targets)
+            column_stack(arrived, columns, offsets, jnp.minimum(y, 3), log_targets)
 
         prepare(0)
 
@@ -236,35 +241,49 @@
     return body
 
 
-def row_kernel(parts, features, columns, out, core_out, former, highest, total, *tiles):
+def row_kernel(
+    parts, features, columns, out, core_out, shares, top_out, former, highest, scores
+):
     core = core_from_rows(sum(parts[10 * k : 10 * k + 10, :] for k in range(parts.shape[0] // 10)))
     core_out[...] = core
     former[...] = former_stack(weighted_core(core, features[...]), None, 1.0)
     rows = features.shape[1]
-    highest[...] = jnp.full(highest.shape, jnp.finfo(F32).min, F32)
-    total[...] = jnp.zeros_like(total)
-
-    def consume(tile, _):
-        for r in range(0, rows, 64):
-            at = pl.ds(r, 64)
-            pieces = [tile[at, LANES * k : LANES * k + LANES] for k in range(tile.shape[1] // LANES)]
-            before = highest[at, :]
-            now = largest([before, *pieces])
-            highest[at, :] = now
-            total[at, :] = total[at, :] * jnp.exp2(before - now) + sum(
-                jnp.exp2(p - now) for p in pieces
-            )
-
-    in_turns(former, columns, consume, tiles)
-    lanes = highest[...]
-    top = jnp.max(lanes, 1, keepdims=True)
-    added = jnp.sum(total[...] * jnp.exp2(lanes - top), 1, keepdims=True)
-    part = top * LN2 + jnp.log(added)
-    wide = jnp.broadcast_to(part, (rows, LANES))
-    flat = [jnp.transpose(wide[LANES * k : LANES * k + LANES])[0:1] for k in range(4)]
-    both = jnp.concatenate(flat, 0)
+    highest[...] = jnp.full(highest.shape, -jnp.inf, F32)
+
+    def fill(b, _):
+        at = pl.ds(pl.multiple_of(2048 * b, 2048), 2048)
+        tile = dot(former[...], columns[:, at], ((0,), (0,)))
+        scores[:, at] = tile
+        pieces = [tile[:, LANES * k : LANES * k + LANES] for k in range(16)]
+        highest[...] = largest([highest[...], *pieces])
+        return 0
+
+    lax.fori_loop(0, columns.shape[1] // 2048, fill, 0)
+    top = jnp.max(highest[...], 1, keepdims=True)
+    highest[...] = jnp.broadcast_to(top, highest.shape)
+
+    added = []
+    for r in range(0, rows, 8):
+        of = pl.ds(r, 8)
+        shift = highest[of, :]
+        sums = [jnp.zeros((8, LANES), F32) for _ in range(4)]
+        for k in range(columns.shape[1] // LANES):
+            at = pl.ds(LANES * k, LANES)
+            share = jnp.exp2(scores[of, at] - shift)
+            shares[of, at] = share
+            sums[k % 4] = sums[k % 4] + share
+        added.append(sum(sums))
+    total = jnp.concatenate(added, 0)
+    part = top * LN2 + jnp.log(jnp.sum(total, 1, keepdims=True))
+    both = across(jnp.broadcast_to(part, (rows, LANES)))
     for k in range(out.shape[0] // 4):
         out[4 * k : 4 * k + 4, :] = both
+    top_out[...] = across(highest)
+
+
+def across(wide):
+    flat = [jnp.transpose(wide[LANES * k : LANES * k + LANES, :])[0:1] for k in range(4)]
+    return jnp.concatenate(flat, 0)
 
 
 def largest(values):
@@ -286,31 +305,74 @@
     return jnp.concatenate([rows[k : k + 1] for k in range(rows.shape[0])], 1)
 
 
-def column_kernel(
-    parts, log_source, features, core, columns, own_out, out, former, held, mine, *tiles
-):
-    merged = in_lanes(combined([parts[4 * k : 4 * k + 4, :] for k in range(parts.shape[0] // 4)]))
-    logs = log_source[...]
-    source_new = EPSILON * (logs - merged)
-    own = own_out.shape[1]
-    for k in range(mine.shape[0]):
-        mine[k : k + 1, :] = source_new[:, own * k : own * k + own]
-    own_out[...] = mine[pl.ds(lax.axis_index("z"), 1), :]
-    weighted = weighted_core(core[...], features[...])
-    former[...] = former_stack(weighted, logs + source_new * (1.0 / EPSILON), 0.0)
-
-    def consume(tile, b):
-        for at, piece in column_pieces(tile, b):
-            highest = jnp.max(piece, 0, keepdims=True)
-            total = jnp.sum(jnp.exp2(piece - highest), 0, keepdims=True)
-            held[at, :] = highest * LN2 + jnp.log(total)
-
-    in_turns(former, columns, consume, tiles)
-    for y in range(4):
-        piece = held[8 * y : 8 * y + 8, :]
-        for s in range(8):
-            at = 8 * (4 * s + y)
-            out[at : at + 8, :] = piece
+def column_kernel(log_sources):
+    def body(
+        parts,
+        top,
+        shares,
+        offsets,
+        log_source,
+        features,
+        core,
+        columns,
+        own_out,
+        out,
+        former,
+        sums,
+        held,
+        weights,
+        mine,
+        *tiles,
+    ):
+        merged = combined([parts[4 * k : 4 * k + 4, :] for k in range(parts.shape[0] // 4)])
+        merged = in_lanes(merged)
+        logs = log_source[...]
+        source_new = EPSILON * (logs - merged)
+        own = own_out.shape[1]
+        for k in range(mine.shape[0]):
+            mine[k : k + 1, :] = source_new[:, own * k : own * k + own]
+        own_out[...] = mine[pl.ds(lax.axis_index("z"), 1), :]
+
+        lift = 2.0 * log_sources + LIFT
+        term = logs + source_new * (1.0 / EPSILON)
+        weight = jnp.exp(term + (in_lanes(top[...]) * LN2 + lift))
+        for k in range(4):
+            wide = jnp.broadcast_to(weight[:, LANES * k : LANES * k + LANES], (LANES, LANES))
+            weights[LANES * k : LANES * k + LANES, :] = jnp.transpose(wide)
+        rows = weights.shape[0]
+
+        for b in range(0, shares.shape[1] // LANES, 4):
+            totals = [jnp.zeros((8, LANES), F32) for _ in range(4)]
+            for r in range(0, rows, 8):
+                factor = weights[r : r + 8, :]
+                for k in range(4):
+                    at = pl.ds(LANES * (b + k), LANES)
+                    totals[k] = totals[k] + shares[r : r + 8, at] * factor
+            for k in range(4):
+                sums[b + k : b + k + 1, :] = jnp.sum(totals[k], 0, keepdims=True)
+
+        held[...] = jnp.log(sums[...]) - offsets[...] * LN2 - lift
+        safe = jnp.min(sums[...]) >= FLOOR
+
+        @pl.when(jnp.logical_not(safe))
+        def _():
+            former[...] = former_stack(weighted_core(core[...], features[...]), term, 0.0)
+
+            def consume(tile, b):
+                for at, piece in column_pieces(tile, b):
+                    highest = jnp.max(piece, 0, keepdims=True)
+                    total = jnp.sum(jnp.exp2(piece - highest), 0, keepdims=True)
+                    held[at, :] = highest * LN2 + jnp.log(total)
+
+            in_turns(former, columns, consume, tiles)
+
+        for y in range(4):
+            piece = held[8 * y : 8 * y + 8, :]
+            for s in range(8):
+                at = 8 * (4 * s + y)
+                out[at : at + 8, :] = piece
+
+    return body
 
 
 def last_kernel(log_targets):
@@ -368,13 +430,15 @@
     mine = exchange(mine.reshape(n_z, 1, 10 * LANES), "z").reshape(-1, LANES)
     former = pltpu.VMEM((DEPTH, rows), BF16)
     tile = pltpu.VMEM((rows, 512), F32)
-    packed, stack, features, log_source = call(
+    per_column = (columns // LANES, LANES)
+    packed, stack, features, log_source, offsets = call(
         core_kernel(log_sources, log_targets),
         [
             ((10 * n_plane, LANES), F32),
             ((DEPTH, columns), BF16),
             ((PAD, rows), F32),
             ((1, rows), F32),
+            (per_column, F32),
         ],
         (mine, theirs),
         scratch=[former, pltpu.VMEM((rows, DEPTH), F32), tile, tile],
@@ -386,24 +450,32 @@
     parts = exchange(parts, "z").reshape(-1, LANES)
 
     per_lane = pltpu.VMEM((rows, LANES), F32)
-    row_parts, core = call(
+    row_parts, core, shares, top = call(
         row_kernel,
-        [((4 * n_z, LANES), F32), ((PAD, PAD), F32)],
+        [
+            ((4 * n_z, LANES), F32),
+            ((PAD, PAD), F32),
+            ((rows, columns), F32),
+            ((rows // LANES, LANES), F32),
+        ],
         (parts, features, stack),
-        scratch=[former, per_lane, per_lane, tile, tile, tile, tile],
+        scratch=[former, per_lane, pltpu.VMEM((rows, columns), F32)],
         name="rows",
-        grant=16,
+        grant=24,
     )
     row_parts = exchange(row_parts.reshape(n_z, 1, rows), "z").reshape(-1, LANES)
     own_rows, column_parts = call(
-        column_kernel,
+        column_kernel(log_sources),
         [((1, own), F32), ((8 * n_plane, LANES), F32)],
-        (row_parts, log_source, features, core, stack),
+        (row_parts, top, shares, offsets, log_source, features, core, stack),
         scratch=[
             former,
-            pltpu.VMEM((columns // LANES, LANES), F32),
+            pltpu.VMEM(per_column, F32),
+            pltpu.VMEM(per_column, F32),
+            per_lane,
             pltpu.VMEM((n_z, own), F32),
-            *(tile, tile, tile, tile),
+            tile,
+            tile,
         ],
         name="columns",
         grant=16,

time: 119 us -> 120 us (level)
  Pallas kernels: 14.2 us -> 15.7 us
    pallas_call x4, Pallas kernels: 13.3 us -> 14.7 us  [call(): pl.pallas_call(body, out_shape=tuple((jax.ShapeDtypeStruct(s, d) for s, d...]
where the time goes in v8:
time: 120 us
  blocking collectives  103 us (86%)
  Pallas kernels  15.7 us (13%)
    all_to_all x6, blocking collectives, exchange(): return lax.all_to_all(copies, axis, split_axis=0, concat_axis=0, tiled=True)  103 us
    pallas_call x4, Pallas kernels, call(): pl.pallas_call(body, out_shape=tuple((jax.ShapeDtypeStruct(s, d) for s, d...  14.7 us

profile of v8, /device:TPU:1, one launch (start us, length us, event | category | flops | bytes accessed | tf_op | source)
XLA Modules:
  0.0 119.5 jit_solution(392254814393390743)
XLA Ops:
  0.6 0.0 copy-start
  0.6 1.0 pack.1
  1.6 27.3 %all_to_all.30 = f32[16,1,1280]{2,1,0:T(1,128)S(1)} all-to-all(f32[16,1,1280]{2,1,0:T(1,128)S(1)} %bitcast.24), channel_id=1, replica_groups=mesh['x'=4,'core'=2,'y'=4,'z'=16] {'z'}, dimensions={0} | all-to-all | bytes 163840 | tf_op jit(solution)/shard_map/all_to_all | solution.py:40
  28.9 20.6 %all_to_all.31 = f32[32,1,4352]{2,1,0:T(1,128)S(1)} all-to-all(f32[32,1,4352]{2,1,0:T(1,128)S(1)} %bitcast.17), channel_id=1, replica_groups=mesh['x'=4,'core'=2,'y'=4,'z'=16] {'x','core','y'}, dimensions={0} | all-to-all | bytes 1114112 | tf_op jit(solution)/shard_map/all_to_all | solution.py:40
  49.6 6.4 %core.1 = (f32[320,128]{1,0:T(8,128)S(1)}, bf16[256,4096]{1,0:T(8,128)(2,1)S(1)}, f32[40,512]{1,0:T(8,128)S(1)}, f32[1,512]{1,0:T(1,128)S(1)}, f32[32,128]{1,0:T(8,128)S(1)}) custom-call(f32[160,128]{1,0:T(8,128)S(1)} %bitcast.20, f32[1088,128]{1,0:T(8,128)S(1)} %bitcast.16), custom_call_target="tpu_custom_call" | custom-call | tf_op jit(solution)/shard_map/core/pallas_call | solution.py:28
  56.0 12.2 %all_to_all.32 = f32[32,1,1280]{2,1,0:T(1,128)S(1)} all-to-all(f32[32,1,1280]{2,1,0:T(1,128)S(1)} %bitcast.21), channel_id=1, replica_groups=mesh['x'=4,'core'=2,'y'=4,'z'=16] {'x','core','y'}, dimensions={0} | all-to-all | bytes 327680 | tf_op jit(solution)/shard_map/all_to_all | solution.py:40
  68.2 0.1 reduce_sum.9
  68.4 14.5 %all_to_all.33 = f32[16,1,1280]{2,1,0:T(1,128)S(1)} all-to-all(f32[16,1,1280]{2,1,0:T(1,128)S(1)} %broadcast_in_dim.2), channel_id=1, replica_groups=mesh['x'=4,'core'=2,'y'=4,'z'=16] {'z'}, dimensions={0} | all-to-all | bytes 163840 | tf_op jit(solution)/shard_map/all_to_all | solution.py:40
  82.9 3.2 %rows.1 = (f32[64,128]{1,0:T(8,128)S(1)}, f32[40,40]{1,0:T(8,128)S(1)}, f32[512,4096]{1,0:T(8,128)S(1)}, f32[4,128]{1,0:T(4,128)S(1)}) custom-call(f32[160,128]{1,0:T(8,128)S(1)} %bitcast.19, f32[40,512]{1,0:T(8,128)S(1)} %get-tuple-element.22.features, bf16[256,4096]{1,0:T(8,128)(2,1)S(1)} %get-tuple-element.23.columns), custom_call_target="tpu_custom_call" | custom-call | tf_op jit(solution)/shard_map/rows/pallas_call | solution.py:28
  86.0 15.6 %all_to_all.34 = f32[16,1,512]{2,1,0:T(1,128)S(1)} all-to-all(f32[16,1,512]{2,1,0:T(1,128)S(1)} %bitcast.25), channel_id=1, replica_groups=mesh['x'=4,'core'=2,'y'=4,'z'=16] {'z'}, dimensions={0} | all-to-all | bytes 65536 | tf_op jit(solution)/shard_map/all_to_all | solution.py:40
  101.7 4.4 %columns.1 = (f32[1,32]{1,0:T(1,128)S(1)}, f32[256,128]{1,0:T(8,128)S(1)}) custom-call(f32[64,128]{1,0:T(8,128)S(1)} %bitcast.22, f32[4,128]{1,0:T(4,128)S(1)} %get-tuple-element.25.top, f32[512,4096]{1,0:T(8,128)S(1)} %get-tuple-element.26.shares, f32[32,128]{1,0:T(8,128)S(1)} %get-tuple-element.27.offsets, f32[1,512]{1,0:T(1,128)S(1)} %get-tuple-element.28.log_source, ...), custom_call_target="tpu_custom_call" | custom-call | tf_op jit(solution)/shard_map/columns/pallas_call | solution.py:28
  106.1 12.8 %all_to_all.35 = f32[32,1,1024]{2,1,0:T(1,128)S(1)} all-to-all(f32[32,1,1024]{2,1,0:T(1,128)S(1)} %bitcast.23), channel_id=1, replica_groups=mesh['x'=4,'core'=2,'y'=4,'z'=16] {'x','core','y'}, dimensions={0} | all-to-all | bytes 262144 | tf_op jit(solution)/shard_map/all_to_all | solution.py:40
  118.9 0.0 copy-done
  118.9 0.7 last.1
  (1 shorter events, 0.0 us)
Async XLA Ops:
  0.6 118.2 %copy-start = (f32[1024]{0:T(1024)S(1)}, f32[1024]{0:T(1024)}, u32[]{:S(2)}) copy-start(f32[1024]{0:T(1024)} %param.12) | copy-start | bytes 12292

commit v9 on v8

--- a/solution.py
+++ b/solution.py
@@ -59,8 +59,8 @@
     return jnp.concatenate([*blocks, filler], 0).astype(BF16)
 
 
-LATTER_ORDER = (0, 0, 1, 0, 2, 1)
-FORMER_ORDER = (0, 1, 0, 2, 0, 1)
+LATTER_ORDER = (0, 1, 2, 0, 0, 1)
+FORMER_ORDER = (0, 0, 0, 1, 2, 1)
 
 
 def pack(*refs):
@@ -221,7 +221,7 @@
 
         def consume(tile, b):
             width = tile.shape[1]
-            stack = columns[:, pl.ds(pl.multiple_of(b * width, width), width)]
+            stack = columns[0:LANES, pl.ds(pl.multiple_of(b * width, width), width)]
             plan = jnp.exp2(tile[...])
             high = plan.astype(BF16)
             low = (plan - high.astype(F32)).astype(BF16)
@@ -229,7 +229,7 @@
 
         in_turns(former, columns, consume, tiles, prepare)
         carried = (
-            total[:, 0:PAD] + total[:, 2 * PAD : 3 * PAD] + total[:, 4 * PAD : 5 * PAD]
+            total[:, 0:PAD] + total[:, PAD : 2 * PAD] + total[:, 2 * PAD : 3 * PAD]
         )
         part = dot(features[...], carried, ((1,), (0,)), HIGHEST)
         part = jnp.concatenate([part[0:32], part[33:34], part[32:33]], 0)
@@ -441,7 +441,7 @@
             (per_column, F32),
         ],
         (mine, theirs),
-        scratch=[former, pltpu.VMEM((rows, DEPTH), F32), tile, tile],
+        scratch=[former, pltpu.VMEM((rows, LANES), F32), tile, tile],
         name="core",
         grant=16,
     )

time: 120 us -> 119 us (level)
  no operation moved by 1% of the time
where the time goes in v9:
time: 119 us
  blocking collectives  103 us (87%)
  Pallas kernels  15 us (13%)
    all_to_all x6, blocking collectives, exchange(): return lax.all_to_all(copies, axis, split_axis=0, concat_axis=0, tiled=True)  103 us
    pallas_call x4, Pallas kernels, call(): pl.pallas_call(body, out_shape=tuple((jax.ShapeDtypeStruct(s, d) for s, d...  14 us

profile of v9, /device:TPU:1, one launch (start us, length us, event | category | flops | bytes accessed | tf_op | source)
XLA Modules:
  0.0 118.9 jit_solution(9928894862600975254)
XLA Ops:
  0.6 0.0 copy-start
  0.6 1.0 pack.1
  1.6 27.3 %all_to_all.30 = f32[16,1,1280]{2,1,0:T(1,128)S(1)} all-to-all(f32[16,1,1280]{2,1,0:T(1,128)S(1)} %bitcast.24), channel_id=1, replica_groups=mesh['x'=4,'core'=2,'y'=4,'z'=16] {'z'}, dimensions={0} | all-to-all | bytes 163840 | tf_op jit(solution)/shard_map/all_to_all | solution.py:40
  28.9 20.6 %all_to_all.31 = f32[32,1,4352]{2,1,0:T(1,128)S(1)} all-to-all(f32[32,1,4352]{2,1,0:T(1,128)S(1)} %bitcast.17), channel_id=1, replica_groups=mesh['x'=4,'core'=2,'y'=4,'z'=16] {'x','core','y'}, dimensions={0} | all-to-all | bytes 1114112 | tf_op jit(solution)/shard_map/all_to_all | solution.py:40
  49.6 5.7 %core.1 = (f32[320,128]{1,0:T(8,128)S(1)}, bf16[256,4096]{1,0:T(8,128)(2,1)S(1)}, f32[40,512]{1,0:T(8,128)S(1)}, f32[1,512]{1,0:T(1,128)S(1)}, f32[32,128]{1,0:T(8,128)S(1)}) custom-call(f32[160,128]{1,0:T(8,128)S(1)} %bitcast.20, f32[1088,128]{1,0:T(8,128)S(1)} %bitcast.16), custom_call_target="tpu_custom_call" | custom-call | tf_op jit(solution)/shard_map/core/pallas_call | solution.py:28
  55.3 12.2 %all_to_all.32 = f32[32,1,1280]{2,1,0:T(1,128)S(1)} all-to-all(f32[32,1,1280]{2,1,0:T(1,128)S(1)} %bitcast.21), channel_id=1, replica_groups=mesh['x'=4,'core'=2,'y'=4,'z'=16] {'x','core','y'}, dimensions={0} | all-to-all | bytes 327680 | tf_op jit(solution)/shard_map/all_to_all | solution.py:40
  67.5 0.1 reduce_sum.9
  67.6 14.5 %all_to_all.33 = f32[16,1,1280]{2,1,0:T(1,128)S(1)} all-to-all(f32[16,1,1280]{2,1,0:T(1,128)S(1)} %broadcast_in_dim.2), channel_id=1, replica_groups=mesh['x'=4,'core'=2,'y'=4,'z'=16] {'z'}, dimensions={0} | all-to-all | bytes 163840 | tf_op jit(solution)/shard_map/all_to_all | solution.py:40
  82.2 3.2 %rows.1 = (f32[64,128]{1,0:T(8,128)S(1)}, f32[40,40]{1,0:T(8,128)S(1)}, f32[512,4096]{1,0:T(8,128)S(1)}, f32[4,128]{1,0:T(4,128)S(1)}) custom-call(f32[160,128]{1,0:T(8,128)S(1)} %bitcast.19, f32[40,512]{1,0:T(8,128)S(1)} %get-tuple-element.22.features, bf16[256,4096]{1,0:T(8,128)(2,1)S(1)} %get-tuple-element.23.columns), custom_call_target="tpu_custom_call" | custom-call | tf_op jit(solution)/shard_map/rows/pallas_call | solution.py:28
  85.4 15.6 %all_to_all.34 = f32[16,1,512]{2,1,0:T(1,128)S(1)} all-to-all(f32[16,1,512]{2,1,0:T(1,128)S(1)} %bitcast.25), channel_id=1, replica_groups=mesh['x'=4,'core'=2,'y'=4,'z'=16] {'z'}, dimensions={0} | all-to-all | bytes 65536 | tf_op jit(solution)/shard_map/all_to_all | solution.py:40
  101.0 4.4 %columns.1 = (f32[1,32]{1,0:T(1,128)S(1)}, f32[256,128]{1,0:T(8,128)S(1)}) custom-call(f32[64,128]{1,0:T(8,128)S(1)} %bitcast.22, f32[4,128]{1,0:T(4,128)S(1)} %get-tuple-element.25.top, f32[512,4096]{1,0:T(8,128)S(1)} %get-tuple-element.26.shares, f32[32,128]{1,0:T(8,128)S(1)} %get-tuple-element.27.offsets, f32[1,512]{1,0:T(1,128)S(1)} %get-tuple-element.28.log_source, ...), custom_call_target="tpu_custom_call" | custom-call | tf_op jit(solution)/shard_map/columns/pallas_call | solution.py:28
  105.4 12.8 %all_to_all.35 = f32[32,1,1024]{2,1,0:T(1,128)S(1)} all-to-all(f32[32,1,1024]{2,1,0:T(1,128)S(1)} %bitcast.23), channel_id=1, replica_groups=mesh['x'=4,'core'=2,'y'=4,'z'=16] {'x','core','y'}, dimensions={0} | all-to-all | bytes 262144 | tf_op jit(solution)/shard_map/all_to_all | solution.py:40
  118.2 0.0 copy-done
  118.2 0.7 last.1
  (1 shorter events, 0.0 us)
Async XLA Ops:
  0.6 117.5 %copy-start = (f32[1024]{0:T(1024)S(1)}, f32[1024]{0:T(1024)}, u32[]{:S(2)}) copy-start(f32[1024]{0:T(1024)} %param.12) | copy-start | bytes 12292
